TPU v7x, 32 devices: a whole 2x2x4 slice. The times are simulated.
32 devices in a mesh: real: 2 (over x), row: 16 (over z, y, core).
Axes of the slice: x: 2, y: 2, z: 4, core: 2. Of those that a mesh axis runs over, the one named last changes fastest.
Arguments:
- site_tensor: float32 [32, 2, 256, 256], P(('real', 'row')), parts along dimension 0, may hold values from -20 to 20
- left_env: float32 [32, 14, 256, 256], P(('real', 'row')), parts along dimension 0, may hold values from -10 to 10
- right_env: float32 [32, 14, 256, 256], P(('real', 'row')), parts along dimension 0, may hold values from -10 to 10
- sector_size: int32 [32], P('real'), parts along dimension 0, may hold values from 64 to 256
Outputs:
- left_out: float32 [32, 2, 256, 256], P(('real', 'row')), parts along dimension 0
- bond_out: float32 [32, 256, 256], P(('real', 'row')), parts along dimension 0
There are 2 independent parts, one for each index of `real`. A program takes and returns all parts, laid end to end along the dimension named above; each array names one. Nothing has to cross between parts.
All inputs are finite; a program needn't handle non-finite values.
Results may differ from a plain program's by a relative error of at most 0.00005.
Values sent between devices are 32-bit elements; how exact they have to be, the bound alone decides.
No kernel may reach another device: no remote copies, remote signals or barrier semaphores. Data moves between devices by JAX's collectives and lax.ppermute only.
A program may use at most 64 MiB of HBM per device.

v0:
```python
import jax
import jax.numpy as jnp
from jax import lax
from jax.sharding import PartitionSpec as P

W_DN = 4
W_UP = 4


highest = lax.Precision.HIGHEST
time_step = 0.15


def padded(block, sides, width):
    for axis, dim in sides:
        count = lax.axis_size(axis)
        forward = [(i, i + 1) for i in range(count - 1)]
        backward = [(target, source) for source, target in forward]
        low = lax.ppermute(
            lax.slice_in_dim(block, block.shape[dim] - width, None, axis=dim), axis, forward
        )
        high = lax.ppermute(lax.slice_in_dim(block, 0, width, axis=dim), axis, backward)
        block = jnp.concatenate([low, block, high], axis=dim)
    return block


def shifted_2(value, axis, steps):
    count = lax.axis_size(axis)
    leading, last = (max(0, -steps), min(count, count - steps))
    return lax.ppermute(value, axis, [(source, source + steps) for source in range(leading, last)])


def apply_moved(operand, left_local, right_local, right_down, right_upper, mask_pair):
    bordered = padded(operand[None], (("row", 0),), 1)
    down_terms = jnp.einsum("ik,akl->ail", bordered[0], right_down, precision=highest)
    upper_terms = jnp.einsum("ik,akl->ail", bordered[2], right_upper, precision=highest)
    own_terms = jnp.einsum("ik,akl->ail", operand, right_local[W_DN + W_UP :], precision=highest)
    combined = jnp.concatenate([down_terms, upper_terms, own_terms], 0)
    return jnp.einsum("aij,ajl->il", left_local, combined, precision=highest) * mask_pair


def on_device(site_tensor, left_env, right_env, sector_size):
    states = site_tensor.shape[-1]
    left_local = left_env[0]
    right_local = right_env[0]
    right_down = shifted_2(right_local[:W_DN], "row", 1)
    right_upper = shifted_2(right_local[W_DN : W_DN + W_UP], "row", -1)
    own_size = lax.dynamic_index_in_dim(sector_size, lax.axis_index("row"), 0, keepdims=False)
    live_mask = (jnp.arange(states, dtype=jnp.int32) < own_size).astype(jnp.float32)
    mask_pair = live_mask[:, None] * live_mask[None, :]
    lower_source = site_tensor[0, 1] * live_mask[:, None]
    lower_block = shifted_2(lower_source, "row", 1) * live_mask[None, :]
    upper_block = site_tensor[0, 0] * mask_pair
    stacked = jnp.concatenate([upper_block, lower_block], 0)
    identity = jnp.eye(states, dtype=jnp.float32)
    gram_matrix = (
        jnp.einsum("ij,ik->jk", stacked, stacked, precision=highest)
        + identity * (1.0 - live_mask)[None, :]
    )
    factor = jnp.linalg.cholesky(gram_matrix)
    orthonormal = jax.scipy.linalg.solve_triangular(factor, stacked.T, lower=True).T
    moved_back = shifted_2(orthonormal[states:], "row", -1)
    left_out = jnp.stack([orthonormal[:states], moved_back], 0)[None]
    bond_matrix = factor.T * mask_pair

    def operator(operand):
        return apply_moved(operand, left_local, right_local, right_down, right_upper, mask_pair)

    local_norm = jnp.sum(bond_matrix * bond_matrix)
    start_norm = lax.psum(local_norm, "row")
    applied = operator(bond_matrix)
    correlation_sum = lax.psum(jnp.sum(bond_matrix * applied), "row")
    energy = correlation_sum / start_norm
    shifted = applied - energy * bond_matrix
    second = operator(shifted) - energy * shifted
    evolved = bond_matrix + time_step * shifted + 0.5 * time_step * time_step * second
    final_norm = lax.psum(jnp.sum(evolved * evolved), "row")
    return (left_out, (evolved * jnp.sqrt(start_norm / final_norm))[None])


def solution(mesh):
    placed = (
        P(("real", "row"), None, None, None),
        P(("real", "row"), None, None, None),
        P(("real", "row"), None, None, None),
        P("real"),
    )
    return jax.shard_map(
        on_device,
        mesh=mesh,
        in_specs=placed,
        out_specs=(P(("real", "row"), None, None, None), P(("real", "row"), None, None)),
        check_vma=False,
    )
```

profile of v0, /device:TPU:0, one launch (start us, length us, event | category | flops | bytes accessed | tf_op | source)
XLA Modules:
  0.0 187.4 jit_solution(6890272348640759516)
XLA Ops:
  0.6 1.2 dynamic_slice.4
  1.9 0.6 compare_convert_fusion
  2.5 1.1 fusion.86
  3.6 0.1 copy.12
  3.8 2.4 %collective-permute-start = (f32[256,256]{0,1:T(8,128)S(1)}, f32[256,256]{0,1:T(8,128)S(1)}, u32[]{:S(2)}, u32[]{:S(2)}) collective-permute-start(f32[256,256]{0,1:T(8,128)S(1)} %bitcast_multiply_fusion), channel_id=1, source_target_pairs={{0,1},{1,2},{2,3},{3,4},{4,5},{5,6},{6,7},{7,8},{8,9},{9,10},{10,1... | collective-permute-start | bytes 786440 | tf_op jit(solution)/shard_map/ppermute | solution.py:30
  6.2 3.0 %slice_bitcast_fusion.1 = (f32[4,256,256]{2,1,0:T(8,128)}, f32[4,256,256]{2,1,0:T(8,128)}) fusion(f32[1,14,256,256]{3,2,1,0:T(8,128)} %param.6), kind=kLoop, calls=%fused_computation.37 | loop fusion | bytes 4194304 | tf_op jit(solution)/shard_map/slice | solution.py:46
  9.2 1.3 collective-permute-start.5
  10.5 6.1 %collective-permute-start.3 = (f32[4,256,256]{2,1,0:T(8,128)}, f32[4,256,256]{2,1,0:T(8,128)}, u32[]{:S(2)}, u32[]{:S(2)}) collective-permute-start(f32[4,256,256]{2,1,0:T(8,128)} %get-tuple-element.26), channel_id=1, source_target_pairs={{0,1},{1,2},{2,3},{3,4},{4,5},{5,6},{6,7},{7,8},{8,9},{9,10},{10,1... | collective-permute-start | bytes 3145736 | tf_op jit(solution)/shard_map/ppermute | solution.py:30
  16.6 0.1 copy.11
  16.8 0.7 broadcast_subtract_fusion
  17.4 0.0 collective-permute-done
  17.5 0.1 multiply_multiply_fusion.1
  17.6 0.6 fusion.62
  18.2 0.1 copy.8
  18.3 0.1 fusion.73
  18.4 11.7 %cholesky.49 = f32[128,128]{1,0:T(8,128)S(1)} custom-call(f32[128,128]{1,0:T(8,128)S(1)} %cholesky.115), custom_call_target="Cholesky" | custom-call | tf_op jit(solution)/shard_map/jit(cholesky)/cholesky | solution.py:60
  30.2 9.8 %custom-call.15 = f32[1,128,128]{1,2,0:T(8,128)S(1)} custom-call(f32[1,128,128]{2,1,0:T(8,128)S(1)} %get-tuple-element.35), custom_call_target="InvertDiagBlocksLowerTriangular" | custom-call | tf_op jit(solution)/shard_map/jit(cholesky)/cholesky | solution.py:60
  40.0 0.2 constant_dynamic-update-slice_fusion.1
  40.2 0.3 convolution_subtract_fusion
  40.5 11.7 %cholesky.103 = f32[128,128]{1,0:T(8,128)S(1)} custom-call(f32[128,128]{1,0:T(8,128)S(1)} %convolution_subtract_fusion), custom_call_target="Cholesky" | custom-call | tf_op jit(solution)/shard_map/jit(cholesky)/cholesky | solution.py:60
  52.3 0.6 compare_reduce_fusion
  54.1 0.8 fusion.84
  54.9 1.3 collective-permute-start.4
  56.2 4.2 %collective-permute-start.2 = (f32[1,256,256]{1,2,0:T(8,128)}, f32[1,256,256]{1,2,0:T(8,128)}, u32[]{:S(2)}, u32[]{:S(2)}) collective-permute-start(f32[1,256,256]{1,2,0:T(8,128)} %fusion.84), channel_id=1, source_target_pairs={{0,1},{1,2},{2,3},{3,4},{4,5},{5,6},{6,7},{7,8},{8,9},{9,10},{10,1... | collective-permute-start | bytes 786440 | tf_op jit(solution)/shard_map/ppermute | solution.py:19
  60.4 0.1 fusion.61
  60.5 0.1 triangular_solve.63
  60.6 3.9 %while.1 = (s32[]{:T(128)}, f32[256,256]{1,0:T(8,128)S(1)}, s32[2,2]{1,0:T(2,128)S(1)}, f32[2,128,128]{2,1,0:T(8,128)S(1)}, s32[]{:T(128)}) while((s32[]{:T(128)}, f32[256,256]{1,0:T(8,128)S(1)}, s32[2,2]{1,0:T(2,128)S(1)}, f32[2,128,128]{2,1,0:T(8,128)S(1)}, s32[]{:T(128)}) %tuple.35), condition=%wide.while_cond, body=%wide.while_body.sunk | while | flops 2 | bytes 131181 | solution.py:61
  60.6 0.6 fusion.95
  61.2 1.3 bitcast_dynamic-update-slice_fusion.2
  62.6 0.6 fusion.95
  63.1 1.3 bitcast_dynamic-update-slice_fusion.2
  64.5 19.7 %custom-call.16 = f32[2,128,128]{1,2,0:T(8,128)S(1)} custom-call(f32[2,128,128]{2,1,0:T(8,128)S(1)} %get-tuple-element.9), custom_call_target="InvertDiagBlocksLowerTriangular" | custom-call | tf_op jit(solution)/shard_map/jit(_solve_triangular)/triangular_solve | solution.py:61
  84.2 0.4 fusion.64
  84.6 0.4 fusion.76
  85.0 0.4 fusion.63
  85.5 1.3 collective-permute-start.1
  86.8 4.1 %fusion.18 = f32[6,256,256]{1,2,0:T(8,128)S(1)} fusion(f32[1,14,256,256]{3,2,1,0:T(8,128)} %param.6, f32[256,256]{1,0:T(8,128)S(1)} %get-tuple-element.33, f32[256]{0:T(256)S(1)} %compare_convert_fusion, pred[]{:T(512)S(6)} %cholesky.108), kind=kOutput, calls=%fused_computation.20 | convolution fusion | flops 1208287232 | bytes 3409921 | tf_op jit(solution)/shard_map/ik,akl->ail/dot_general | solution.py:37
  90.9 0.0 collective-permute-done.1
  91.0 1.0 copy.9
  92.0 0.0 copy-start
  92.0 0.0 collective-permute-done.4
  92.0 0.0 collective-permute-done.5
  92.0 2.9 %convolution_bitcast_fusion.2 = f32[4,256,256]{1,2,0:T(8,128)S(1)} fusion(f32[4,256,256]{2,1,0:T(8,128)S(1)} %collective-permute-done.5, f32[1,256,256]{1,2,0:T(8,128)} %collective-permute-done.4), kind=kOutput, calls=%fused_computation.26 | convolution fusion | flops 805306368 | bytes 2359296 | tf_op jit(solution)/shard_map/ik,akl->ail/dot_general | solution.py:36
  94.9 0.0 collective-permute-done.2
  94.9 0.0 collective-permute-done.3
  94.9 3.1 %convolution_bitcast_fusion.3 = f32[4,256,256]{1,2,0:T(8,128)S(1)} fusion(f32[4,256,256]{2,1,0:T(8,128)} %collective-permute-done.3, f32[1,256,256]{1,2,0:T(8,128)} %collective-permute-done.2), kind=kOutput, calls=%fused_computation.27 | convolution fusion | flops 805306368 | bytes 2359296 | tf_op jit(solution)/shard_map/ik,akl->ail/dot_general | solution.py:35
  98.0 0.0 copy-done
  98.1 3.8 %multiply_reduce_fusion.1 = (f32[]{:T(128)}, f32[]{:T(128)}, f32[256,256]{0,1:T(8,128)S(1)}) fusion(f32[256]{0:T(256)S(1)} %compare_convert_fusion, f32[256,256]{1,0:T(8,128)S(1)} %get-tuple-element.33, pred[]{:T(512)S(6)} %cholesky.108, f32[1,14,256,256]{3,2,1,0:T(8,128)S(1)} %copy-done, f32[6,256,256]{1,2,0:T(8,128)S(1)} %fusion.18, ...), kind=kOutput, calls=%fused_computation.63 | convolution fusion | flops 2821062656 | bytes 7865353 | tf_op jit(solution)/shard_map/aij,ajl->il/dot_general | solution.py:39
  101.9 34.8 %all-reduce.1 = (f32[]{:T(128)}, f32[]{:T(128)}) all-reduce(f32[]{:T(128)} %get-tuple-element.13, f32[]{:T(128)} %get-tuple-element.12), channel_id=1, replica_groups=mesh['real'=2,'row'=16] {'row'}, use_global_device_ids=true, to_apply=%region_5.6 | all-reduce | flops 2 | bytes 16 | tf_op jit(solution)/shard_map/psum | solution.py:72
  137.9 0.1 fusion.75
  138.0 0.0 copy-start.1
  138.0 1.6 collective-permute-start.6
  139.6 1.5 collective-permute-start.7
  141.1 4.1 %fusion.21 = f32[6,256,256]{1,2,0:T(8,128)S(1)} fusion(f32[1,14,256,256]{3,2,1,0:T(8,128)} %param.6, f32[256,256]{0,1:T(8,128)S(1)} %get-tuple-element.40, f32[]{:T(128)S(6)} %div.16, f32[256,256]{1,0:T(8,128)S(1)} %get-tuple-element.33, f32[256]{0:T(256)S(1)} %compare_convert_fusion, pred[]{:T(512)S(6)} %cholesky.108), kind=kOutput, calls=%fused_computation.21 | convolution fusion | flops 1208418304 | bytes 3672069 | tf_op jit(solution)/shard_map/ik,akl->ail/dot_general | solution.py:37
  145.2 0.0 collective-permute-done.6
  145.2 3.0 %convolution_bitcast_fusion.1 = f32[4,256,256]{1,2,0:T(8,128)S(1)} fusion(f32[4,256,256]{2,1,0:T(8,128)} %collective-permute-done.3, f32[1,256,256]{1,2,0:T(8,128)S(1)} %collective-permute-done.6), kind=kOutput, calls=%fused_computation.25 | convolution fusion | flops 805306368 | bytes 2359296 | tf_op jit(solution)/shard_map/ik,akl->ail/dot_general | solution.py:35
  148.3 0.0 collective-permute-done.7
  148.3 1.8 convolution_bitcast_fusion
  150.1 0.0 copy-done.1
  150.1 3.8 %multiply_reduce_fusion = (f32[]{:T(128)}, f32[256,256]{0,1:T(8,128)S(1)}) fusion(f32[1,14,256,256]{3,2,1,0:T(8,128)S(1)} %copy-done.1, f32[6,256,256]{1,2,0:T(8,128)S(1)} %fusion.21, f32[4,256,256]{1,2,0:T(8,128)S(1)} %convolution_bitcast_fusion, f32[4,256,256]{1,2,0:T(8,128)S(1)} %convolution_bitcast_fusion.1, f32[256,256]{0,1:T(8,128)S(1)} %get-tuple-element.40, ...), kind=kOutput, calls=%fused_computation.61 | convolution fusion | flops 2821455872 | bytes 8127497 | tf_op jit(solution)/shard_map/aij,ajl->il/dot_general | solution.py:39
  154.0 31.3 %psum.23 = f32[]{:T(128)} all-reduce(f32[]{:T(128)} %get-tuple-element.41), channel_id=1, replica_groups=mesh['real'=2,'row'=16] {'row'}, use_global_device_ids=true, to_apply=%region_9.10 | all-reduce | flops 1 | bytes 8 | tf_op jit(solution)/shard_map/psum | solution.py:77
  186.6 0.8 copy.10
  (14 shorter events, 0.3 us)
Async XLA Ops:
  3.8 13.7 %collective-permute-start = (f32[256,256]{0,1:T(8,128)S(1)}, f32[256,256]{0,1:T(8,128)S(1)}, u32[]{:S(2)}, u32[]{:S(2)}) collective-permute-start(f32[256,256]{0,1:T(8,128)S(1)} %bitcast_multiply_fusion), channel_id=1, source_target_pairs={{0,1},{1,2},{2,3},{3,4},{4,5},{5,6},{6,7},{7,8},{8,9},{9,10},{10,1... | collective-permute-start | bytes 786440 | tf_op jit(solution)/shard_map/ppermute | solution.py:30
  9.2 82.7 %collective-permute-start.5 = (f32[4,256,256]{2,1,0:T(8,128)}, f32[4,256,256]{2,1,0:T(8,128)S(1)}, u32[]{:S(2)}, u32[]{:S(2)}) collective-permute-start(f32[4,256,256]{2,1,0:T(8,128)} %get-tuple-element.27), channel_id=1, source_target_pairs={{1,0},{2,1},{3,2},{4,3},{5,4},{6,5},{7,6},{8,7},{9,8},{10,9},{11,1... | collective-permute-start | bytes 3145736 | tf_op jit(solution)/shard_map/ppermute | solution.py:30
  10.5 84.4 %collective-permute-start.3 = (f32[4,256,256]{2,1,0:T(8,128)}, f32[4,256,256]{2,1,0:T(8,128)}, u32[]{:S(2)}, u32[]{:S(2)}) collective-permute-start(f32[4,256,256]{2,1,0:T(8,128)} %get-tuple-element.26), channel_id=1, source_target_pairs={{0,1},{1,2},{2,3},{3,4},{4,5},{5,6},{6,7},{7,8},{8,9},{9,10},{10,1... | collective-permute-start | bytes 3145736 | tf_op jit(solution)/shard_map/ppermute | solution.py:30
  54.9 37.0 %collective-permute-start.4 = (f32[1,256,256]{1,2,0:T(8,128)}, f32[1,256,256]{1,2,0:T(8,128)}, u32[]{:S(2)}, u32[]{:S(2)}) collective-permute-start(f32[1,256,256]{1,2,0:T(8,128)} %fusion.84), channel_id=1, source_target_pairs={{1,0},{2,1},{3,2},{4,3},{5,4},{6,5},{7,6},{8,7},{9,8},{10,9},{11,1... | collective-permute-start | bytes 786440 | tf_op jit(solution)/shard_map/ppermute | solution.py:22
  56.2 38.7 %collective-permute-start.2 = (f32[1,256,256]{1,2,0:T(8,128)}, f32[1,256,256]{1,2,0:T(8,128)}, u32[]{:S(2)}, u32[]{:S(2)}) collective-permute-start(f32[1,256,256]{1,2,0:T(8,128)} %fusion.84), channel_id=1, source_target_pairs={{0,1},{1,2},{2,3},{3,4},{4,5},{5,6},{6,7},{7,8},{8,9},{9,10},{10,1... | collective-permute-start | bytes 786440 | tf_op jit(solution)/shard_map/ppermute | solution.py:19
  85.5 5.4 %collective-permute-start.1 = (f32[256,256]{0,1:T(8,128)S(1)}, f32[256,256]{0,1:T(8,128)S(1)}, u32[]{:S(2)}, u32[]{:S(2)}) collective-permute-start(f32[256,256]{0,1:T(8,128)S(1)} %get-tuple-element.29), channel_id=1, source_target_pairs={{1,0},{2,1},{3,2},{4,3},{5,4},{6,5},{7,6},{8,7},{9,8},{10,9},{11,1... | collective-permute-start | bytes 786440 | tf_op jit(solution)/shard_map/ppermute | solution.py:30
  92.0 6.1 %copy-start = (f32[1,14,256,256]{3,2,1,0:T(8,128)S(1)}, f32[1,14,256,256]{3,2,1,0:T(8,128)}, u32[]{:S(2)}) copy-start(f32[1,14,256,256]{3,2,1,0:T(8,128)} %param.5) | copy-start | bytes 11010052
  138.0 12.1 %copy-start.1 = (f32[1,14,256,256]{3,2,1,0:T(8,128)S(1)}, f32[1,14,256,256]{3,2,1,0:T(8,128)}, u32[]{:S(2)}) copy-start(f32[1,14,256,256]{3,2,1,0:T(8,128)} %param.5) | copy-start | bytes 11010052
  138.0 7.2 %collective-permute-start.6 = (f32[1,256,256]{1,2,0:T(8,128)S(1)}, f32[1,256,256]{1,2,0:T(8,128)S(1)}, u32[]{:S(2)}, u32[]{:S(2)}) collective-permute-start(f32[1,256,256]{1,2,0:T(8,128)S(1)} %fusion.75), channel_id=1, source_target_pairs={{0,1},{1,2},{2,3},{3,4},{4,5},{5,6},{6,7},{7,8},{8,9},{9,10},{10,1... | collective-permute-start | bytes 786440 | tf_op jit(solution)/shard_map/ppermute | solution.py:19
  139.6 8.7 %collective-permute-start.7 = (f32[1,256,256]{1,2,0:T(8,128)S(1)}, f32[1,256,256]{1,2,0:T(8,128)S(1)}, u32[]{:S(2)}, u32[]{:S(2)}) collective-permute-start(f32[1,256,256]{1,2,0:T(8,128)S(1)} %fusion.75), channel_id=1, source_target_pairs={{1,0},{2,1},{3,2},{4,3},{5,4},{6,5},{7,6},{8,7},{9,8},{10,9},{11,1... | collective-permute-start | bytes 786440 | tf_op jit(solution)/shard_map/ppermute | solution.py:22
where the time goes:
time: 188 us; the launch traced here: 187 us
  blocking collectives  66.1 us (35%)
  other arithmetic  56.2 us (30%)
  matrix products  29 us (15%)
  starting transfers between devices  19.7 us (10%)
  local copies, waits for them, and re-layouts  11.6 us (6%)
  between operations  4.75 us (3%)
    psum x1, blocking collectives, on_device(): correlation_sum = lax.psum(jnp.sum(bond_matrix * applied), 'row')  34.8 us
    another operation x6, other arithmetic, on_device(): factor = jnp.linalg.cholesky(gram_matrix)  33.9 us
    psum x1, blocking collectives, on_device(): final_norm = lax.psum(jnp.sum(evolved * evolved), 'row')  31.3 us
    another operation x3, other arithmetic, on_device(): jax.scipy.linalg.solve_triangular(factor, stacked.T, lower=True)  19.7 us
    ppermute x4, starting transfers between devices, shifted_2(): lax.ppermute(value, axis, [(source, source + steps) for source in range(l...  11.1 us
    dot_general x2, matrix products, apply_moved(): jnp.einsum('ik,akl->ail', operand, right_local[W_DN + W_UP:], precision=h...  8.2 us
    dot_general x2, matrix products, apply_moved(): jnp.einsum('aij,ajl->il', left_local, combined, precision=highest)  7.64 us
    dot_general x2, matrix products, apply_moved(): jnp.einsum('ik,akl->ail', bordered[0], right_down, precision=highest)  6.16 us
  transfers between devices with their start and end apart: 8, of which 0 were waited for; matrix products, arithmetic and copies ran while one was open for 43% of the time, Pallas kernels for 0%

commit v1 on v0

v1 whole, which is shorter than its diff:
```python
import jax
import jax.numpy as jnp
from jax import lax
from jax.sharding import PartitionSpec as P

W_DN = 4
W_UP = 4


highest = lax.Precision.HIGHEST
high = lax.Precision.HIGH
time_step = 0.15


def shifted_2(value, axis, steps):
    count = lax.axis_size(axis)
    leading, last = (max(0, -steps), min(count, count - steps))
    return lax.ppermute(value, axis, [(source, source + steps) for source in range(leading, last)])


def row_sum(partials):
    count = lax.axis_size("row")
    spread = jnp.broadcast_to(partials[None], (count,) + partials.shape)
    return jnp.sum(lax.all_to_all(spread, "row", 0, 0, tiled=True), 0)


def apply_moved(operand, left_local, right_local, right_down, right_upper, mask_pair):
    low = shifted_2(operand, "row", 1)
    upper = shifted_2(operand, "row", -1)
    own_terms = jnp.einsum("ik,akl->ail", operand, right_local[W_DN + W_UP :], precision=high)
    own = jnp.einsum("aij,ajl->il", left_local[W_DN + W_UP :], own_terms, precision=high)
    down_terms = jnp.einsum("ik,akl->ail", low, right_down, precision=high)
    upper_terms = jnp.einsum("ik,akl->ail", upper, right_upper, precision=high)
    moved = jnp.einsum("aij,ajl->il", left_local[:W_DN], down_terms, precision=high)
    moved += jnp.einsum("aij,ajl->il", left_local[W_DN : W_DN + W_UP], upper_terms, precision=high)
    return (own + moved) * mask_pair


def on_device(site_tensor, left_env, right_env, sector_size):
    states = site_tensor.shape[-1]
    left_local = left_env[0]
    right_local = right_env[0]
    own_size = lax.dynamic_index_in_dim(sector_size, lax.axis_index("row"), 0, keepdims=False)
    live_mask = (jnp.arange(states, dtype=jnp.int32) < own_size).astype(jnp.float32)
    mask_pair = live_mask[:, None] * live_mask[None, :]
    lower_source = site_tensor[0, 1] * live_mask[:, None]
    lower_block = shifted_2(lower_source, "row", 1) * live_mask[None, :]
    right_down = shifted_2(right_local[:W_DN], "row", 1)
    right_upper = shifted_2(right_local[W_DN : W_DN + W_UP], "row", -1)
    upper_block = site_tensor[0, 0] * mask_pair
    stacked = jnp.concatenate([upper_block, lower_block], 0)
    identity = jnp.eye(states, dtype=jnp.float32)
    gram_matrix = (
        jnp.einsum("ij,ik->jk", stacked, stacked, precision=highest)
        + identity * (1.0 - live_mask)[None, :]
    )
    factor = jnp.linalg.cholesky(gram_matrix)
    bond_matrix = factor.T * mask_pair

    def operator(operand):
        return apply_moved(operand, left_local, right_local, right_down, right_upper, mask_pair)

    orthonormal = jax.scipy.linalg.solve_triangular(factor, stacked.T, lower=True).T
    moved_back = shifted_2(orthonormal[states:], "row", -1)
    left_out = jnp.stack([orthonormal[:states], moved_back], 0)[None]

    applied = operator(bond_matrix)
    lanes = jnp.arange(128)[None]
    norm_row = jnp.where(lanes == 0, jnp.sum(bond_matrix * bond_matrix), 0.0)
    local_row = jnp.where(lanes == 1, jnp.sum(bond_matrix * applied), norm_row)
    sums = row_sum(local_row)
    start_norm = sums[0, 0]
    energy = sums[0, 1] / start_norm
    twice = operator(applied)
    shifted = applied - energy * bond_matrix
    second = twice - energy * applied - energy * shifted
    evolved = bond_matrix + time_step * shifted + 0.5 * time_step * time_step * second
    final_row = jnp.where(lanes == 0, jnp.sum(evolved * evolved), 0.0)
    final_norm = row_sum(final_row)[0, 0]
    return (left_out, (evolved * jnp.sqrt(start_norm / final_norm))[None])


def solution(mesh):
    placed = (
        P(("real", "row"), None, None, None),
        P(("real", "row"), None, None, None),
        P(("real", "row"), None, None, None),
        P("real"),
    )
    return jax.shard_map(
        on_device,
        mesh=mesh,
        in_specs=placed,
        out_specs=(P(("real", "row"), None, None, None), P(("real", "row"), None, None)),
        check_vma=False,
    )
```

time: 188 us -> 148 us (0.79)
  blocking collectives: 66.1 us -> 0 us
  starting transfers between devices: 19.7 us -> 34.5 us
  waiting for transfers between devices: 0.02 us -> 7.31 us
  local copies, waits for them, and re-layouts: 11.6 us -> 15.2 us
  other arithmetic: 56.2 us -> 59.1 us
  matrix products: 29 us -> 26.5 us
    psum x2 -> x0, blocking collectives: 66.1 us -> none  [the longest x1 34.8 us: on_device(): correlation_sum = lax.psum(jnp.sum(bond_matrix * applied), 'row')]
    all_to_all x0 -> x2, starting transfers between devices: none -> 11.7 us  [row_sum(): return jnp.sum(lax.all_to_all(spread, 'row', 0, 0, tiled=True), 0)]
    ppermute x4 -> x8, starting transfers between devices: 11.1 us -> 22.8 us  [shifted_2(): lax.ppermute(value, axis, [(source, source + steps) for source in range(l...]
    ppermute x4 -> x0, starting transfers between devices: 8.56 us -> none  [the longest x2 5.77 us: padded(): lax.ppermute(lax.slice_in_dim(block, block.shape[dim] - width, None, axis...]
    all_to_all x0 -> x2, waiting for transfers between devices: none -> 7.28 us  [row_sum(): return jnp.sum(lax.all_to_all(spread, 'row', 0, 0, tiled=True), 0)]
    dot_general x2, matrix products: 8.2 us -> 4.53 us  [apply_moved(): jnp.einsum('ik,akl->ail', operand, right_local[W_DN + W_UP:], precision=h...]
    select_n x0 -> x2, other arithmetic: none -> 1.93 us  [the longest x1 1.28 us: on_device(): local_row = jnp.where(lanes == 1, jnp.sum(bond_matrix * applied), norm_row)]
    dot_general x6 -> x10, matrix products: 18.5 us -> 19.7 us  [the longest x2 4.96 us: apply_moved(): jnp.einsum('aij,ajl->il', left_local[W_DN + W_UP:], own_terms, precision=...]
  transfers between devices with their start and end apart: 8 -> 10, of which waited for: 0 -> 2; matrix products, arithmetic and copies ran while one was open for 43% -> 66% of each run, Pallas kernels for 0% -> 0%
where the time goes in v1:
time: 148 us; the launch traced here: 147 us
  other arithmetic  59.1 us (40%)
  starting transfers between devices  34.5 us (23%)
  matrix products  26.5 us (18%)
  local copies, waits for them, and re-layouts  15.2 us (10%)
  waiting for transfers between devices  7.31 us (5%)
  between operations  4.22 us (3%)
    another operation x6, other arithmetic, on_device(): factor = jnp.linalg.cholesky(gram_matrix)  34 us
    ppermute x8, starting transfers between devices, shifted_2(): lax.ppermute(value, axis, [(source, source + steps) for source in range(l...  22.8 us
    another operation x3, other arithmetic, on_device(): jax.scipy.linalg.solve_triangular(factor, stacked.T, lower=True)  20.5 us
    all_to_all x2, starting transfers between devices, row_sum(): return jnp.sum(lax.all_to_all(spread, 'row', 0, 0, tiled=True), 0)  11.7 us
    all_to_all x2, waiting for transfers between devices, row_sum(): return jnp.sum(lax.all_to_all(spread, 'row', 0, 0, tiled=True), 0)  7.28 us
    another operation x6, local copies, waits for them, and re-layouts  4.97 us
    dot_general x2, matrix products, apply_moved(): jnp.einsum('aij,ajl->il', left_local[W_DN + W_UP:], own_terms, precision=...  4.96 us
    dot_general x2, matrix products, apply_moved(): jnp.einsum('aij,ajl->il', left_local[:W_DN], down_terms, precision=high)  4.57 us
  transfers between devices with their start and end apart: 10, of which 2 were waited for; matrix products, arithmetic and copies ran while one was open for 66% of the time, Pallas kernels for 0%

profile of v1, /device:TPU:0, one launch (start us, length us, event | category | flops | bytes accessed | tf_op | source)
XLA Modules:
  0.0 146.7 jit_solution(3189845369070765148)
XLA Ops:
  0.6 1.1 fusion.65
  1.7 1.2 dynamic_slice.4
  3.0 0.6 compare_convert_fusion
  3.6 0.1 copy.54
  3.7 2.4 %collective-permute-start = (f32[256,256]{0,1:T(8,128)S(1)}, f32[256,256]{0,1:T(8,128)S(1)}, u32[]{:S(2)}, u32[]{:S(2)}) collective-permute-start(f32[256,256]{0,1:T(8,128)S(1)} %bitcast_multiply_fusion), channel_id=1, source_target_pairs={{0,1},{1,2},{2,3},{3,4},{4,5},{5,6},{6,7},{7,8},{8,9},{9,10},{10,1... | collective-permute-start | bytes 786440 | tf_op jit(solution)/shard_map/ppermute | solution.py:18
  6.2 3.0 %slice_bitcast_fusion.1 = (f32[4,256,256]{2,1,0:T(8,128)}, f32[4,256,256]{2,1,0:T(8,128)}) fusion(f32[1,14,256,256]{3,2,1,0:T(8,128)} %param.6), kind=kLoop, calls=%fused_computation.44 | loop fusion | bytes 4194304 | tf_op jit(solution)/shard_map/slice | solution.py:48
  9.2 1.3 collective-permute-start.5
  10.5 5.2 %collective-permute-start.3 = (f32[4,256,256]{2,1,0:T(8,128)}, f32[4,256,256]{2,1,0:T(8,128)S(1)}, u32[]{:S(2)}, u32[]{:S(2)}) collective-permute-start(f32[4,256,256]{2,1,0:T(8,128)} %get-tuple-element.28), channel_id=1, source_target_pairs={{0,1},{1,2},{2,3},{3,4},{4,5},{5,6},{6,7},{7,8},{8,9},{9,10},{10,1... | collective-permute-start | bytes 3145736 | tf_op jit(solution)/shard_map/ppermute | solution.py:18
  15.7 0.1 copy.53
  15.8 0.6 broadcast_subtract_fusion
  16.5 0.1 multiply_multiply_fusion.1
  16.6 0.1 fusion.44
  16.7 0.6 fusion.45
  17.3 0.1 copy.18
  17.4 0.1 fusion.56
  17.5 11.7 %cholesky.49 = f32[128,128]{1,0:T(8,128)S(1)} custom-call(f32[128,128]{1,0:T(8,128)S(1)} %cholesky.115), custom_call_target="Cholesky" | custom-call | tf_op jit(solution)/shard_map/jit(cholesky)/cholesky | solution.py:57
  29.3 9.8 %custom-call.15 = f32[1,128,128]{1,2,0:T(8,128)S(1)} custom-call(f32[1,128,128]{2,1,0:T(8,128)S(1)} %get-tuple-element.37), custom_call_target="InvertDiagBlocksLowerTriangular" | custom-call | tf_op jit(solution)/shard_map/jit(cholesky)/cholesky | solution.py:57
  39.1 0.2 constant_dynamic-update-slice_fusion.1
  39.3 0.3 convolution_subtract_fusion
  39.6 11.7 %cholesky.103 = f32[128,128]{1,0:T(8,128)S(1)} custom-call(f32[128,128]{1,0:T(8,128)S(1)} %convolution_subtract_fusion), custom_call_target="Cholesky" | custom-call | tf_op jit(solution)/shard_map/jit(cholesky)/cholesky | solution.py:57
  51.4 0.6 compare_reduce_fusion
  53.2 0.1 multiply_multiply_fusion
  53.3 1.3 collective-permute-start.4
  54.6 4.9 %collective-permute-start.2 = (f32[256,256]{0,1:T(8,128)S(1)}, f32[256,256]{0,1:T(8,128)}, u32[]{:S(2)}, u32[]{:S(2)}) collective-permute-start(f32[256,256]{0,1:T(8,128)S(1)} %multiply_multiply_fusion), channel_id=1, source_target_pairs={{0,1},{1,2},{2,3},{3,4},{4,5},{5,6},{6,7},{7,8},{8,9},{9,10},{10,1... | collective-permute-start | bytes 786440 | tf_op jit(solution)/shard_map/ppermute | solution.py:18
  59.5 0.1 triangular_solve.63
  59.6 5.0 %while.1 = (s32[]{:T(128)}, f32[256,256]{1,0:T(8,128)S(1)}, s32[2,2]{1,0:T(2,128)S(1)}, f32[2,128,128]{2,1,0:T(8,128)}, s32[]{:T(128)}) while((s32[]{:T(128)}, f32[256,256]{1,0:T(8,128)S(1)}, s32[2,2]{1,0:T(2,128)S(1)}, f32[2,128,128]{2,1,0:T(8,128)}, s32[]{:T(128)}) %tuple.38), condition=%wide.while_cond, body=%wide.while_body.sunk | while | flops 2 | bytes 132205 | solution.py:63
  59.6 0.6 fusion.79
  60.2 1.9 %bitcast_dynamic-update-slice_fusion.2 = f32[2,128,128]{2,1,0:T(8,128)} fusion(f32[2,128,128]{2,1,0:T(8,128)} %get-tuple-element.86, s32[]{:T(128)S(6)} %copy.60, f32[256,256]{1,0:T(8,128)S(1)} %get-tuple-element.89, s32[]{:T(128)} %bitcast.183, s32[]{:T(128)} %bitcast.184), kind=kLoop, calls=%fused_computation.clone.1 | loop fusion | bytes 132100 | tf_op jit(solution)/shard_map/jit(_solve_triangular)/triangular_solve
  62.1 0.6 fusion.79
  62.7 1.9 %bitcast_dynamic-update-slice_fusion.2 = f32[2,128,128]{2,1,0:T(8,128)} fusion(f32[2,128,128]{2,1,0:T(8,128)} %get-tuple-element.86, s32[]{:T(128)S(6)} %copy.60, f32[256,256]{1,0:T(8,128)S(1)} %get-tuple-element.89, s32[]{:T(128)} %bitcast.183, s32[]{:T(128)} %bitcast.184), kind=kLoop, calls=%fused_computation.clone.1 | loop fusion | bytes 132100 | tf_op jit(solution)/shard_map/jit(_solve_triangular)/triangular_solve
  64.6 20.5 %custom-call.16 = f32[2,128,128]{1,2,0:T(8,128)S(1)} custom-call(f32[2,128,128]{2,1,0:T(8,128)} %get-tuple-element.9), custom_call_target="InvertDiagBlocksLowerTriangular" | custom-call | tf_op jit(solution)/shard_map/jit(_solve_triangular)/triangular_solve | solution.py:63
  85.1 0.0 copy-start
  85.1 0.4 fusion.47
  85.5 0.4 fusion.58
  85.9 0.4 fusion.46
  86.3 2.3 %fusion.8 = f32[256,6,256]{2,0,1:T(8,128)S(1)} fusion(f32[1,14,256,256]{3,2,1,0:T(8,128)} %param.6, f32[256,256]{0,1:T(8,128)S(1)} %multiply_multiply_fusion), kind=kOutput, calls=%fused_computation.10 | convolution fusion | flops 603979776 | bytes 3407872 | tf_op jit(solution)/shard_map/ik,akl->ail/dot_general | solution.py:30
  88.7 0.7 slice_bitcast_fusion.2
  89.4 1.3 collective-permute-start.1
  90.7 1.4 fusion.14
  92.2 0.0 collective-permute-done.4
  92.2 1.8 %convolution_bitcast_fusion.2 = f32[4,256,256]{2,1,0:T(8,128)S(1)} fusion(f32[4,256,256]{2,1,0:T(8,128)S(1)} %collective-permute-done.5, f32[256,256]{0,1:T(8,128)} %collective-permute-done.4), kind=kOutput, calls=%fused_computation.18 | convolution fusion | flops 402653184 | bytes 2359296 | tf_op jit(solution)/shard_map/ik,akl->ail/dot_general | solution.py:33
  94.0 1.0 convolution_bitcast_fusion.6
  95.0 1.6 %convolution_bitcast_fusion.3 = f32[4,256,256]{2,1,0:T(8,128)S(1)} fusion(f32[4,256,256]{2,1,0:T(8,128)S(1)} %collective-permute-done.3, f32[256,256]{0,1:T(8,128)} %collective-permute-done.2), kind=kOutput, calls=%fused_computation.19 | convolution fusion | flops 402653184 | bytes 2359296 | tf_op jit(solution)/shard_map/ik,akl->ail/dot_general | solution.py:32
  96.6 1.7 %multiply_reduce_fusion.2 = (f32[]{:T(128)}, f32[]{:T(128)}, f32[256,256]{0,1:T(8,128)S(1)}) fusion(f32[256,256]{0,1:T(8,128)S(1)} %multiply_multiply_fusion, f32[256]{0:T(256)S(1)} %compare_convert_fusion, f32[256,256]{1,0:T(8,128)S(1)} %fusion.14, f32[256,256]{1,0:T(8,128)S(1)} %convolution_bitcast_fusion.6, ...), kind=kOutput, calls=%fused_computation.74 | convolution fusion | flops 403177472 | bytes 3147784 | tf_op jit(solution)/shard_map/aij,ajl->il/dot_general | solution.py:34
  98.3 2.3 %fusion.6 = f32[256,6,256]{2,0,1:T(8,128)S(1)} fusion(f32[1,14,256,256]{3,2,1,0:T(8,128)} %param.6, f32[256,256]{0,1:T(8,128)S(1)} %get-tuple-element.44), kind=kOutput, calls=%fused_computation.8 | convolution fusion | flops 603979776 | bytes 3407872 | tf_op jit(solution)/shard_map/ik,akl->ail/dot_general | solution.py:30
  100.6 1.3 collective-permute-start.7
  101.9 5.1 %collective-permute-start.6 = (f32[256,256]{0,1:T(8,128)S(1)}, f32[256,256]{0,1:T(8,128)}, u32[]{:S(2)}, u32[]{:S(2)}) collective-permute-start(f32[256,256]{0,1:T(8,128)S(1)} %get-tuple-element.44), channel_id=1, source_target_pairs={{0,1},{1,2},{2,3},{3,4},{4,5},{5,6},{6,7},{7,8},{8,9},{9,10},{10,1... | collective-permute-start | bytes 786440 | tf_op jit(solution)/shard_map/ppermute | solution.py:18
  106.9 1.3 compare_select_fusion
  108.2 0.6 broadcast_in_dim.46
  108.8 8.3 %all-to-all-start = ((f32[16,1,128]{2,1,0:T(1,128)}), f32[16,1,128]{2,1,0:T(1,128)S(1)}, u32[]{:S(2)}, u32[]{:S(2)}) async-start(f32[16,1,128]{2,1,0:T(1,128)} %broadcast_in_dim.46), calls=%async_computation | async-start | bytes 16384 | tf_op jit(solution)/shard_map/all_to_all | solution.py:24
  117.1 3.5 %fusion.19 = f32[256,256]{1,0:T(8,128)} fusion(f32[1,14,256,256]{3,2,1,0:T(8,128)} %param.5, f32[256,6,256]{2,0,1:T(8,128)S(1)} %fusion.6), kind=kOutput, calls=%fused_computation.21 | convolution fusion | flops 603979776 | bytes 3407872 | tf_op jit(solution)/shard_map/aij,ajl->il/dot_general | solution.py:31
  120.6 2.9 %all-to-all-done = f32[16,1,128]{2,1,0:T(1,128)S(1)} async-done(((f32[16,1,128]{2,1,0:T(1,128)}), f32[16,1,128]{2,1,0:T(1,128)S(1)}, u32[]{:S(2)}, u32[]{:S(2)}) %all-to-all-start) | async-done | bytes 8224 | tf_op jit(solution)/shard_map/all_to_all | solution.py:24
  123.6 0.6 fusion.66
  125.4 1.9 %convolution_bitcast_fusion = f32[4,256,256]{2,1,0:T(8,128)S(1)} fusion(f32[4,256,256]{2,1,0:T(8,128)} %copy-done.1, f32[256,256]{0,1:T(8,128)} %collective-permute-done.7), kind=kOutput, calls=%fused_computation.16 | convolution fusion | flops 402653184 | bytes 2359296 | tf_op jit(solution)/shard_map/ik,akl->ail/dot_general | solution.py:33
  127.3 2.2 %convolution_bitcast_fusion.4 = f32[256,256]{1,0:T(8,128)S(1)} fusion(f32[4,256,256]{2,1,0:T(8,128)S(1)} %convolution_bitcast_fusion, f32[1,14,256,256]{3,2,1,0:T(8,128)} %param.5), kind=kOutput, calls=%fused_computation.22 | convolution fusion | flops 402653184 | bytes 2359296 | tf_op jit(solution)/shard_map/aij,ajl->il/dot_general | solution.py:35
  129.6 1.6 %convolution_bitcast_fusion.1 = f32[4,256,256]{2,1,0:T(8,128)S(1)} fusion(f32[4,256,256]{2,1,0:T(8,128)S(1)} %collective-permute-done.3, f32[256,256]{0,1:T(8,128)} %collective-permute-done.6), kind=kOutput, calls=%fused_computation.17 | convolution fusion | flops 402653184 | bytes 2359296 | tf_op jit(solution)/shard_map/ik,akl->ail/dot_general | solution.py:32
  131.2 2.9 %multiply_reduce_fusion = (f32[]{:T(128)}, f32[256,256]{0,1:T(8,128)S(1)}) fusion(f32[256,256]{0,1:T(8,128)S(1)} %get-tuple-element.44, f32[256]{0:T(256)S(1)} %compare_convert_fusion, f32[256,256]{1,0:T(8,128)S(1)} %copy-done.2, f32[256,256]{1,0:T(8,128)S(1)} %convolution_bitcast_fusion.4, f32[4,256,256]{2,1,0:T(8,128)S(1)} %convolution_bitcast_fusion.1, ...), kind=kOutput, calls=%fused_computation.72 | convolution fusion | flops 403701760 | bytes 3410436 | tf_op jit(solution)/shard_map/aij,ajl->il/dot_general | solution.py:34
  134.0 0.6 compare_select_fusion.1
  134.7 0.6 broadcast_in_dim.48
  135.3 3.4 %all-to-all-start.1 = ((f32[16,1,128]{2,1,0:T(1,128)}), f32[16,1,128]{2,1,0:T(1,128)S(1)}, u32[]{:S(2)}, u32[]{:S(2)}) async-start(f32[16,1,128]{2,1,0:T(1,128)} %broadcast_in_dim.48), calls=%async_computation.1 | async-start | bytes 16384 | tf_op jit(solution)/shard_map/all_to_all | solution.py:24
  138.8 1.0 maximum_bitcast_fusion.1
  139.7 1.0 copy.33
  140.7 4.4 %all-to-all-done.1 = f32[16,1,128]{2,1,0:T(1,128)S(1)} async-done(((f32[16,1,128]{2,1,0:T(1,128)}), f32[16,1,128]{2,1,0:T(1,128)S(1)}, u32[]{:S(2)}, u32[]{:S(2)}) %all-to-all-start.1) | async-done | bytes 8224 | tf_op jit(solution)/shard_map/all_to_all | solution.py:24
  145.9 0.8 copy.34
  (26 shorter events, 0.3 us)
Async XLA Ops:
  3.7 12.7 %collective-permute-start = (f32[256,256]{0,1:T(8,128)S(1)}, f32[256,256]{0,1:T(8,128)S(1)}, u32[]{:S(2)}, u32[]{:S(2)}) collective-permute-start(f32[256,256]{0,1:T(8,128)S(1)} %bitcast_multiply_fusion), channel_id=1, source_target_pairs={{0,1},{1,2},{2,3},{3,4},{4,5},{5,6},{6,7},{7,8},{8,9},{9,10},{10,1... | collective-permute-start | bytes 786440 | tf_op jit(solution)/shard_map/ppermute | solution.py:18
  9.2 83.0 %collective-permute-start.5 = (f32[4,256,256]{2,1,0:T(8,128)}, f32[4,256,256]{2,1,0:T(8,128)S(1)}, u32[]{:S(2)}, u32[]{:S(2)}) collective-permute-start(f32[4,256,256]{2,1,0:T(8,128)} %get-tuple-element.29), channel_id=1, source_target_pairs={{1,0},{2,1},{3,2},{4,3},{5,4},{6,5},{7,6},{8,7},{9,8},{10,9},{11,1... | collective-permute-start | bytes 3145736 | tf_op jit(solution)/shard_map/ppermute | solution.py:18
  10.5 84.5 %collective-permute-start.3 = (f32[4,256,256]{2,1,0:T(8,128)}, f32[4,256,256]{2,1,0:T(8,128)S(1)}, u32[]{:S(2)}, u32[]{:S(2)}) collective-permute-start(f32[4,256,256]{2,1,0:T(8,128)} %get-tuple-element.28), channel_id=1, source_target_pairs={{0,1},{1,2},{2,3},{3,4},{4,5},{5,6},{6,7},{7,8},{8,9},{9,10},{10,1... | collective-permute-start | bytes 3145736 | tf_op jit(solution)/shard_map/ppermute | solution.py:18
  53.3 38.8 %collective-permute-start.4 = (f32[256,256]{0,1:T(8,128)S(1)}, f32[256,256]{0,1:T(8,128)}, u32[]{:S(2)}, u32[]{:S(2)}) collective-permute-start(f32[256,256]{0,1:T(8,128)S(1)} %multiply_multiply_fusion), channel_id=1, source_target_pairs={{1,0},{2,1},{3,2},{4,3},{5,4},{6,5},{7,6},{8,7},{9,8},{10,9},{11,1... | collective-permute-start | bytes 786440 | tf_op jit(solution)/shard_map/ppermute | solution.py:18
  54.6 40.4 %collective-permute-start.2 = (f32[256,256]{0,1:T(8,128)S(1)}, f32[256,256]{0,1:T(8,128)}, u32[]{:S(2)}, u32[]{:S(2)}) collective-permute-start(f32[256,256]{0,1:T(8,128)S(1)} %multiply_multiply_fusion), channel_id=1, source_target_pairs={{0,1},{1,2},{2,3},{3,4},{4,5},{5,6},{6,7},{7,8},{8,9},{9,10},{10,1... | collective-permute-start | bytes 786440 | tf_op jit(solution)/shard_map/ppermute | solution.py:18
  85.1 5.6 %copy-start = (f32[1,14,256,256]{3,2,1,0:T(8,128)S(1)}, f32[1,14,256,256]{3,2,1,0:T(8,128)}, u32[]{:S(2)}) copy-start(f32[1,14,256,256]{3,2,1,0:T(8,128)} %param.5) | copy-start | bytes 11010052
  89.4 49.4 %collective-permute-start.1 = (f32[256,256]{0,1:T(8,128)}, f32[256,256]{0,1:T(8,128)}, u32[]{:S(2)}, u32[]{:S(2)}) collective-permute-start(f32[256,256]{0,1:T(8,128)} %get-tuple-element.31), channel_id=1, source_target_pairs={{1,0},{2,1},{3,2},{4,3},{5,4},{6,5},{7,6},{8,7},{9,8},{10,9},{11,1... | collective-permute-start | bytes 786440 | tf_op jit(solution)/shard_map/ppermute | solution.py:18
  92.2 6.1 %copy-start.1 = (f32[4,256,256]{2,1,0:T(8,128)}, f32[4,256,256]{2,1,0:T(8,128)S(1)}, u32[]{:S(2)}) copy-start(f32[4,256,256]{2,1,0:T(8,128)S(1)} %collective-permute-done.5) | copy-start | bytes 3145732
  100.6 24.8 %collective-permute-start.7 = (f32[256,256]{0,1:T(8,128)S(1)}, f32[256,256]{0,1:T(8,128)}, u32[]{:S(2)}, u32[]{:S(2)}) collective-permute-start(f32[256,256]{0,1:T(8,128)S(1)} %get-tuple-element.44), channel_id=1, source_target_pairs={{1,0},{2,1},{3,2},{4,3},{5,4},{6,5},{7,6},{8,7},{9,8},{10,9},{11,1... | collective-permute-start | bytes 786440 | tf_op jit(solution)/shard_map/ppermute | solution.py:18
  101.9 27.7 %collective-permute-start.6 = (f32[256,256]{0,1:T(8,128)S(1)}, f32[256,256]{0,1:T(8,128)}, u32[]{:S(2)}, u32[]{:S(2)}) collective-permute-start(f32[256,256]{0,1:T(8,128)S(1)} %get-tuple-element.44), channel_id=1, source_target_pairs={{0,1},{1,2},{2,3},{3,4},{4,5},{5,6},{6,7},{7,8},{8,9},{9,10},{10,1... | collective-permute-start | bytes 786440 | tf_op jit(solution)/shard_map/ppermute | solution.py:18
  108.8 14.7 %all-to-all-start = ((f32[16,1,128]{2,1,0:T(1,128)}), f32[16,1,128]{2,1,0:T(1,128)S(1)}, u32[]{:S(2)}, u32[]{:S(2)}) async-start(f32[16,1,128]{2,1,0:T(1,128)} %broadcast_in_dim.46), calls=%async_computation | async-start | bytes 16384 | tf_op jit(solution)/shard_map/all_to_all | solution.py:24
  120.6 10.5 %copy-start.2 = (f32[256,256]{1,0:T(8,128)S(1)}, f32[256,256]{1,0:T(8,128)}, u32[]{:S(2)}) copy-start(f32[256,256]{1,0:T(8,128)} %fusion.19) | copy-start | bytes 786436
  135.3 9.8 %all-to-all-start.1 = ((f32[16,1,128]{2,1,0:T(1,128)}), f32[16,1,128]{2,1,0:T(1,128)S(1)}, u32[]{:S(2)}, u32[]{:S(2)}) async-start(f32[16,1,128]{2,1,0:T(1,128)} %broadcast_in_dim.48), calls=%async_computation.1 | async-start | bytes 16384 | tf_op jit(solution)/shard_map/all_to_all | solution.py:24

commit v2 on v0

v2 whole, which is shorter than its diff:
```python
import functools

import jax
import jax.numpy as jnp
from jax import lax
from jax.experimental import pallas as pl
from jax.experimental.pallas import tpu as pltpu
from jax.sharding import PartitionSpec as P

W_DN = 4
W_UP = 4
PANEL = 16
LANES = 128

f32, bf16 = jnp.float32, jnp.bfloat16
time_step = 0.15

VM = pl.BlockSpec(memory_space=pltpu.VMEM)
SM = pl.BlockSpec(memory_space=pltpu.SMEM)
ANY = pl.BlockSpec(memory_space=pl.ANY)
HB = pl.BlockSpec(memory_space=pltpu.HBM)


def params(mib):
    return pltpu.CompilerParams(vmem_limit_bytes=mib << 20)


def split2(x):
    hi = x.astype(bf16)
    return hi, (x - hi.astype(f32)).astype(bf16)


def split3(x):
    hi = x.astype(bf16)
    rest = x - hi.astype(f32)
    mid = rest.astype(bf16)
    return hi, mid, (rest - mid.astype(f32)).astype(bf16)


def dot(a, b, ca=1, cb=0):
    return lax.dot_general(a, b, (((ca,), (cb,)), ((), ())), preferred_element_type=f32)


def dot3(a, b):
    ah, al = a
    bh, bl = b
    return dot(ah, bh) + dot(al, bh) + dot(ah, bl)


def dot6(a, b, cb=0):
    ah, am, al = a
    bh, bm, bl = b
    pairs = ((ah, bh), (ah, bm), (am, bh), (am, bm), (ah, bl), (al, bh))
    return sum(dot(x, y, 1, cb) for x, y in pairs)


def places(n, rows=None):
    shape = (n if rows is None else rows, n)
    return lax.broadcasted_iota(jnp.int32, shape, 0), lax.broadcasted_iota(jnp.int32, shape, 1)


def own_sizes(sizes):
    q = lax.axis_index("row")
    return q, sizes[q], sizes[jnp.maximum(q - 1, 0)]


def pick_kernel(right, after, out, sem, *, far):
    odd = lax.rem(lax.axis_index("row"), 2)
    first = (1 - odd if far else odd) * W_DN
    copy = pltpu.make_async_copy(right.at[0, pl.ds(first, W_UP)], out, sem.at[0])
    copy.start()
    copy.wait()


def pick(right, after, far):
    n = right.shape[-1]
    return pl.pallas_call(
        functools.partial(pick_kernel, far=far),
        out_shape=jax.ShapeDtypeStruct((W_UP, n, n), f32),
        in_specs=[HB, ANY],
        out_specs=ANY,
        scratch_shapes=[pltpu.SemaphoreType.DMA((1,))],
        compiler_params=params(4),
        name="pick",
    )(pltpu.with_memory_space_constraint(right, pltpu.HBM), after)


def factor_kernel(sizes, site, lower, bond, inv0, packed, work, turn, rows, erows, lstack, rstack):
    n = lower.shape[-1]
    _, own, prev = own_sizes(sizes)
    row_id, col_id = places(n)
    live_col = col_id < own
    top = jnp.where(live_col & (row_id < own), site[0, 0], 0.0)
    bot = jnp.where(live_col & (row_id < prev), lower[...], 0.0)
    gram = jnp.where((row_id == col_id) & (row_id >= own), 1.0, 0.0)
    for part in (top, bot):
        gram = gram + dot6(split3(part.T), split3(part))
    work[pl.ds(0, n), :] = gram
    work[pl.ds(n, PANEL), :] = jnp.zeros((PANEL, n), f32)
    lstack[...] = jnp.zeros(lstack.shape, bf16)
    rstack[...] = jnp.zeros(rstack.shape, bf16)
    inv0[...] = jnp.zeros((n, n), f32)
    lane = lax.broadcasted_iota(jnp.int32, (PANEL, LANES), 1)
    sub = lax.broadcasted_iota(jnp.int32, (PANEL, LANES), 0)
    tiles = n // LANES

    def body(p, carry):
        r0 = pl.multiple_of(p * PANEL, PANEL)
        tile = pl.multiple_of((r0 // LANES) * LANES, LANES)
        off = r0 - tile
        after = r0 + PANEL
        ntile = pl.multiple_of(jnp.minimum((after // LANES) * LANES, n - LANES), LANES)
        noff = pl.multiple_of(lax.rem(after, LANES), PANEL)
        w = work[pl.ds(r0, PANEL), :]
        diag = work[pl.ds(r0, PANEL), pl.ds(tile, LANES)]
        turn[...] = work[pl.ds(r0, PANEL), pl.ds(ntile, LANES)].T
        update = dot(lstack[...], rstack[...], 0, 0)
        ahead = turn[pl.ds(noff, PANEL), :]
        here, there = [], []
        for j in range(PANEL):
            at = jnp.full((PANEL, LANES), off + j, jnp.int32)
            here.append(jnp.take_along_axis(diag, at, axis=1, mode="promise_in_bounds"))
            there.append(jnp.broadcast_to(ahead[:, j : j + 1], (PANEL, LANES)))
        ext = jnp.where(lane == off + sub, 1.0, 0.0)
        acc = jnp.zeros((PANEL, n), f32)
        for k in range(PANEL):
            scale = lax.rsqrt(jnp.broadcast_to(here[k][k : k + 1, :], (PANEL, LANES)))
            a = here[k] * scale
            b = there[k] * scale
            rk = w[k : k + 1, :] * jnp.concatenate([scale[:1]] * tiles, 1)
            ek = ext[k : k + 1, :] * scale[:1]
            rows[k : k + 1, :] = rk
            erows[k : k + 1, :] = ek
            spread = jnp.broadcast_to(rk, (PANEL, n))
            acc = acc + jnp.concatenate([b] * tiles, 1) * spread
            if k + 1 < PANEL:
                w = w - jnp.concatenate([a] * tiles, 1) * spread
                ext = ext - a * jnp.broadcast_to(ek, (PANEL, LANES))
            for j in range(k + 1, PANEL):
                s = jnp.broadcast_to(a[j : j + 1, :], (PANEL, LANES))
                here[j] = here[j] - a * s
                there[j] = there[j] - b * s
        work[pl.ds(0, n), :] = work[pl.ds(0, n), :] - update
        work[pl.ds(after, PANEL), :] = work[pl.ds(after, PANEL), :] - acc
        r = rows[...]
        inv0[pl.ds(r0, PANEL), pl.ds(tile, LANES)] = erows[...]
        h, m, l = split3(r)
        for i, (x, y) in enumerate(((h, h), (m, h), (h, m), (m, m), (l, h), (h, l))):
            lstack[pl.ds(i * PANEL, PANEL), :] = x
            rstack[pl.ds(i * PANEL, PANEL), :] = y
        rid, cid = places(n, PANEL)
        rid = rid + r0
        bond[pl.ds(r0, PANEL), :] = jnp.where((cid >= rid) & (rid < own) & (cid < own), r, 0.0)
        return carry

    lax.fori_loop(0, n // PANEL, body, 0)
    at = 0
    for i in range(tiles):
        for j in range(i, tiles):
            packed[pl.ds(at, LANES), :] = bond[pl.ds(i * LANES, LANES), pl.ds(j * LANES, LANES)]
            at += LANES


def factor(sizes, site, lower):
    n = lower.shape[-1]
    tiles = n // LANES
    return pl.pallas_call(
        factor_kernel,
        out_shape=[jax.ShapeDtypeStruct((n, n), f32)] * 2
        + [jax.ShapeDtypeStruct((tiles * (tiles + 1) // 2 * LANES, LANES), f32)],
        in_specs=[SM, VM, VM],
        out_specs=[VM] * 3,
        scratch_shapes=[
            pltpu.VMEM((n + PANEL, n), f32),
            pltpu.VMEM((LANES, PANEL), f32),
            pltpu.VMEM((PANEL, n), f32),
            pltpu.VMEM((PANEL, LANES), f32),
            pltpu.VMEM((6 * PANEL, n), bf16),
            pltpu.VMEM((6 * PANEL, n), bf16),
        ],
        compiler_params=params(12),
        name="factor",
    )(sizes, site, lower)


def inverse_kernel(bond, inv0, out):
    n = bond.shape[-1]
    rid, cid = places(n)
    low_tri = bond[...].T
    x = inv0[...]
    size = PANEL
    while size < n:
        off = (rid // (2 * size) == cid // (2 * size)) & (rid // size > cid // size)
        part = split3(jnp.where(off, low_tri, 0.0))
        xs = split3(x)
        x = x - dot6(xs, split3(dot6(part, xs)))
        size *= 2
    out[...] = x


def inverse(bond, inv0):
    n = bond.shape[-1]
    return pl.pallas_call(
        inverse_kernel,
        out_shape=jax.ShapeDtypeStruct((n, n), f32),
        in_specs=[VM] * 2,
        out_specs=VM,
        compiler_params=params(16),
        name="inverse",
    )(bond, inv0)


def ortho_kernel(sizes, inv, site, lower, top_out, low_out):
    n = inv.shape[-1]
    _, own, prev = own_sizes(sizes)
    rid, cid = places(n)
    xs = split3(inv[...])
    live_col = cid < own
    low_out[...] = dot6(split3(jnp.where(live_col & (rid < prev), lower[...], 0.0)), xs, 1)
    top_out[...] = dot6(split3(jnp.where(live_col & (rid < own), site[0, 0], 0.0)), xs, 1)


def ortho(sizes, inv, site, lower):
    n = inv.shape[-1]
    return pl.pallas_call(
        ortho_kernel,
        out_shape=[jax.ShapeDtypeStruct((n, n), f32)] * 2,
        in_specs=[SM] + [VM] * 3,
        out_specs=[VM] * 2,
        compiler_params=params(16),
        name="ortho",
    )(sizes, inv, site, lower)


def channel(left, a, field, right):
    return dot3(split2(left[0, a]), split2(dot3(field, split2(right))))


def own_kernel(field, left, right, out):
    f = split2(field[...])
    total = None
    for a in range(W_DN + W_UP, left.shape[1]):
        term = channel(left, a, f, right[0, a])
        total = term if total is None else total + term
    out[...] = total


def own_terms(field, left, right):
    n = field.shape[-1]
    return pl.pallas_call(
        own_kernel,
        out_shape=jax.ShapeDtypeStruct((n, n), f32),
        in_specs=[VM] * 3,
        out_specs=VM,
        compiler_params=params(16),
        name="own",
    )(field, left, right)


def unpacked(ref, n):
    if ref.shape[-1] == n:
        return ref[...]
    tiles, at, rows = n // LANES, 0, []
    for i in range(tiles):
        row = [jnp.zeros((LANES, LANES), f32)] * i
        for _ in range(i, tiles):
            row.append(ref[pl.ds(at, LANES), :])
            at += LANES
        rows.append(jnp.concatenate(row, 1))
    return jnp.concatenate(rows, 0)


def moved_total(near, far, left, right_near, right_far, part, own):
    odd = lax.rem(lax.axis_index("row"), 2)
    total = part[...]
    for field, right, base in ((near, right_near, (1 - odd) * W_DN), (far, right_far, odd * W_DN)):
        f = split2(unpacked(field, part.shape[-1]))
        for a in range(right.shape[0]):
            total = total + channel(left, base + a, f, right[a])
    rid, cid = places(part.shape[-1])
    return jnp.where((rid < own) & (cid < own), total, 0.0)


def first_kernel(sizes, near, far, left, right_near, right_far, part, out):
    _, own, _ = own_sizes(sizes)
    out[...] = moved_total(near, far, left, right_near, right_far, part, own)


def first_apply(sizes, near, far, left, right_near, right_far, part):
    n = part.shape[-1]
    return pl.pallas_call(
        first_kernel,
        out_shape=jax.ShapeDtypeStruct((n, n), f32),
        in_specs=[SM] + [VM] * 6,
        out_specs=VM,
        compiler_params=params(16),
        name="first",
    )(sizes, near, far, left, right_near, right_far, part)


def second_kernel(sizes, near, far, left, right_near, right_far, part, bond, applied, out, spread):
    _, own, _ = own_sizes(sizes)
    twice = moved_total(near, far, left, right_near, right_far, part, own)
    out[...] = twice
    basis = (bond[...], time_step * applied[...], (0.5 * time_step * time_step) * twice)
    sums = []
    for i in range(3):
        for j in range(i, 3):
            line = jnp.sum(basis[i] * basis[j], 0, keepdims=True)
            sums.append(sum(line[:, t : t + LANES] for t in range(0, line.shape[1], LANES)))
    block = jnp.concatenate(sums + [jnp.zeros((2, LANES), f32)], 0)
    for i in range(spread.shape[0]):
        spread[i] = block


def second_apply(sizes, near, far, left, right_near, right_far, part, bond, applied, count):
    n = part.shape[-1]
    return pl.pallas_call(
        second_kernel,
        out_shape=[
            jax.ShapeDtypeStruct((n, n), f32),
            jax.ShapeDtypeStruct((count, 8, LANES), f32),
        ],
        in_specs=[SM] + [VM] * 8,
        out_specs=[VM, VM],
        compiler_params=params(16),
        name="second",
    )(sizes, near, far, left, right_near, right_far, part, bond, applied)


def stack_kernel(top, back, out, sems):
    top_copy = pltpu.make_async_copy(top, out.at[0, 0], sems.at[0])
    back_copy = pltpu.make_async_copy(back, out.at[0, 1], sems.at[1])
    top_copy.start()
    back_copy.start()
    top_copy.wait()
    back_copy.wait()


def stack(top, back):
    n = top.shape[-1]
    return pl.pallas_call(
        stack_kernel,
        out_shape=jax.ShapeDtypeStruct((1, 2, n, n), f32),
        in_specs=[ANY] * 2,
        out_specs=ANY,
        scratch_shapes=[pltpu.SemaphoreType.DMA((2,))],
        compiler_params=params(4),
        name="stack",
    )(top, back)


def final_kernel(gathered, bond, applied, twice, out):
    sums = jnp.sum(jnp.sum(gathered[...], 0), 1, keepdims=True)
    bb, ba, bt, aa, at, tt = (jnp.broadcast_to(sums[i : i + 1, :], (1, bond.shape[-1])) for i in range(6))
    rate = ba / bb
    c0 = 1.0 - rate + 0.5 * rate * rate
    c1 = 1.0 - rate
    norm = c0 * (c0 * bb + 2.0 * (c1 * ba + bt)) + c1 * (c1 * aa + 2.0 * at) + tt
    scale = jnp.sqrt(bb / norm)
    steps = (c0 * scale, (c1 * time_step) * scale, (0.5 * time_step * time_step) * scale)
    out[0] = steps[0] * bond[...] + steps[1] * applied[...] + steps[2] * twice[...]


def final(gathered, bond, applied, twice):
    n = bond.shape[-1]
    return pl.pallas_call(
        final_kernel,
        out_shape=jax.ShapeDtypeStruct((1, n, n), f32),
        in_specs=[VM] * 4,
        out_specs=VM,
        compiler_params=params(4),
        name="final",
    )(gathered, bond, applied, twice)


def shifted_by(value, steps):
    count = lax.axis_size("row")
    first, last = max(0, -steps), min(count, count - steps)
    return lax.ppermute(value, "row", [(source, source + steps) for source in range(first, last)])


def swapped(value, first):
    count = lax.axis_size("row")
    pairs = [(i, i + 1) for i in range(first, count - 1, 2)]
    return lax.ppermute(value, "row", pairs + [(j, i) for i, j in pairs])


def bond_update(site, left, right, sizes):
    count = lax.axis_size("row")
    source = site[0, 1]
    lower = shifted_by(source, 1)
    to_far = pick(right, source, True)
    right_far = swapped(to_far, 1)
    to_near = pick(right, source, False)
    right_near = swapped(to_near, 0)
    bond, inv0, packed = factor(sizes, site, lower)
    far = swapped(packed, 1)
    near = swapped(packed, 0)
    part = own_terms(bond, left, right)
    inv = inverse(bond, inv0)
    applied = first_apply(sizes, near, far, left, right_near, right_far, part)
    far = swapped(applied, 1)
    near = swapped(applied, 0)
    part = own_terms(applied, left, right)
    top, low = ortho(sizes, inv, site, lower)
    back = shifted_by(low, -1)
    twice, spread = second_apply(sizes, near, far, left, right_near, right_far, part, bond, applied, count)
    gathered = lax.all_to_all(spread, "row", 0, 0, tiled=True)
    left_out = stack(top, back)
    bond_out = final(gathered, bond, applied, twice)
    return left_out, bond_out


def solution(mesh):
    placed = (
        P(("real", "row"), None, None, None),
        P(("real", "row"), None, None, None),
        P(("real", "row"), None, None, None),
        P("real"),
    )
    return jax.shard_map(
        bond_update,
        mesh=mesh,
        in_specs=placed,
        out_specs=(P(("real", "row"), None, None, None), P(("real", "row"), None, None)),
        check_vma=False,
    )
```

time: 188 us -> 85.2 us (0.45)
  blocking collectives: 66.1 us -> 0 us
  other arithmetic: 56.2 us -> 0 us
  starting transfers between devices: 19.7 us -> 48.7 us
  matrix products: 29 us -> 0 us
  Pallas kernels: 0 us -> 27.1 us
  local copies, waits for them, and re-layouts: 11.6 us -> 1 us
  waiting for transfers between devices: 0.02 us -> 7.22 us
  between operations: 4.75 us -> 0.86 us
    psum x2 -> x0, blocking collectives: 66.1 us -> none  [the longest x1 34.8 us: on_device(): correlation_sum = lax.psum(jnp.sum(bond_matrix * applied), 'row')]
    another operation x9 -> x0, other arithmetic: 53.7 us -> none  [the longest x6 33.9 us: on_device(): factor = jnp.linalg.cholesky(gram_matrix)]
    dot_general x9 -> x0, matrix products: 27.3 us -> none  [the longest x2 8.2 us: apply_moved(): jnp.einsum('ik,akl->ail', operand, right_local[W_DN + W_UP:], precision=h...]
    pallas_call x0 -> x11, Pallas kernels: none -> 27.1 us  [the longest x1 7.69 us: factor(): pl.pallas_call(factor_kernel, out_shape=[jax.ShapeDtypeStruct((n, n), f32...]
    ppermute x8, starting transfers between devices: 19.7 us -> 39.3 us  [the longest x6 32.1 us: swapped(): return lax.ppermute(value, 'row', pairs + [(j, i) for i, j in pairs])]
    all_to_all x0 -> x1, starting transfers between devices: none -> 9.4 us  [bond_update(): gathered = lax.all_to_all(spread, 'row', 0, 0, tiled=True)]
    all_to_all x0 -> x1, waiting for transfers between devices: none -> 6.07 us  [bond_update(): gathered = lax.all_to_all(spread, 'row', 0, 0, tiled=True)]
    slice x2 -> x0, local copies, waits for them, and re-layouts: 4.1 us -> none  [the longest x1 3.03 us: on_device(): right_down = shifted_2(right_local[:W_DN], 'row', 1)]
  transfers between devices with their start and end apart: 8 -> 9, of which waited for: 0 -> 2; matrix products, arithmetic and copies ran while one was open for 43% -> 0% of each run, Pallas kernels for 0% -> 26%
where the time goes in v2:
time: 85.2 us; the launch traced here: 84.9 us
  starting transfers between devices  48.7 us (57%)
  Pallas kernels  27.1 us (32%)
  waiting for transfers between devices  7.22 us (8%)
  local copies, waits for them, and re-layouts  1 us (1%)
  between operations  0.86 us (1%)
    ppermute x6, starting transfers between devices, swapped(): return lax.ppermute(value, 'row', pairs + [(j, i) for i, j in pairs])  32.1 us
    all_to_all x1, starting transfers between devices, bond_update(): gathered = lax.all_to_all(spread, 'row', 0, 0, tiled=True)  9.4 us
    pallas_call x1, Pallas kernels, factor(): pl.pallas_call(factor_kernel, out_shape=[jax.ShapeDtypeStruct((n, n), f32...  7.69 us
    ppermute x2, starting transfers between devices, shifted_by(): lax.ppermute(value, 'row', [(source, source + steps) for source in range(...  7.14 us
    all_to_all x1, waiting for transfers between devices, bond_update(): gathered = lax.all_to_all(spread, 'row', 0, 0, tiled=True)  6.07 us
    pallas_call x1, Pallas kernels, inverse(): pl.pallas_call(inverse_kernel, out_shape=jax.ShapeDtypeStruct((n, n), f32...  4.31 us
    pallas_call x1, Pallas kernels, second_apply(): pl.pallas_call(second_kernel, out_shape=[jax.ShapeDtypeStruct((n, n), f32...  3.39 us
    pallas_call x2, Pallas kernels, own_terms(): pl.pallas_call(own_kernel, out_shape=jax.ShapeDtypeStruct((n, n), f32), i...  3.37 us
  transfers between devices with their start and end apart: 9, of which 2 were waited for; matrix products, arithmetic and copies ran while one was open for 0% of the time, Pallas kernels for 26%

profile of v2, /device:TPU:0, one launch (start us, length us, event | category | flops | bytes accessed | tf_op | source)
XLA Modules:
  0.0 84.9 jit_solution(8612365388749486056)
XLA Ops:
  0.6 1.0 %slice_bitcast_fusion.after = f32[256,256]{1,0:T(8,128)S(1)} fusion(f32[1,2,256,256]{3,2,1,0:T(8,128)} %site.3), kind=kLoop, calls=%fused_computation | loop fusion | bytes 524288 | tf_op jit(solution)/shard_map/squeeze | solution.py:391
  1.6 0.0 copy-start.1
  1.6 1.4 %pick.2 = f32[4,256,256]{2,1,0:T(8,128)S(1)} custom-call(f32[1,14,256,256]{3,2,1,0:T(8,128)} %right.7, f32[256,256]{1,0:T(8,128)S(1)} %slice_bitcast_fusion.after), custom_call_target="tpu_custom_call" | custom-call | tf_op jit(solution)/shard_map/pick/pallas_call | solution.py:77
  3.0 0.0 copy-start.2
  3.0 0.0 copy-start.3
  3.0 0.0 copy-start
  3.1 0.6 collective-permute-start.4
  3.6 1.4 %pick.3 = f32[4,256,256]{2,1,0:T(8,128)S(1)} custom-call(f32[1,14,256,256]{3,2,1,0:T(8,128)} %right.7, f32[256,256]{1,0:T(8,128)S(1)} %slice_bitcast_fusion.after), custom_call_target="tpu_custom_call" | custom-call | tf_op jit(solution)/shard_map/pick/pallas_call | solution.py:77
  5.0 0.7 collective-permute-start.5
  5.8 5.9 %collective-permute-start = (f32[256,256]{1,0:T(8,128)S(1)}, f32[256,256]{1,0:T(8,128)S(1)}, u32[]{:S(2)}, u32[]{:S(2)}) collective-permute-start(f32[256,256]{1,0:T(8,128)S(1)} %slice_bitcast_fusion.after), channel_id=1, source_target_pairs={{0,1},{1,2},{2,3},{3,4},{4,5},{5,6},{6,7},{7,8},{8,9},{9,10},{10,1... | collective-permute-start | bytes 786440 | tf_op jit(solution)/shard_map/ppermute | solution.py:380
  11.6 1.1 %collective-permute-done.lower = f32[256,256]{1,0:T(8,128)S(1)} collective-permute-done((f32[256,256]{1,0:T(8,128)S(1)}, f32[256,256]{1,0:T(8,128)S(1)}, u32[]{:S(2)}, u32[]{:S(2)}) %collective-permute-start) | collective-permute-done | bytes 262176 | tf_op jit(solution)/shard_map/ppermute | solution.py:380
  12.7 0.0 copy-done.2
  12.8 0.0 copy-done.3
  12.8 7.7 %factor.1 = (f32[256,256]{1,0:T(8,128)S(1)}, f32[256,256]{1,0:T(8,128)S(1)}, f32[384,128]{1,0:T(8,128)S(1)}) custom-call(s32[16]{0:T(128)S(1)} %copy-done.3, f32[1,2,256,256]{3,2,1,0:T(8,128)S(1)} %copy-done.2, f32[256,256]{1,0:T(8,128)S(1)} %collective-permute-done.lower), custom_call_target="tpu_custom_call" | custom-call | tf_op jit(solution)/shard_map/factor/pallas_call | solution.py:167
  20.5 22.8 %collective-permute-start.2 = (f32[384,128]{1,0:T(8,128)S(1)}, f32[384,128]{1,0:T(8,128)S(1)}, u32[]{:S(2)}, u32[]{:S(2)}) collective-permute-start(f32[384,128]{1,0:T(8,128)S(1)} %get-tuple-element.13), channel_id=1, source_target_pairs={{0,1},{2,3},{4,5},{6,7},{8,9},{10,11},{12,13},{14,15},{1,0},{3,2},... | collective-permute-start | bytes 589832 | tf_op jit(solution)/shard_map/ppermute | solution.py:386
  43.2 0.7 collective-permute-start.3
  43.9 0.0 copy-done.1
  43.9 0.0 copy-done
  43.9 1.7 %own.2.part = f32[256,256]{1,0:T(8,128)S(1)} custom-call(f32[256,256]{1,0:T(8,128)S(1)} %get-tuple-element.9.bond.field, f32[1,14,256,256]{3,2,1,0:T(8,128)S(1)} %copy-done, f32[1,14,256,256]{3,2,1,0:T(8,128)S(1)} %copy-done.1), custom_call_target="tpu_custom_call" | custom-call | tf_op jit(solution)/shard_map/own/pallas_call | solution.py:250
  45.6 0.0 collective-permute-done.2.near
  45.6 0.0 collective-permute-done.3.far
  45.6 0.0 collective-permute-done.4.right_near
  45.6 0.0 collective-permute-done.5.right_far
  45.6 2.7 %first.1.field.applied = f32[256,256]{1,0:T(8,128)S(1)} custom-call(s32[16]{0:T(128)S(1)} %copy-done.3, f32[384,128]{1,0:T(8,128)S(1)} %collective-permute-done.2.near, f32[384,128]{1,0:T(8,128)S(1)} %collective-permute-done.3.far, f32[1,14,256,256]{3,2,1,0:T(8,128)S(1)} %copy-done, f32[4,256,256]{2,1,0:T(8,128)S(1)} %collective-permute-done.4.right_near, ...), custom_call_target="tpu_custom_call" | custom-call | tf_op jit(solution)/shard_map/first/pallas_call | solution.py:291
  48.3 6.8 %collective-permute-start.6 = (f32[256,256]{1,0:T(8,128)S(1)}, f32[256,256]{1,0:T(8,128)S(1)}, u32[]{:S(2)}, u32[]{:S(2)}) collective-permute-start(f32[256,256]{1,0:T(8,128)S(1)} %first.1.field.applied), channel_id=1, source_target_pairs={{0,1},{2,3},{4,5},{6,7},{8,9},{10,11},{12,13},{14,15},{1,0},{3,2},... | collective-permute-start | bytes 786440 | tf_op jit(solution)/shard_map/ppermute | solution.py:386
  55.1 0.7 collective-permute-start.7
  55.8 4.3 %inverse.1.inv = f32[256,256]{1,0:T(8,128)S(1)} custom-call(f32[256,256]{1,0:T(8,128)S(1)} %get-tuple-element.9.bond.field, f32[256,256]{1,0:T(8,128)S(1)} %get-tuple-element.10.inv0), custom_call_target="tpu_custom_call" | custom-call | tf_op jit(solution)/shard_map/inverse/pallas_call | solution.py:203
  60.1 1.2 %ortho.1 = (f32[256,256]{1,0:T(8,128)S(1)}, f32[256,256]{1,0:T(8,128)S(1)}) custom-call(s32[16]{0:T(128)S(1)} %copy-done.3, f32[256,256]{1,0:T(8,128)S(1)} %inverse.1.inv, f32[1,2,256,256]{3,2,1,0:T(8,128)S(1)} %copy-done.2, f32[256,256]{1,0:T(8,128)S(1)} %collective-permute-done.lower), custom_call_target="tpu_custom_call" | custom-call | tf_op jit(solution)/shard_map/ortho/pallas_call | solution.py:225
  61.3 1.3 %collective-permute-start.1 = (f32[256,256]{1,0:T(8,128)S(1)}, f32[256,256]{1,0:T(8,128)S(1)}, u32[]{:S(2)}, u32[]{:S(2)}) collective-permute-start(f32[256,256]{1,0:T(8,128)S(1)} %get-tuple-element.12), channel_id=1, source_target_pairs={{1,0},{2,1},{3,2},{4,3},{5,4},{6,5},{7,6},{8,7},{9,8},{10,9},{11,1... | collective-permute-start | bytes 786440 | tf_op jit(solution)/shard_map/ppermute | solution.py:380
  62.6 1.7 %own.3.part = f32[256,256]{1,0:T(8,128)S(1)} custom-call(f32[256,256]{1,0:T(8,128)S(1)} %first.1.field.applied, f32[1,14,256,256]{3,2,1,0:T(8,128)S(1)} %copy-done, f32[1,14,256,256]{3,2,1,0:T(8,128)S(1)} %copy-done.1), custom_call_target="tpu_custom_call" | custom-call | tf_op jit(solution)/shard_map/own/pallas_call | solution.py:250
  64.3 0.0 collective-permute-done.6.near
  64.3 0.0 collective-permute-done.7.far
  64.3 3.4 %second.1 = (f32[256,256]{1,0:T(8,128)S(1)}, f32[16,8,128]{2,1,0:T(8,128)}) custom-call(s32[16]{0:T(128)S(1)} %copy-done.3, f32[256,256]{1,0:T(8,128)S(1)} %collective-permute-done.6.near, f32[256,256]{1,0:T(8,128)S(1)} %collective-permute-done.7.far, f32[1,14,256,256]{3,2,1,0:T(8,128)S(1)} %copy-done, f32[4,256,256]{2,1,0:T(8,128)S(1)} %collective-permute-done.4.right_near, ...), custom_call_target="tpu_custom_call" | custom-call | tf_op jit(solution)/shard_map/second/pallas_call | solution.py:318
  67.7 9.4 %all-to-all-start = ((f32[16,8,128]{2,1,0:T(8,128)}), f32[16,8,128]{2,1,0:T(8,128)S(1)}, u32[]{:S(2)}, u32[]{:S(2)}) async-start(f32[16,8,128]{2,1,0:T(8,128)} %get-tuple-element.14), calls=%async_computation | async-start | bytes 131072 | tf_op jit(solution)/shard_map/all_to_all | solution.py:409
  77.1 0.0 collective-permute-done.1.back
  77.1 0.8 stack.1
  77.9 6.1 %all-to-all-done.gathered = f32[16,8,128]{2,1,0:T(8,128)S(1)} async-done(((f32[16,8,128]{2,1,0:T(8,128)}), f32[16,8,128]{2,1,0:T(8,128)S(1)}, u32[]{:S(2)}, u32[]{:S(2)}) %all-to-all-start) | async-done | bytes 65568 | tf_op jit(solution)/shard_map/all_to_all | solution.py:409
  84.0 0.9 %final.1 = f32[1,256,256]{2,1,0:T(8,128)} custom-call(f32[16,8,128]{2,1,0:T(8,128)S(1)} %all-to-all-done.gathered, f32[256,256]{1,0:T(8,128)S(1)} %get-tuple-element.9.bond.field, f32[256,256]{1,0:T(8,128)S(1)} %first.1.field.applied, f32[256,256]{1,0:T(8,128)S(1)} %get-tuple-element.15.twice), custom_call_target="tpu_custom_call" | custom-call | tf_op jit(solution)/shard_map/final/pallas_call | solution.py:367
Async XLA Ops:
  1.6 42.3 %copy-start.1 = (f32[1,14,256,256]{3,2,1,0:T(8,128)S(1)}, f32[1,14,256,256]{3,2,1,0:T(8,128)}, u32[]{:S(2)}) copy-start(f32[1,14,256,256]{3,2,1,0:T(8,128)} %right.7) | copy-start | bytes 11010052
  3.0 9.7 %copy-start.2 = (f32[1,2,256,256]{3,2,1,0:T(8,128)S(1)}, f32[1,2,256,256]{3,2,1,0:T(8,128)}, u32[]{:S(2)}) copy-start(f32[1,2,256,256]{3,2,1,0:T(8,128)} %site.3) | copy-start | bytes 1572868
  3.0 9.7 %copy-start.3 = (s32[16]{0:T(128)S(1)}, s32[16]{0:T(128)}, u32[]{:S(2)}) copy-start(s32[16]{0:T(128)} %sizes.7) | copy-start | bytes 196
  3.0 40.9 %copy-start = (f32[1,14,256,256]{3,2,1,0:T(8,128)S(1)}, f32[1,14,256,256]{3,2,1,0:T(8,128)}, u32[]{:S(2)}) copy-start(f32[1,14,256,256]{3,2,1,0:T(8,128)} %left.7) | copy-start | bytes 11010052
  3.1 42.6 %collective-permute-start.4 = (f32[4,256,256]{2,1,0:T(8,128)S(1)}, f32[4,256,256]{2,1,0:T(8,128)S(1)}, u32[]{:S(2)}, u32[]{:S(2)}) collective-permute-start(f32[4,256,256]{2,1,0:T(8,128)S(1)} %pick.2), channel_id=1, source_target_pairs={{0,1},{2,3},{4,5},{6,7},{8,9},{10,11},{12,13},{14,15},{1,0},{3,2},... | collective-permute-start | bytes 3145736 | tf_op jit(solution)/shard_map/ppermute | solution.py:386
  5.0 40.6 %collective-permute-start.5 = (f32[4,256,256]{2,1,0:T(8,128)S(1)}, f32[4,256,256]{2,1,0:T(8,128)S(1)}, u32[]{:S(2)}, u32[]{:S(2)}) collective-permute-start(f32[4,256,256]{2,1,0:T(8,128)S(1)} %pick.3), channel_id=1, source_target_pairs={{1,2},{3,4},{5,6},{7,8},{9,10},{11,12},{13,14},{2,1},{4,3},{6,5},{... | collective-permute-start | bytes 3145736 | tf_op jit(solution)/shard_map/ppermute | solution.py:386
  5.8 7.0 %collective-permute-start = (f32[256,256]{1,0:T(8,128)S(1)}, f32[256,256]{1,0:T(8,128)S(1)}, u32[]{:S(2)}, u32[]{:S(2)}) collective-permute-start(f32[256,256]{1,0:T(8,128)S(1)} %slice_bitcast_fusion.after), channel_id=1, source_target_pairs={{0,1},{1,2},{2,3},{3,4},{4,5},{5,6},{6,7},{7,8},{8,9},{9,10},{10,1... | collective-permute-start | bytes 786440 | tf_op jit(solution)/shard_map/ppermute | solution.py:380
  20.5 25.2 %collective-permute-start.2 = (f32[384,128]{1,0:T(8,128)S(1)}, f32[384,128]{1,0:T(8,128)S(1)}, u32[]{:S(2)}, u32[]{:S(2)}) collective-permute-start(f32[384,128]{1,0:T(8,128)S(1)} %get-tuple-element.13), channel_id=1, source_target_pairs={{0,1},{2,3},{4,5},{6,7},{8,9},{10,11},{12,13},{14,15},{1,0},{3,2},... | collective-permute-start | bytes 589832 | tf_op jit(solution)/shard_map/ppermute | solution.py:386
  43.2 2.4 %collective-permute-start.3 = (f32[384,128]{1,0:T(8,128)S(1)}, f32[384,128]{1,0:T(8,128)S(1)}, u32[]{:S(2)}, u32[]{:S(2)}) collective-permute-start(f32[384,128]{1,0:T(8,128)S(1)} %get-tuple-element.13), channel_id=1, source_target_pairs={{1,2},{3,4},{5,6},{7,8},{9,10},{11,12},{13,14},{2,1},{4,3},{6,5},{... | collective-permute-start | bytes 589832 | tf_op jit(solution)/shard_map/ppermute | solution.py:386
  48.3 15.9 %collective-permute-start.6 = (f32[256,256]{1,0:T(8,128)S(1)}, f32[256,256]{1,0:T(8,128)S(1)}, u32[]{:S(2)}, u32[]{:S(2)}) collective-permute-start(f32[256,256]{1,0:T(8,128)S(1)} %first.1.field.applied), channel_id=1, source_target_pairs={{0,1},{2,3},{4,5},{6,7},{8,9},{10,11},{12,13},{14,15},{1,0},{3,2},... | collective-permute-start | bytes 786440 | tf_op jit(solution)/shard_map/ppermute | solution.py:386
  55.1 9.2 %collective-permute-start.7 = (f32[256,256]{1,0:T(8,128)S(1)}, f32[256,256]{1,0:T(8,128)S(1)}, u32[]{:S(2)}, u32[]{:S(2)}) collective-permute-start(f32[256,256]{1,0:T(8,128)S(1)} %first.1.field.applied), channel_id=1, source_target_pairs={{1,2},{3,4},{5,6},{7,8},{9,10},{11,12},{13,14},{2,1},{4,3},{6,5},{... | collective-permute-start | bytes 786440 | tf_op jit(solution)/shard_map/ppermute | solution.py:386
  61.3 15.8 %collective-permute-start.1 = (f32[256,256]{1,0:T(8,128)S(1)}, f32[256,256]{1,0:T(8,128)S(1)}, u32[]{:S(2)}, u32[]{:S(2)}) collective-permute-start(f32[256,256]{1,0:T(8,128)S(1)} %get-tuple-element.12), channel_id=1, source_target_pairs={{1,0},{2,1},{3,2},{4,3},{5,4},{6,5},{7,6},{8,7},{9,8},{10,9},{11,1... | collective-permute-start | bytes 786440 | tf_op jit(solution)/shard_map/ppermute | solution.py:380
  67.7 16.3 %all-to-all-start = ((f32[16,8,128]{2,1,0:T(8,128)}), f32[16,8,128]{2,1,0:T(8,128)S(1)}, u32[]{:S(2)}, u32[]{:S(2)}) async-start(f32[16,8,128]{2,1,0:T(8,128)} %get-tuple-element.14), calls=%async_computation | async-start | bytes 131072 | tf_op jit(solution)/shard_map/all_to_all | solution.py:409

commit v3 on v2

--- a/solution.py
+++ b/solution.py
@@ -1,5 +1,3 @@
-import functools
-
 import jax
 import jax.numpy as jnp
 from jax import lax
@@ -64,28 +62,62 @@
     return q, sizes[q], sizes[jnp.maximum(q - 1, 0)]
 
 
-def pick_kernel(right, after, out, sem, *, far):
+def far_kind(q):
+    return lax.rem((q + 1) // 2, 2)
+
+
+def take_far_kernel(site, right, source, early, middle, late, sems):
+    q = lax.axis_index("row")
+    half = W_UP // 2
+    first = (1 - lax.rem(q, 2)) * W_DN
+    turn = jnp.where(far_kind(q) == 0, first + half, first)
+    copies = [pltpu.make_async_copy(site.at[0, 1], source, sems.at[0])]
+    for i, (start, out) in enumerate(((first, early), (turn, middle), (first + half, late))):
+        copies.append(pltpu.make_async_copy(right.at[0, pl.ds(start, half)], out, sems.at[i + 1]))
+    for copy in copies:
+        copy.start()
+    for copy in copies:
+        copy.wait()
+
+
+def in_hbm(x):
+    return pltpu.with_memory_space_constraint(x, pltpu.HBM)
+
+
+def take_far(site, right):
+    n = right.shape[-1]
+    return pl.pallas_call(
+        take_far_kernel,
+        out_shape=[jax.ShapeDtypeStruct((n, n), f32)] + [jax.ShapeDtypeStruct((W_UP // 2, n, n), f32)] * 3,
+        in_specs=[HB] * 2,
+        out_specs=[ANY] * 4,
+        scratch_shapes=[pltpu.SemaphoreType.DMA((4,))],
+        compiler_params=params(4),
+        name="take_far",
+    )(in_hbm(site), in_hbm(right))
+
+
+def take_near_kernel(right, near, sem):
     odd = lax.rem(lax.axis_index("row"), 2)
-    first = (1 - odd if far else odd) * W_DN
-    copy = pltpu.make_async_copy(right.at[0, pl.ds(first, W_UP)], out, sem.at[0])
+    copy = pltpu.make_async_copy(right.at[0, pl.ds(odd * W_DN, W_DN)], near, sem.at[0])
     copy.start()
     copy.wait()
 
 
-def pick(right, after, far):
+def take_near(right):
     n = right.shape[-1]
     return pl.pallas_call(
-        functools.partial(pick_kernel, far=far),
-        out_shape=jax.ShapeDtypeStruct((W_UP, n, n), f32),
-        in_specs=[HB, ANY],
+        take_near_kernel,
+        out_shape=jax.ShapeDtypeStruct((W_DN, n, n), f32),
+        in_specs=[HB],
         out_specs=ANY,
         scratch_shapes=[pltpu.SemaphoreType.DMA((1,))],
         compiler_params=params(4),
-        name="pick",
-    )(pltpu.with_memory_space_constraint(right, pltpu.HBM), after)
-
-
-def factor_kernel(sizes, site, lower, bond, inv0, packed, work, turn, rows, erows, lstack, rstack):
+        name="take_near",
+    )(in_hbm(right))
+
+
+def factor_kernel(sizes, site, lower, bond, packed, inv0, work, turn, rows, erows, lstack, rstack):
     n = lower.shape[-1]
     _, own, prev = own_sizes(sizes)
     row_id, col_id = places(n)
@@ -154,10 +186,16 @@
         return carry
 
     lax.fori_loop(0, n // PANEL, body, 0)
+    rid, cid = places(LANES)
+    lower_part = rid > cid
     at = 0
     for i in range(tiles):
         for j in range(i, tiles):
-            packed[pl.ds(at, LANES), :] = bond[pl.ds(i * LANES, LANES), pl.ds(j * LANES, LANES)]
+            where = (pl.ds(i * LANES, LANES), pl.ds(j * LANES, LANES))
+            tile = bond[where]
+            if i == j:
+                tile = jnp.where(lower_part, inv0[where], tile)
+            packed[pl.ds(at, LANES), :] = tile
             at += LANES
 
 
@@ -166,11 +204,14 @@
     tiles = n // LANES
     return pl.pallas_call(
         factor_kernel,
-        out_shape=[jax.ShapeDtypeStruct((n, n), f32)] * 2
-        + [jax.ShapeDtypeStruct((tiles * (tiles + 1) // 2 * LANES, LANES), f32)],
+        out_shape=[
+            jax.ShapeDtypeStruct((n, n), f32),
+            jax.ShapeDtypeStruct((tiles * (tiles + 1) // 2 * LANES, LANES), f32),
+        ],
         in_specs=[SM, VM, VM],
-        out_specs=[VM] * 3,
+        out_specs=[VM] * 2,
         scratch_shapes=[
+            pltpu.VMEM((n, n), f32),
             pltpu.VMEM((n + PANEL, n), f32),
             pltpu.VMEM((LANES, PANEL), f32),
             pltpu.VMEM((PANEL, n), f32),
@@ -183,110 +224,170 @@
     )(sizes, site, lower)
 
 
-def inverse_kernel(bond, inv0, out):
-    n = bond.shape[-1]
+def unpacked(message, n):
+    tiles, at, rows = n // LANES, 0, []
+    for i in range(tiles):
+        row = [jnp.zeros((LANES, LANES), f32)] * i
+        for _ in range(i, tiles):
+            row.append(message[at : at + LANES, :])
+            at += LANES
+        rows.append(jnp.concatenate(row, 1))
+    both = jnp.concatenate(rows, 0)
     rid, cid = places(n)
-    low_tri = bond[...].T
-    x = inv0[...]
-    size = PANEL
-    while size < n:
+    return jnp.where(cid >= rid, both, 0.0), jnp.where(cid < rid, both, 0.0)
+
+
+def block_inverse(message, n):
+    bond, x = unpacked(message, n)
+    rid, cid = places(n)
+    diagonal = rid == cid
+    return jnp.where(diagonal, 1.0 / jnp.where(diagonal & (bond != 0.0), bond, 1.0), x)
+
+
+def grown_inverse(message, x, size, stop):
+    n = x.shape[-1]
+    rid, cid = places(n)
+    low_tri = unpacked(message, n)[0].T
+    while size < stop:
         off = (rid // (2 * size) == cid // (2 * size)) & (rid // size > cid // size)
         part = split3(jnp.where(off, low_tri, 0.0))
         xs = split3(x)
         x = x - dot6(xs, split3(dot6(part, xs)))
         size *= 2
-    out[...] = x
-
-
-def inverse(bond, inv0):
-    n = bond.shape[-1]
-    return pl.pallas_call(
-        inverse_kernel,
+    return x
+
+
+def upper_rows_kernel(sizes, packed, site, out):
+    n = out.shape[-1]
+    _, own, _ = own_sizes(sizes)
+    x = split3(grown_inverse(packed[...], block_inverse(packed[...], n), PANEL, n))
+    rid, cid = places(n)
+    out[...] = dot6(split3(jnp.where((cid < own) & (rid < own), site[0, 0], 0.0)), x, 1)
+
+
+def upper_rows(sizes, packed, site):
+    n = site.shape[-1]
+    return pl.pallas_call(
+        upper_rows_kernel,
+        out_shape=jax.ShapeDtypeStruct((n, n), f32),
+        in_specs=[SM, VM, VM],
+        out_specs=VM,
+        compiler_params=params(16),
+        name="upper_rows",
+    )(sizes, packed, site)
+
+
+SPLIT_AT = 4 * PANEL
+
+
+def next_message(near, far):
+    odd = lax.rem(lax.axis_index("row"), 2) == 1
+    return jnp.where(jnp.broadcast_to(odd, near.shape), far[...], near[...])
+
+
+def next_inverse_kernel(near, far, out):
+    message = next_message(near, far)
+    n = out.shape[-1]
+    out[...] = grown_inverse(message, block_inverse(message, n), PANEL, SPLIT_AT)
+
+
+def next_inverse(near, far, n):
+    return pl.pallas_call(
+        next_inverse_kernel,
         out_shape=jax.ShapeDtypeStruct((n, n), f32),
         in_specs=[VM] * 2,
         out_specs=VM,
         compiler_params=params(16),
-        name="inverse",
-    )(bond, inv0)
-
-
-def ortho_kernel(sizes, inv, site, lower, top_out, low_out):
-    n = inv.shape[-1]
-    _, own, prev = own_sizes(sizes)
+        name="next_inverse",
+    )(near, far)
+
+
+def lower_rows_kernel(sizes, near, far, inv, site, top, out, low, sems):
+    n = low.shape[-1]
+    top_copy = pltpu.make_async_copy(top, out.at[0, 0], sems.at[0])
+    top_copy.start()
+    q, own, _ = own_sizes(sizes)
+    count = lax.axis_size("row")
+    after = sizes[jnp.minimum(q + 1, count - 1)]
+    after = jnp.where(q + 1 < count, after, 0)
+    x = split3(grown_inverse(next_message(near, far), inv[...], SPLIT_AT, n))
     rid, cid = places(n)
-    xs = split3(inv[...])
-    live_col = cid < own
-    low_out[...] = dot6(split3(jnp.where(live_col & (rid < prev), lower[...], 0.0)), xs, 1)
-    top_out[...] = dot6(split3(jnp.where(live_col & (rid < own), site[0, 0], 0.0)), xs, 1)
-
-
-def ortho(sizes, inv, site, lower):
-    n = inv.shape[-1]
-    return pl.pallas_call(
-        ortho_kernel,
-        out_shape=[jax.ShapeDtypeStruct((n, n), f32)] * 2,
-        in_specs=[SM] + [VM] * 3,
-        out_specs=[VM] * 2,
+    low[...] = dot6(split3(jnp.where((cid < after) & (rid < own), site[0, 1], 0.0)), x, 1)
+    low_copy = pltpu.make_async_copy(low, out.at[0, 1], sems.at[1])
+    low_copy.start()
+    top_copy.wait()
+    low_copy.wait()
+
+
+def lower_rows(sizes, near, far, inv, site, top):
+    n = site.shape[-1]
+    return pl.pallas_call(
+        lower_rows_kernel,
+        out_shape=jax.ShapeDtypeStruct((1, 2, n, n), f32),
+        in_specs=[SM] + [VM] * 4 + [ANY],
+        out_specs=ANY,
+        scratch_shapes=[pltpu.VMEM((n, n), f32), pltpu.SemaphoreType.DMA((2,))],
         compiler_params=params(16),
-        name="ortho",
-    )(sizes, inv, site, lower)
+        name="lower_rows",
+    )(sizes, near, far, inv, site, top)
 
 
 def channel(left, a, field, right):
     return dot3(split2(left[0, a]), split2(dot3(field, split2(right))))
 
 
-def own_kernel(field, left, right, out):
+def field_of(ref, n):
+    return ref[...] if ref.shape[-1] == n else unpacked(ref[...], n)[0]
+
+
+def moved_terms(field, left, right, base, total):
+    f = split2(field)
+    for a in range(right.shape[0]):
+        total = total + channel(left, base + a, f, right[a])
+    return total
+
+
+def local_kernel(field, near, left, right, right_near, out):
+    n = out.shape[-1]
     f = split2(field[...])
-    total = None
+    total = jnp.zeros((n, n), f32)
     for a in range(W_DN + W_UP, left.shape[1]):
-        term = channel(left, a, f, right[0, a])
-        total = term if total is None else total + term
-    out[...] = total
-
-
-def own_terms(field, left, right):
+        total = total + channel(left, a, f, right[0, a])
+    odd = lax.rem(lax.axis_index("row"), 2)
+    out[...] = moved_terms(field_of(near, n), left, right_near, (1 - odd) * W_DN, total)
+
+
+def local_terms(field, near, left, right, right_near):
     n = field.shape[-1]
     return pl.pallas_call(
-        own_kernel,
+        local_kernel,
         out_shape=jax.ShapeDtypeStruct((n, n), f32),
-        in_specs=[VM] * 3,
+        in_specs=[VM] * 5,
         out_specs=VM,
         compiler_params=params(16),
-        name="own",
-    )(field, left, right)
-
-
-def unpacked(ref, n):
-    if ref.shape[-1] == n:
-        return ref[...]
-    tiles, at, rows = n // LANES, 0, []
-    for i in range(tiles):
-        row = [jnp.zeros((LANES, LANES), f32)] * i
-        for _ in range(i, tiles):
-            row.append(ref[pl.ds(at, LANES), :])
-            at += LANES
-        rows.append(jnp.concatenate(row, 1))
-    return jnp.concatenate(rows, 0)
-
-
-def moved_total(near, far, left, right_near, right_far, part, own):
-    odd = lax.rem(lax.axis_index("row"), 2)
+        name="local_terms",
+    )(field, near, left, right, right_near)
+
+
+def with_far(sizes, far, left, early, middle, late, part):
+    n = part.shape[-1]
+    q, own, _ = own_sizes(sizes)
+    kind = jnp.broadcast_to(far_kind(q) == 0, (n, n))
+    half = early.shape[0]
     total = part[...]
-    for field, right, base in ((near, right_near, (1 - odd) * W_DN), (far, right_far, odd * W_DN)):
-        f = split2(unpacked(field, part.shape[-1]))
-        for a in range(right.shape[0]):
-            total = total + channel(left, base + a, f, right[a])
-    rid, cid = places(part.shape[-1])
+    f = split2(field_of(far, n))
+    for a in range(2 * half):
+        pair = (early[a], middle[a]) if a < half else (middle[a - half], late[a - half])
+        total = total + channel(left, lax.rem(q, 2) * W_DN + a, f, jnp.where(kind, *pair))
+    rid, cid = places(n)
     return jnp.where((rid < own) & (cid < own), total, 0.0)
 
 
-def first_kernel(sizes, near, far, left, right_near, right_far, part, out):
-    _, own, _ = own_sizes(sizes)
-    out[...] = moved_total(near, far, left, right_near, right_far, part, own)
-
-
-def first_apply(sizes, near, far, left, right_near, right_far, part):
+def first_kernel(sizes, far, left, early, middle, late, part, out):
+    out[...] = with_far(sizes, far, left, early, middle, late, part)
+
+
+def first_apply(sizes, far, left, right_far, part):
     n = part.shape[-1]
     return pl.pallas_call(
         first_kernel,
@@ -295,12 +396,11 @@
         out_specs=VM,
         compiler_params=params(16),
         name="first",
-    )(sizes, near, far, left, right_near, right_far, part)
-
-
-def second_kernel(sizes, near, far, left, right_near, right_far, part, bond, applied, out, spread):
-    _, own, _ = own_sizes(sizes)
-    twice = moved_total(near, far, left, right_near, right_far, part, own)
+    )(sizes, far, left, *right_far, part)
+
+
+def second_kernel(sizes, far, left, early, middle, late, part, bond, applied, out, spread):
+    twice = with_far(sizes, far, left, early, middle, late, part)
     out[...] = twice
     basis = (bond[...], time_step * applied[...], (0.5 * time_step * time_step) * twice)
     sums = []
@@ -313,7 +413,7 @@
         spread[i] = block
 
 
-def second_apply(sizes, near, far, left, right_near, right_far, part, bond, applied, count):
+def second_apply(sizes, far, left, right_far, part, bond, applied, count):
     n = part.shape[-1]
     return pl.pallas_call(
         second_kernel,
@@ -325,29 +425,7 @@
         out_specs=[VM, VM],
         compiler_params=params(16),
         name="second",
-    )(sizes, near, far, left, right_near, right_far, part, bond, applied)
-
-
-def stack_kernel(top, back, out, sems):
-    top_copy = pltpu.make_async_copy(top, out.at[0, 0], sems.at[0])
-    back_copy = pltpu.make_async_copy(back, out.at[0, 1], sems.at[1])
-    top_copy.start()
-    back_copy.start()
-    top_copy.wait()
-    back_copy.wait()
-
-
-def stack(top, back):
-    n = top.shape[-1]
-    return pl.pallas_call(
-        stack_kernel,
-        out_shape=jax.ShapeDtypeStruct((1, 2, n, n), f32),
-        in_specs=[ANY] * 2,
-        out_specs=ANY,
-        scratch_shapes=[pltpu.SemaphoreType.DMA((2,))],
-        compiler_params=params(4),
-        name="stack",
-    )(top, back)
+    )(sizes, far, left, *right_far, part, bond, applied)
 
 
 def final_kernel(gathered, bond, applied, twice, out):
@@ -380,34 +458,35 @@
     return lax.ppermute(value, "row", [(source, source + steps) for source in range(first, last)])
 
 
-def swapped(value, first):
+def swapped(value, first, step=2):
     count = lax.axis_size("row")
-    pairs = [(i, i + 1) for i in range(first, count - 1, 2)]
+    pairs = [(i, i + 1) for i in range(first, count - 1, step)]
     return lax.ppermute(value, "row", pairs + [(j, i) for i, j in pairs])
 
 
 def bond_update(site, left, right, sizes):
     count = lax.axis_size("row")
-    source = site[0, 1]
+    source, early, middle, late = take_far(site, right)
+    early = swapped(early, 3, 4)
     lower = shifted_by(source, 1)
-    to_far = pick(right, source, True)
-    right_far = swapped(to_far, 1)
-    to_near = pick(right, source, False)
+    middle = swapped(middle, 1)
+    late = swapped(late, 1, 4)
+    right_far = (early, middle, late)
+    to_near = take_near(right)
     right_near = swapped(to_near, 0)
-    bond, inv0, packed = factor(sizes, site, lower)
-    far = swapped(packed, 1)
-    near = swapped(packed, 0)
-    part = own_terms(bond, left, right)
-    inv = inverse(bond, inv0)
-    applied = first_apply(sizes, near, far, left, right_near, right_far, part)
+    bond, packed = factor(sizes, site, lower)
+    bond_far = swapped(packed, 1)
+    bond_near = swapped(packed, 0)
+    top = upper_rows(sizes, packed, site)
+    part = local_terms(bond, bond_near, left, right, right_near)
+    applied = first_apply(sizes, bond_far, left, right_far, part)
     far = swapped(applied, 1)
     near = swapped(applied, 0)
-    part = own_terms(applied, left, right)
-    top, low = ortho(sizes, inv, site, lower)
-    back = shifted_by(low, -1)
-    twice, spread = second_apply(sizes, near, far, left, right_near, right_far, part, bond, applied, count)
+    inv = next_inverse(bond_near, bond_far, bond.shape[-1])
+    part = local_terms(applied, near, left, right, right_near)
+    twice, spread = second_apply(sizes, far, left, right_far, part, bond, applied, count)
     gathered = lax.all_to_all(spread, "row", 0, 0, tiled=True)
-    left_out = stack(top, back)
+    left_out = lower_rows(sizes, bond_near, bond_far, inv, site, top)
     bond_out = final(gathered, bond, applied, twice)
     return left_out, bond_out
 

time: 85.2 us -> 72.7 us (0.85)
  starting transfers between devices: 48.7 us -> 37.3 us
  waiting for transfers between devices: 7.22 us -> 1.58 us
  Pallas kernels: 27.1 us -> 32.7 us
  local copies, waits for them, and re-layouts: 1 us -> 0.02 us
    ppermute x6 -> x8, starting transfers between devices: 32.1 us -> 23 us  [swapped(): return lax.ppermute(value, 'row', pairs + [(j, i) for i, j in pairs])]
    pallas_call x7, Pallas kernels: 12.5 us -> 19.6 us  [the longest x1 5.23 us: upper_rows(): pl.pallas_call(upper_rows_kernel, out_shape=jax.ShapeDtypeStruct((n, n),...]
    all_to_all x1, waiting for transfers between devices: 6.07 us -> 0.01 us  [bond_update(): gathered = lax.all_to_all(spread, 'row', 0, 0, tiled=True)]
    ppermute x2 -> x1, starting transfers between devices: 7.14 us -> 1.74 us  [shifted_by(): lax.ppermute(value, 'row', [(source, source + steps) for source in range(...]
    all_to_all x1, starting transfers between devices: 9.4 us -> 12.6 us  [bond_update(): gathered = lax.all_to_all(spread, 'row', 0, 0, tiled=True)]
    ppermute x6 -> x8, waiting for transfers between devices: 0.02 us -> 1.58 us  [swapped(): return lax.ppermute(value, 'row', pairs + [(j, i) for i, j in pairs])]
    ppermute x2 -> x1, waiting for transfers between devices: 1.13 us -> 0.01 us  [shifted_by(): lax.ppermute(value, 'row', [(source, source + steps) for source in range(...]
    squeeze x1 -> x0, local copies, waits for them, and re-layouts: 0.97 us -> none  [bond_update(): source = site[0, 1]]
  transfers between devices with their start and end apart: 9 -> 10, of which waited for: 2 -> 2; matrix products, arithmetic and copies ran while one was open for 0% -> 0% of each run, Pallas kernels for 26% -> 36%
where the time goes in v3:
time: 72.7 us; the launch traced here: 72.5 us
  starting transfers between devices  37.3 us (51%)
  Pallas kernels  32.7 us (45%)
  waiting for transfers between devices  1.58 us (2%)
  between operations  0.88 us (1%)
    ppermute x8, starting transfers between devices, swapped(): return lax.ppermute(value, 'row', pairs + [(j, i) for i, j in pairs])  23 us
    all_to_all x1, starting transfers between devices, bond_update(): gathered = lax.all_to_all(spread, 'row', 0, 0, tiled=True)  12.6 us
    pallas_call x1, Pallas kernels, factor(): pl.pallas_call(factor_kernel, out_shape=[jax.ShapeDtypeStruct((n, n), f32...  7.69 us
    pallas_call x1, Pallas kernels, upper_rows(): pl.pallas_call(upper_rows_kernel, out_shape=jax.ShapeDtypeStruct((n, n),...  5.23 us
    pallas_call x2, Pallas kernels, local_terms(): pl.pallas_call(local_kernel, out_shape=jax.ShapeDtypeStruct((n, n), f32),...  5.06 us
    pallas_call x1, Pallas kernels, lower_rows(): pl.pallas_call(lower_rows_kernel, out_shape=jax.ShapeDtypeStruct((1, 2, n...  3.84 us
    pallas_call x1, Pallas kernels, second_apply(): pl.pallas_call(second_kernel, out_shape=[jax.ShapeDtypeStruct((n, n), f32...  2.56 us
    pallas_call x1, Pallas kernels, next_inverse(): pl.pallas_call(next_inverse_kernel, out_shape=jax.ShapeDtypeStruct((n, n)...  2.24 us
  transfers between devices with their start and end apart: 10, of which 2 were waited for; matrix products, arithmetic and copies ran while one was open for 0% of the time, Pallas kernels for 36%

profile of v3, /device:TPU:0, one launch (start us, length us, event | category | flops | bytes accessed | tf_op | source)
XLA Modules:
  0.0 72.5 jit_solution(338036589896762864)
XLA Ops:
  0.6 0.0 copy-start.2
  0.6 0.0 copy-start.3
  0.7 0.0 copy-start.1
  0.7 1.4 %take_near.1 = f32[4,256,256]{2,1,0:T(8,128)S(1)} custom-call(f32[1,14,256,256]{3,2,1,0:T(8,128)} %right.7), custom_call_target="tpu_custom_call" | custom-call | tf_op jit(solution)/shard_map/take_near/pallas_call | solution.py:109
  2.1 0.0 copy-start
  2.1 0.6 collective-permute-start.6
  2.6 1.9 %take_far.1 = (f32[256,256]{1,0:T(8,128)S(1)}, f32[2,256,256]{2,1,0:T(8,128)S(1)}, f32[2,256,256]{2,1,0:T(8,128)S(1)}, f32[2,256,256]{2,1,0:T(8,128)S(1)}) custom-call(f32[1,2,256,256]{3,2,1,0:T(8,128)} %site.7, f32[1,14,256,256]{3,2,1,0:T(8,128)} %right.7), custom_call_target="tpu_custom_call" | custom-call | tf_op jit(solution)/shard_map/take_far/pallas_call | solution.py:89
  4.5 1.7 %collective-permute-start = (f32[256,256]{1,0:T(8,128)S(1)}, f32[256,256]{1,0:T(8,128)S(1)}, u32[]{:S(2)}, u32[]{:S(2)}) collective-permute-start(f32[256,256]{1,0:T(8,128)S(1)} %get-tuple-element.10), channel_id=1, source_target_pairs={{0,1},{1,2},{2,3},{3,4},{4,5},{5,6},{6,7},{7,8},{8,9},{9,10},{10,1... | collective-permute-start | bytes 786440 | tf_op jit(solution)/shard_map/ppermute | solution.py:458
  6.3 0.7 collective-permute-start.3
  7.0 0.7 collective-permute-start.4
  7.7 0.7 collective-permute-start.5
  8.4 0.0 collective-permute-done.lower
  8.4 0.0 copy-done.2
  8.4 0.0 copy-done.3
  8.4 7.7 %factor.1 = (f32[256,256]{1,0:T(8,128)S(1)}, f32[384,128]{1,0:T(8,128)S(1)}) custom-call(s32[16]{0:T(128)S(1)} %copy-done.3, f32[1,2,256,256]{3,2,1,0:T(8,128)S(1)} %copy-done.2, f32[256,256]{1,0:T(8,128)S(1)} %collective-permute-done.lower), custom_call_target="tpu_custom_call" | custom-call | tf_op jit(solution)/shard_map/factor/pallas_call | solution.py:205
  16.1 6.8 %collective-permute-start.1 = (f32[384,128]{1,0:T(8,128)S(1)}, f32[384,128]{1,0:T(8,128)S(1)}, u32[]{:S(2)}, u32[]{:S(2)}) collective-permute-start(f32[384,128]{1,0:T(8,128)S(1)} %get-tuple-element.11.packed), channel_id=1, source_target_pairs={{0,1},{2,3},{4,5},{6,7},{8,9},{10,11},{12,13},{14,15},{1,0},{3,2},... | collective-permute-start | bytes 589832 | tf_op jit(solution)/shard_map/ppermute | solution.py:464
  22.9 1.1 %collective-permute-done.1.near = f32[384,128]{1,0:T(8,128)S(1)} collective-permute-done((f32[384,128]{1,0:T(8,128)S(1)}, f32[384,128]{1,0:T(8,128)S(1)}, u32[]{:S(2)}, u32[]{:S(2)}) %collective-permute-start.1) | collective-permute-done | bytes 196640 | tf_op jit(solution)/shard_map/ppermute | solution.py:464
  24.0 0.7 collective-permute-start.2
  24.7 0.0 collective-permute-done.6.right_near
  24.7 0.0 copy-done.1
  24.7 0.0 copy-done
  24.7 2.5 %local_terms.2.part = f32[256,256]{1,0:T(8,128)S(1)} custom-call(f32[256,256]{1,0:T(8,128)S(1)} %get-tuple-element.15.field.bond, f32[384,128]{1,0:T(8,128)S(1)} %collective-permute-done.1.near, f32[1,14,256,256]{3,2,1,0:T(8,128)S(1)} %copy-done.1, f32[1,14,256,256]{3,2,1,0:T(8,128)S(1)} %copy-done, f32[4,256,256]{2,1,0:T(8,128)S(1)} %collective-permute-done.6.right_near), custom_call_target="tpu_custom_call" | custom-call | tf_op jit(solution)/shard_map/local_terms/pallas_call | solution.py:362
  27.2 0.0 collective-permute-done.2.far
  27.3 0.0 collective-permute-done.3.early
  27.3 0.0 collective-permute-done.4.middle
  27.3 0.0 collective-permute-done.5.late
  27.3 1.9 %first.1.field.applied = f32[256,256]{1,0:T(8,128)S(1)} custom-call(s32[16]{0:T(128)S(1)} %copy-done.3, f32[384,128]{1,0:T(8,128)S(1)} %collective-permute-done.2.far, f32[1,14,256,256]{3,2,1,0:T(8,128)S(1)} %copy-done.1, f32[2,256,256]{2,1,0:T(8,128)S(1)} %collective-permute-done.3.early, f32[2,256,256]{2,1,0:T(8,128)S(1)} %collective-permute-done.4.middle, ...), custom_call_target="tpu_custom_call" | custom-call | tf_op jit(solution)/shard_map/first/pallas_call | solution.py:392
  29.2 12.2 %collective-permute-start.8 = (f32[256,256]{1,0:T(8,128)S(1)}, f32[256,256]{1,0:T(8,128)S(1)}, u32[]{:S(2)}, u32[]{:S(2)}) collective-permute-start(f32[256,256]{1,0:T(8,128)S(1)} %first.1.field.applied), channel_id=1, source_target_pairs={{0,1},{2,3},{4,5},{6,7},{8,9},{10,11},{12,13},{14,15},{1,0},{3,2},... | collective-permute-start | bytes 786440 | tf_op jit(solution)/shard_map/ppermute | solution.py:464
  41.4 0.7 collective-permute-start.7
  42.0 0.5 collective-permute-done.8.near
  42.5 2.5 %local_terms.3.part = f32[256,256]{1,0:T(8,128)S(1)} custom-call(f32[256,256]{1,0:T(8,128)S(1)} %first.1.field.applied, f32[256,256]{1,0:T(8,128)S(1)} %collective-permute-done.8.near, f32[1,14,256,256]{3,2,1,0:T(8,128)S(1)} %copy-done.1, f32[1,14,256,256]{3,2,1,0:T(8,128)S(1)} %copy-done, f32[4,256,256]{2,1,0:T(8,128)S(1)} %collective-permute-done.6.right_near), custom_call_target="tpu_custom_call" | custom-call | tf_op jit(solution)/shard_map/local_terms/pallas_call | solution.py:362
  45.1 0.0 collective-permute-done.7.far
  45.1 2.6 %second.1 = (f32[256,256]{1,0:T(8,128)S(1)}, f32[16,8,128]{2,1,0:T(8,128)}) custom-call(s32[16]{0:T(128)S(1)} %copy-done.3, f32[256,256]{1,0:T(8,128)S(1)} %collective-permute-done.7.far, f32[1,14,256,256]{3,2,1,0:T(8,128)S(1)} %copy-done.1, f32[2,256,256]{2,1,0:T(8,128)S(1)} %collective-permute-done.3.early, ...), custom_call_target="tpu_custom_call" | custom-call | tf_op jit(solution)/shard_map/second/pallas_call | solution.py:418
  47.6 12.6 %all-to-all-start = ((f32[16,8,128]{2,1,0:T(8,128)}), f32[16,8,128]{2,1,0:T(8,128)S(1)}, u32[]{:S(2)}, u32[]{:S(2)}) async-start(f32[16,8,128]{2,1,0:T(8,128)} %get-tuple-element.16), calls=%async_computation | async-start | bytes 131072 | tf_op jit(solution)/shard_map/all_to_all | solution.py:488
  60.2 5.2 %upper_rows.1.top = f32[256,256]{1,0:T(8,128)S(1)} custom-call(s32[16]{0:T(128)S(1)} %copy-done.3, f32[384,128]{1,0:T(8,128)S(1)} %get-tuple-element.11.packed, f32[1,2,256,256]{3,2,1,0:T(8,128)S(1)} %copy-done.2), custom_call_target="tpu_custom_call" | custom-call | tf_op jit(solution)/shard_map/upper_rows/pallas_call | solution.py:270
  65.5 2.2 %next_inverse.1.inv = f32[256,256]{1,0:T(8,128)S(1)} custom-call(f32[384,128]{1,0:T(8,128)S(1)} %collective-permute-done.1.near, f32[384,128]{1,0:T(8,128)S(1)} %collective-permute-done.2.far), custom_call_target="tpu_custom_call" | custom-call | tf_op jit(solution)/shard_map/next_inverse/pallas_call | solution.py:295
  67.7 3.8 %lower_rows.1 = f32[1,2,256,256]{3,2,1,0:T(8,128)} custom-call(s32[16]{0:T(128)S(1)} %copy-done.3, f32[384,128]{1,0:T(8,128)S(1)} %collective-permute-done.1.near, f32[384,128]{1,0:T(8,128)S(1)} %collective-permute-done.2.far, f32[256,256]{1,0:T(8,128)S(1)} %next_inverse.1.inv, f32[1,2,256,256]{3,2,1,0:T(8,128)S(1)} %copy-done.2, f32[256,256]{1,0:T(8,128)S(1)} %upper_rows.1.top), custom_call_target="tpu_custom_call" | custom-call | tf_op jit(solution)/shard_map/lower_rows/pallas_call | solution.py:324
  71.5 0.0 all-to-all-done.gathered
  71.6 0.9 %final.1 = f32[1,256,256]{2,1,0:T(8,128)} custom-call(f32[16,8,128]{2,1,0:T(8,128)S(1)} %all-to-all-done.gathered, f32[256,256]{1,0:T(8,128)S(1)} %get-tuple-element.15.field.bond, f32[256,256]{1,0:T(8,128)S(1)} %first.1.field.applied, f32[256,256]{1,0:T(8,128)S(1)} %get-tuple-element.17.twice), custom_call_target="tpu_custom_call" | custom-call | tf_op jit(solution)/shard_map/final/pallas_call | solution.py:445
Async XLA Ops:
  0.6 7.7 %copy-start.2 = (f32[1,2,256,256]{3,2,1,0:T(8,128)S(1)}, f32[1,2,256,256]{3,2,1,0:T(8,128)}, u32[]{:S(2)}) copy-start(f32[1,2,256,256]{3,2,1,0:T(8,128)} %site.7) | copy-start | bytes 1572868
  0.6 7.7 %copy-start.3 = (s32[16]{0:T(128)S(1)}, s32[16]{0:T(128)}, u32[]{:S(2)}) copy-start(s32[16]{0:T(128)} %sizes.9) | copy-start | bytes 196
  0.7 24.0 %copy-start.1 = (f32[1,14,256,256]{3,2,1,0:T(8,128)S(1)}, f32[1,14,256,256]{3,2,1,0:T(8,128)}, u32[]{:S(2)}) copy-start(f32[1,14,256,256]{3,2,1,0:T(8,128)} %left.7) | copy-start | bytes 11010052
  2.1 22.6 %copy-start = (f32[1,14,256,256]{3,2,1,0:T(8,128)S(1)}, f32[1,14,256,256]{3,2,1,0:T(8,128)}, u32[]{:S(2)}) copy-start(f32[1,14,256,256]{3,2,1,0:T(8,128)} %right.7) | copy-start | bytes 11010052
  2.1 22.6 %collective-permute-start.6 = (f32[4,256,256]{2,1,0:T(8,128)S(1)}, f32[4,256,256]{2,1,0:T(8,128)S(1)}, u32[]{:S(2)}, u32[]{:S(2)}) collective-permute-start(f32[4,256,256]{2,1,0:T(8,128)S(1)} %take_near.1), channel_id=1, source_target_pairs={{0,1},{2,3},{4,5},{6,7},{8,9},{10,11},{12,13},{14,15},{1,0},{3,2},... | collective-permute-start | bytes 3145736 | tf_op jit(solution)/shard_map/ppermute | solution.py:464
  4.5 3.9 %collective-permute-start = (f32[256,256]{1,0:T(8,128)S(1)}, f32[256,256]{1,0:T(8,128)S(1)}, u32[]{:S(2)}, u32[]{:S(2)}) collective-permute-start(f32[256,256]{1,0:T(8,128)S(1)} %get-tuple-element.10), channel_id=1, source_target_pairs={{0,1},{1,2},{2,3},{3,4},{4,5},{5,6},{6,7},{7,8},{8,9},{9,10},{10,1... | collective-permute-start | bytes 786440 | tf_op jit(solution)/shard_map/ppermute | solution.py:458
  6.3 21.0 %collective-permute-start.3 = (f32[2,256,256]{2,1,0:T(8,128)S(1)}, f32[2,256,256]{2,1,0:T(8,128)S(1)}, u32[]{:S(2)}, u32[]{:S(2)}) collective-permute-start(f32[2,256,256]{2,1,0:T(8,128)S(1)} %get-tuple-element.12), channel_id=1, source_target_pairs={{3,4},{7,8},{11,12},{4,3},{8,7},{12,11},{19,20},{23,24},{27,28},{2... | collective-permute-start | bytes 1572872 | tf_op jit(solution)/shard_map/ppermute | solution.py:464
  7.0 20.3 %collective-permute-start.4 = (f32[2,256,256]{2,1,0:T(8,128)S(1)}, f32[2,256,256]{2,1,0:T(8,128)S(1)}, u32[]{:S(2)}, u32[]{:S(2)}) collective-permute-start(f32[2,256,256]{2,1,0:T(8,128)S(1)} %get-tuple-element.13), channel_id=1, source_target_pairs={{1,2},{3,4},{5,6},{7,8},{9,10},{11,12},{13,14},{2,1},{4,3},{6,5},{... | collective-permute-start | bytes 1572872 | tf_op jit(solution)/shard_map/ppermute | solution.py:464
  7.7 19.6 %collective-permute-start.5 = (f32[2,256,256]{2,1,0:T(8,128)S(1)}, f32[2,256,256]{2,1,0:T(8,128)S(1)}, u32[]{:S(2)}, u32[]{:S(2)}) collective-permute-start(f32[2,256,256]{2,1,0:T(8,128)S(1)} %get-tuple-element.14), channel_id=1, source_target_pairs={{1,2},{5,6},{9,10},{13,14},{2,1},{6,5},{10,9},{14,13},{17,18},{21,... | collective-permute-start | bytes 1572872 | tf_op jit(solution)/shard_map/ppermute | solution.py:464
  16.1 7.9 %collective-permute-start.1 = (f32[384,128]{1,0:T(8,128)S(1)}, f32[384,128]{1,0:T(8,128)S(1)}, u32[]{:S(2)}, u32[]{:S(2)}) collective-permute-start(f32[384,128]{1,0:T(8,128)S(1)} %get-tuple-element.11.packed), channel_id=1, source_target_pairs={{0,1},{2,3},{4,5},{6,7},{8,9},{10,11},{12,13},{14,15},{1,0},{3,2},... | collective-permute-start | bytes 589832 | tf_op jit(solution)/shard_map/ppermute | solution.py:464
  24.0 3.2 %collective-permute-start.2 = (f32[384,128]{1,0:T(8,128)S(1)}, f32[384,128]{1,0:T(8,128)S(1)}, u32[]{:S(2)}, u32[]{:S(2)}) collective-permute-start(f32[384,128]{1,0:T(8,128)S(1)} %get-tuple-element.11.packed), channel_id=1, source_target_pairs={{1,2},{3,4},{5,6},{7,8},{9,10},{11,12},{13,14},{2,1},{4,3},{6,5},{... | collective-permute-start | bytes 589832 | tf_op jit(solution)/shard_map/ppermute | solution.py:464
  29.2 13.3 %collective-permute-start.8 = (f32[256,256]{1,0:T(8,128)S(1)}, f32[256,256]{1,0:T(8,128)S(1)}, u32[]{:S(2)}, u32[]{:S(2)}) collective-permute-start(f32[256,256]{1,0:T(8,128)S(1)} %first.1.field.applied), channel_id=1, source_target_pairs={{0,1},{2,3},{4,5},{6,7},{8,9},{10,11},{12,13},{14,15},{1,0},{3,2},... | collective-permute-start | bytes 786440 | tf_op jit(solution)/shard_map/ppermute | solution.py:464
  41.4 3.7 %collective-permute-start.7 = (f32[256,256]{1,0:T(8,128)S(1)}, f32[256,256]{1,0:T(8,128)S(1)}, u32[]{:S(2)}, u32[]{:S(2)}) collective-permute-start(f32[256,256]{1,0:T(8,128)S(1)} %first.1.field.applied), channel_id=1, source_target_pairs={{1,2},{3,4},{5,6},{7,8},{9,10},{11,12},{13,14},{2,1},{4,3},{6,5},{... | collective-permute-start | bytes 786440 | tf_op jit(solution)/shard_map/ppermute | solution.py:464
  47.6 23.9 %all-to-all-start = ((f32[16,8,128]{2,1,0:T(8,128)}), f32[16,8,128]{2,1,0:T(8,128)S(1)}, u32[]{:S(2)}, u32[]{:S(2)}) async-start(f32[16,8,128]{2,1,0:T(8,128)} %get-tuple-element.16), calls=%async_computation | async-start | bytes 131072 | tf_op jit(solution)/shard_map/all_to_all | solution.py:488

commit v4 on v3

--- a/solution.py
+++ b/solution.py
@@ -66,64 +66,80 @@
     return lax.rem((q + 1) // 2, 2)
 
 
-def take_far_kernel(site, right, source, early, middle, late, sems):
-    q = lax.axis_index("row")
-    half = W_UP // 2
-    first = (1 - lax.rem(q, 2)) * W_DN
-    turn = jnp.where(far_kind(q) == 0, first + half, first)
-    copies = [pltpu.make_async_copy(site.at[0, 1], source, sems.at[0])]
-    for i, (start, out) in enumerate(((first, early), (turn, middle), (first + half, late))):
-        copies.append(pltpu.make_async_copy(right.at[0, pl.ds(start, half)], out, sems.at[i + 1]))
+def first_far(q):
+    return (1 - lax.rem(q, 2)) * W_DN
+
+
+def run_copies(copies):
     for copy in copies:
         copy.start()
     for copy in copies:
         copy.wait()
 
 
+def take_early_kernel(site, right, source, early, sems):
+    half = early.shape[0]
+    start = first_far(lax.axis_index("row"))
+    run_copies(
+        (
+            pltpu.make_async_copy(site.at[0, 1], source, sems.at[0]),
+            pltpu.make_async_copy(right.at[0, pl.ds(start, half)], early, sems.at[1]),
+        )
+    )
+
+
+def take_rest_kernel(right, middle, late, near, sems):
+    q = lax.axis_index("row")
+    half = late.shape[0]
+    start = first_far(q)
+    turn = jnp.where(far_kind(q) == 0, start + half, start)
+    run_copies(
+        (
+            pltpu.make_async_copy(right.at[0, pl.ds(turn, half)], middle, sems.at[0]),
+            pltpu.make_async_copy(right.at[0, pl.ds(start + half, half)], late, sems.at[1]),
+            pltpu.make_async_copy(right.at[0, pl.ds(lax.rem(q, 2) * W_DN, W_DN)], near, sems.at[2]),
+        )
+    )
+
+
 def in_hbm(x):
     return pltpu.with_memory_space_constraint(x, pltpu.HBM)
 
 
-def take_far(site, right):
+def take_early(site, right):
     n = right.shape[-1]
     return pl.pallas_call(
-        take_far_kernel,
-        out_shape=[jax.ShapeDtypeStruct((n, n), f32)] + [jax.ShapeDtypeStruct((W_UP // 2, n, n), f32)] * 3,
+        take_early_kernel,
+        out_shape=[jax.ShapeDtypeStruct((n, n), f32), jax.ShapeDtypeStruct((W_UP // 2, n, n), f32)],
         in_specs=[HB] * 2,
-        out_specs=[ANY] * 4,
-        scratch_shapes=[pltpu.SemaphoreType.DMA((4,))],
+        out_specs=[ANY] * 2,
+        scratch_shapes=[pltpu.SemaphoreType.DMA((2,))],
         compiler_params=params(4),
-        name="take_far",
+        name="take_early",
     )(in_hbm(site), in_hbm(right))
 
 
-def take_near_kernel(right, near, sem):
-    odd = lax.rem(lax.axis_index("row"), 2)
-    copy = pltpu.make_async_copy(right.at[0, pl.ds(odd * W_DN, W_DN)], near, sem.at[0])
-    copy.start()
-    copy.wait()
-
-
-def take_near(right):
+def take_rest(right):
     n = right.shape[-1]
     return pl.pallas_call(
-        take_near_kernel,
-        out_shape=jax.ShapeDtypeStruct((W_DN, n, n), f32),
+        take_rest_kernel,
+        out_shape=[jax.ShapeDtypeStruct((W_UP // 2, n, n), f32)] * 2 + [jax.ShapeDtypeStruct((W_DN, n, n), f32)],
         in_specs=[HB],
-        out_specs=ANY,
-        scratch_shapes=[pltpu.SemaphoreType.DMA((1,))],
+        out_specs=[ANY] * 3,
+        scratch_shapes=[pltpu.SemaphoreType.DMA((3,))],
         compiler_params=params(4),
-        name="take_near",
+        name="take_rest",
     )(in_hbm(right))
 
 
-def factor_kernel(sizes, site, lower, bond, packed, inv0, work, turn, rows, erows, lstack, rstack):
+def factor_kernel(sizes, site, lower, bond, packed, mask, inv0, work, turn, rows, erows, lstack, rstack):
     n = lower.shape[-1]
     _, own, prev = own_sizes(sizes)
     row_id, col_id = places(n)
     live_col = col_id < own
     top = jnp.where(live_col & (row_id < own), site[0, 0], 0.0)
     bot = jnp.where(live_col & (row_id < prev), lower[...], 0.0)
+    mask[...] = jnp.where(live_col & (row_id < own), 1.0, 0.0)
     gram = jnp.where((row_id == col_id) & (row_id >= own), 1.0, 0.0)
     for part in (top, bot):
         gram = gram + dot6(split3(part.T), split3(part))
@@ -187,16 +203,45 @@
 
     lax.fori_loop(0, n // PANEL, body, 0)
     rid, cid = places(LANES)
-    lower_part = rid > cid
+    diagonal = []
+    for i in range(tiles):
+        where = (pl.ds(i * LANES, LANES), pl.ds(i * LANES, LANES))
+        diagonal.append(jnp.where(rid > cid, inv0[where], bond[where]))
     at = 0
+    for part in fold(diagonal):
+        packed[pl.ds(at, part.shape[0]), :] = part
+        at += part.shape[0]
     for i in range(tiles):
-        for j in range(i, tiles):
-            where = (pl.ds(i * LANES, LANES), pl.ds(j * LANES, LANES))
-            tile = bond[where]
-            if i == j:
-                tile = jnp.where(lower_part, inv0[where], tile)
-            packed[pl.ds(at, LANES), :] = tile
+        for j in range(i + 1, tiles):
+            packed[pl.ds(at, LANES), :] = bond[pl.ds(i * LANES, LANES), pl.ds(j * LANES, LANES)]
             at += LANES
+
+
+def fold(diagonal):
+    half = LANES // 2
+    low = lax.broadcasted_iota(jnp.int32, (half, LANES), 1) < half
+    parts = []
+    for i in range(0, len(diagonal) - 1, 2):
+        first, second = diagonal[i], diagonal[i + 1]
+        parts.append(first[:half])
+        parts.append(jnp.where(low, pltpu.roll(second[:half], half, 1), first[half:]))
+        parts.append(jnp.where(low, second[:half], second[half:]))
+    return parts + diagonal[len(diagonal) - len(diagonal) % 2 :]
+
+
+def unfold(message, tiles):
+    half = LANES // 2
+    low = lax.broadcasted_iota(jnp.int32, (half, LANES), 1) < half
+    diagonal, at = [], 0
+    for _ in range(0, tiles - 1, 2):
+        a, b, c = (message[at + i * half : at + (i + 1) * half, :] for i in range(3))
+        diagonal.append(jnp.concatenate([a, jnp.where(low, 0.0, b)], 0))
+        diagonal.append(jnp.concatenate([jnp.where(low, c, pltpu.roll(b, half, 1)), jnp.where(low, 0.0, c)], 0))
+        at += 3 * half
+    if tiles % 2:
+        diagonal.append(message[at : at + LANES, :])
+        at += LANES
+    return diagonal, at
 
 
 def factor(sizes, site, lower):
@@ -206,10 +251,11 @@
         factor_kernel,
         out_shape=[
             jax.ShapeDtypeStruct((n, n), f32),
-            jax.ShapeDtypeStruct((tiles * (tiles + 1) // 2 * LANES, LANES), f32),
+            jax.ShapeDtypeStruct((tiles * (tiles + 1) // 2 * LANES - tiles // 2 * (LANES // 2), LANES), f32),
+            jax.ShapeDtypeStruct((n, n), f32),
         ],
         in_specs=[SM, VM, VM],
-        out_specs=[VM] * 2,
+        out_specs=[VM] * 3,
         scratch_shapes=[
             pltpu.VMEM((n, n), f32),
             pltpu.VMEM((n + PANEL, n), f32),
@@ -225,10 +271,12 @@
 
 
 def unpacked(message, n):
-    tiles, at, rows = n // LANES, 0, []
+    tiles = n // LANES
+    diagonal, at = unfold(message, tiles)
+    rows = []
     for i in range(tiles):
-        row = [jnp.zeros((LANES, LANES), f32)] * i
-        for _ in range(i, tiles):
+        row = [jnp.zeros((LANES, LANES), f32)] * i + [diagonal[i]]
+        for _ in range(i + 1, tiles):
             row.append(message[at : at + LANES, :])
             at += LANES
         rows.append(jnp.concatenate(row, 1))
@@ -285,21 +333,24 @@
     return jnp.where(jnp.broadcast_to(odd, near.shape), far[...], near[...])
 
 
-def next_inverse_kernel(near, far, out):
+def next_inverse_kernel(near, far, bond, applied, out, known):
+    b, a = bond[...], time_step * applied[...]
+    known[...] = lane_sums(((b, b), (b, a), (a, a)), 0)
     message = next_message(near, far)
     n = out.shape[-1]
     out[...] = grown_inverse(message, block_inverse(message, n), PANEL, SPLIT_AT)
 
 
-def next_inverse(near, far, n):
+def next_inverse(near, far, bond, applied):
+    n = bond.shape[-1]
     return pl.pallas_call(
         next_inverse_kernel,
-        out_shape=jax.ShapeDtypeStruct((n, n), f32),
-        in_specs=[VM] * 2,
-        out_specs=VM,
+        out_shape=[jax.ShapeDtypeStruct((n, n), f32), jax.ShapeDtypeStruct((1, LANES), f32)],
+        in_specs=[VM] * 4,
+        out_specs=[VM] * 2,
         compiler_params=params(16),
         name="next_inverse",
-    )(near, far)
+    )(near, far, bond, applied)
 
 
 def lower_rows_kernel(sizes, near, far, inv, site, top, out, low, sems):
@@ -369,9 +420,9 @@
     )(field, near, left, right, right_near)
 
 
-def with_far(sizes, far, left, early, middle, late, part):
+def with_far(mask, far, left, early, middle, late, part):
     n = part.shape[-1]
-    q, own, _ = own_sizes(sizes)
+    q = lax.axis_index("row")
     kind = jnp.broadcast_to(far_kind(q) == 0, (n, n))
     half = early.shape[0]
     total = part[...]
@@ -379,58 +430,62 @@
     for a in range(2 * half):
         pair = (early[a], middle[a]) if a < half else (middle[a - half], late[a - half])
         total = total + channel(left, lax.rem(q, 2) * W_DN + a, f, jnp.where(kind, *pair))
-    rid, cid = places(n)
-    return jnp.where((rid < own) & (cid < own), total, 0.0)
-
-
-def first_kernel(sizes, far, left, early, middle, late, part, out):
-    out[...] = with_far(sizes, far, left, early, middle, late, part)
-
-
-def first_apply(sizes, far, left, right_far, part):
+    return jnp.where(mask[...] > 0.0, total, 0.0)
+
+
+def first_kernel(mask, far, left, early, middle, late, part, out):
+    out[...] = with_far(mask, far, left, early, middle, late, part)
+
+
+def first_apply(mask, far, left, right_far, part):
     n = part.shape[-1]
     return pl.pallas_call(
         first_kernel,
         out_shape=jax.ShapeDtypeStruct((n, n), f32),
-        in_specs=[SM] + [VM] * 6,
+        in_specs=[VM] * 7,
         out_specs=VM,
         compiler_params=params(16),
         name="first",
-    )(sizes, far, left, *right_far, part)
-
-
-def second_kernel(sizes, far, left, early, middle, late, part, bond, applied, out, spread):
-    twice = with_far(sizes, far, left, early, middle, late, part)
+    )(mask, far, left, *right_far, part)
+
+
+def lane_sums(pairs, first):
+    lane = lax.broadcasted_iota(jnp.int32, (1, LANES), 1)
+    row = jnp.zeros((1, LANES), f32)
+    for i, (x, y) in enumerate(pairs):
+        line = jnp.sum(jnp.sum(x * y, 0, keepdims=True), 1, keepdims=True)
+        row = row + jnp.where(lane == first + i, line, 0.0)
+    return row
+
+
+def second_kernel(mask, far, left, early, middle, late, part, bond, applied, known, out, spread):
+    twice = with_far(mask, far, left, early, middle, late, part)
     out[...] = twice
-    basis = (bond[...], time_step * applied[...], (0.5 * time_step * time_step) * twice)
-    sums = []
-    for i in range(3):
-        for j in range(i, 3):
-            line = jnp.sum(basis[i] * basis[j], 0, keepdims=True)
-            sums.append(sum(line[:, t : t + LANES] for t in range(0, line.shape[1], LANES)))
-    block = jnp.concatenate(sums + [jnp.zeros((2, LANES), f32)], 0)
+    b, a = bond[...], time_step * applied[...]
+    t = (0.5 * time_step * time_step) * twice
+    row = known[...] + lane_sums(((b, t), (a, t), (t, t)), 3)
     for i in range(spread.shape[0]):
-        spread[i] = block
-
-
-def second_apply(sizes, far, left, right_far, part, bond, applied, count):
+        spread[i] = row
+
+
+def second_apply(mask, far, left, right_far, part, bond, applied, known, count):
     n = part.shape[-1]
     return pl.pallas_call(
         second_kernel,
         out_shape=[
             jax.ShapeDtypeStruct((n, n), f32),
-            jax.ShapeDtypeStruct((count, 8, LANES), f32),
+            pltpu.VMEM((count, 1, LANES), f32),
         ],
-        in_specs=[SM] + [VM] * 8,
+        in_specs=[VM] * 10,
         out_specs=[VM, VM],
         compiler_params=params(16),
         name="second",
-    )(sizes, far, left, *right_far, part, bond, applied)
+    )(mask, far, left, *right_far, part, bond, applied, known)
 
 
 def final_kernel(gathered, bond, applied, twice, out):
-    sums = jnp.sum(jnp.sum(gathered[...], 0), 1, keepdims=True)
-    bb, ba, bt, aa, at, tt = (jnp.broadcast_to(sums[i : i + 1, :], (1, bond.shape[-1])) for i in range(6))
+    sums = jnp.sum(gathered[...], 0)
+    bb, ba, aa, bt, at, tt = (jnp.broadcast_to(sums[:, i : i + 1], (1, bond.shape[-1])) for i in range(6))
     rate = ba / bb
     c0 = 1.0 - rate + 0.5 * rate * rate
     c1 = 1.0 - rate
@@ -466,25 +521,25 @@
 
 def bond_update(site, left, right, sizes):
     count = lax.axis_size("row")
-    source, early, middle, late = take_far(site, right)
+    source, early = take_early(site, right)
     early = swapped(early, 3, 4)
     lower = shifted_by(source, 1)
+    middle, late, to_near = take_rest(right)
     middle = swapped(middle, 1)
     late = swapped(late, 1, 4)
     right_far = (early, middle, late)
-    to_near = take_near(right)
     right_near = swapped(to_near, 0)
-    bond, packed = factor(sizes, site, lower)
+    bond, packed, mask = factor(sizes, site, lower)
     bond_far = swapped(packed, 1)
     bond_near = swapped(packed, 0)
     top = upper_rows(sizes, packed, site)
     part = local_terms(bond, bond_near, left, right, right_near)
-    applied = first_apply(sizes, bond_far, left, right_far, part)
+    applied = first_apply(mask, bond_far, left, right_far, part)
     far = swapped(applied, 1)
     near = swapped(applied, 0)
-    inv = next_inverse(bond_near, bond_far, bond.shape[-1])
+    inv, known = next_inverse(bond_near, bond_far, bond, applied)
     part = local_terms(applied, near, left, right, right_near)
-    twice, spread = second_apply(sizes, far, left, right_far, part, bond, applied, count)
+    twice, spread = second_apply(mask, far, left, right_far, part, bond, applied, known, count)
     gathered = lax.all_to_all(spread, "row", 0, 0, tiled=True)
     left_out = lower_rows(sizes, bond_near, bond_far, inv, site, top)
     bond_out = final(gathered, bond, applied, twice)

time: 72.7 us -> 69.1 us (0.950)
  starting transfers between devices: 37.3 us -> 35 us
  Pallas kernels: 32.7 us -> 31.9 us
    all_to_all x1, starting transfers between devices: 12.6 us -> 11.2 us  [bond_update(): gathered = lax.all_to_all(spread, 'row', 0, 0, tiled=True)]
    ppermute x8, starting transfers between devices: 23 us -> 21.7 us  [swapped(): return lax.ppermute(value, 'row', pairs + [(j, i) for i, j in pairs])]
  transfers between devices with their start and end apart: 10 -> 10, of which waited for: 2 -> 1; matrix products, arithmetic and copies ran while one was open for 0% -> 0% of each run, Pallas kernels for 36% -> 38%
where the time goes in v4:
time: 69.1 us; the launch traced here: 68.9 us
  starting transfers between devices  35 us (51%)
  Pallas kernels  31.9 us (46%)
  waiting for transfers between devices  1.05 us (2%)
  between operations  0.88 us (1%)
    ppermute x8, starting transfers between devices, swapped(): return lax.ppermute(value, 'row', pairs + [(j, i) for i, j in pairs])  21.7 us
    all_to_all x1, starting transfers between devices, bond_update(): gathered = lax.all_to_all(spread, 'row', 0, 0, tiled=True)  11.2 us
    pallas_call x1, Pallas kernels, factor(): pl.pallas_call(factor_kernel, out_shape=[jax.ShapeDtypeStruct((n, n), f32...  7.79 us
    pallas_call x1, Pallas kernels, upper_rows(): pl.pallas_call(upper_rows_kernel, out_shape=jax.ShapeDtypeStruct((n, n),...  5.25 us
    pallas_call x2, Pallas kernels, local_terms(): pl.pallas_call(local_kernel, out_shape=jax.ShapeDtypeStruct((n, n), f32),...  5 us
    pallas_call x1, Pallas kernels, lower_rows(): pl.pallas_call(lower_rows_kernel, out_shape=jax.ShapeDtypeStruct((1, 2, n...  3.88 us
    pallas_call x1, Pallas kernels, next_inverse(): pl.pallas_call(next_inverse_kernel, out_shape=[jax.ShapeDtypeStruct((n, n...  2.26 us
    ppermute x1, starting transfers between devices, shifted_by(): lax.ppermute(value, 'row', [(source, source + steps) for source in range(...  2.1 us
  transfers between devices with their start and end apart: 10, of which 1 were waited for; matrix products, arithmetic and copies ran while one was open for 0% of the time, Pallas kernels for 38%

profile of v4, /device:TPU:0, one launch (start us, length us, event | category | flops | bytes accessed | tf_op | source)
XLA Modules:
  0.0 68.9 jit_solution(1614493387097318479)
XLA Ops:
  0.6 0.0 copy-start
  0.6 0.0 copy-start.2
  0.7 0.0 copy-start.3
  0.7 0.0 copy-start.1
  0.7 1.7 %take_rest.1 = (f32[2,256,256]{2,1,0:T(8,128)S(1)}, f32[2,256,256]{2,1,0:T(8,128)S(1)}, f32[4,256,256]{2,1,0:T(8,128)S(1)}) custom-call(f32[1,14,256,256]{3,2,1,0:T(8,128)} %right.7), custom_call_target="tpu_custom_call" | custom-call | tf_op jit(solution)/shard_map/take_rest/pallas_call | solution.py:124
  2.4 0.6 collective-permute-start.6
  3.0 1.7 %take_early.1 = (f32[256,256]{1,0:T(8,128)S(1)}, f32[2,256,256]{2,1,0:T(8,128)S(1)}) custom-call(f32[1,2,256,256]{3,2,1,0:T(8,128)} %site.7, f32[1,14,256,256]{3,2,1,0:T(8,128)} %right.7), custom_call_target="tpu_custom_call" | custom-call | tf_op jit(solution)/shard_map/take_early/pallas_call | solution.py:111
  4.7 2.1 %collective-permute-start = (f32[256,256]{1,0:T(8,128)S(1)}, f32[256,256]{1,0:T(8,128)S(1)}, u32[]{:S(2)}, u32[]{:S(2)}) collective-permute-start(f32[256,256]{1,0:T(8,128)S(1)} %get-tuple-element.14), channel_id=1, source_target_pairs={{0,1},{1,2},{2,3},{3,4},{4,5},{5,6},{6,7},{7,8},{8,9},{9,10},{10,1... | collective-permute-start | bytes 786440 | tf_op jit(solution)/shard_map/ppermute | solution.py:513
  6.8 0.7 %collective-permute-start.4 = (f32[2,256,256]{2,1,0:T(8,128)S(1)}, f32[2,256,256]{2,1,0:T(8,128)S(1)}, u32[]{:S(2)}, u32[]{:S(2)}) collective-permute-start(f32[2,256,256]{2,1,0:T(8,128)S(1)} %get-tuple-element.19), channel_id=1, source_target_pairs={{1,2},{3,4},{5,6},{7,8},{9,10},{11,12},{13,14},{2,1},{4,3},{6,5},{... | collective-permute-start | bytes 1572872 | tf_op jit(solution)/shard_map/ppermute | solution.py:519
  7.5 0.7 %collective-permute-start.5 = (f32[2,256,256]{2,1,0:T(8,128)S(1)}, f32[2,256,256]{2,1,0:T(8,128)S(1)}, u32[]{:S(2)}, u32[]{:S(2)}) collective-permute-start(f32[2,256,256]{2,1,0:T(8,128)S(1)} %get-tuple-element.20), channel_id=1, source_target_pairs={{1,2},{5,6},{9,10},{13,14},{2,1},{6,5},{10,9},{14,13},{17,18},{21,... | collective-permute-start | bytes 1572872 | tf_op jit(solution)/shard_map/ppermute | solution.py:519
  8.2 0.7 %collective-permute-start.3 = (f32[2,256,256]{2,1,0:T(8,128)S(1)}, f32[2,256,256]{2,1,0:T(8,128)S(1)}, u32[]{:S(2)}, u32[]{:S(2)}) collective-permute-start(f32[2,256,256]{2,1,0:T(8,128)S(1)} %get-tuple-element.18), channel_id=1, source_target_pairs={{3,4},{7,8},{11,12},{4,3},{8,7},{12,11},{19,20},{23,24},{27,28},{2... | collective-permute-start | bytes 1572872 | tf_op jit(solution)/shard_map/ppermute | solution.py:519
  8.9 0.0 collective-permute-done.lower
  9.0 0.0 copy-done.2
  9.0 0.0 copy-done.3
  9.0 7.8 %factor.1 = (f32[256,256]{1,0:T(8,128)S(1)}, f32[320,128]{1,0:T(8,128)S(1)}, f32[256,256]{1,0:T(8,128)S(1)}) custom-call(s32[16]{0:T(128)S(1)} %copy-done.3, f32[1,2,256,256]{3,2,1,0:T(8,128)S(1)} %copy-done.2, f32[256,256]{1,0:T(8,128)S(1)} %collective-permute-done.lower), custom_call_target="tpu_custom_call" | custom-call | tf_op jit(solution)/shard_map/factor/pallas_call | solution.py:250
  16.8 6.8 %collective-permute-start.1 = (f32[320,128]{1,0:T(8,128)S(1)}, f32[320,128]{1,0:T(8,128)S(1)}, u32[]{:S(2)}, u32[]{:S(2)}) collective-permute-start(f32[320,128]{1,0:T(8,128)S(1)} %get-tuple-element.15.packed), channel_id=1, source_target_pairs={{0,1},{2,3},{4,5},{6,7},{8,9},{10,11},{12,13},{14,15},{1,0},{3,2},... | collective-permute-start | bytes 491528 | tf_op jit(solution)/shard_map/ppermute | solution.py:519
  23.6 1.0 %collective-permute-done.1.near = f32[320,128]{1,0:T(8,128)S(1)} collective-permute-done((f32[320,128]{1,0:T(8,128)S(1)}, f32[320,128]{1,0:T(8,128)S(1)}, u32[]{:S(2)}, u32[]{:S(2)}) %collective-permute-start.1) | collective-permute-done | bytes 163872 | tf_op jit(solution)/shard_map/ppermute | solution.py:519
  24.6 0.7 collective-permute-start.2
  25.3 0.0 collective-permute-done.6.right_near
  25.3 0.0 copy-done
  25.3 0.0 copy-done.1
  25.3 2.5 %local_terms.2.part = f32[256,256]{1,0:T(8,128)S(1)} custom-call(f32[256,256]{1,0:T(8,128)S(1)} %get-tuple-element.16.field.bond, f32[320,128]{1,0:T(8,128)S(1)} %collective-permute-done.1.near, f32[1,14,256,256]{3,2,1,0:T(8,128)S(1)} %copy-done.1, f32[1,14,256,256]{3,2,1,0:T(8,128)S(1)} %copy-done, f32[4,256,256]{2,1,0:T(8,128)S(1)} %collective-permute-done.6.right_near), custom_call_target="tpu_custom_call" | custom-call | tf_op jit(solution)/shard_map/local_terms/pallas_call | solution.py:413
  27.8 0.0 collective-permute-done.2.far
  27.8 0.0 collective-permute-done.4.middle
  27.9 0.0 collective-permute-done.5.late
  27.9 0.0 collective-permute-done.3.early
  27.9 1.3 %first.1.applied.field = f32[256,256]{1,0:T(8,128)S(1)} custom-call(f32[256,256]{1,0:T(8,128)S(1)} %get-tuple-element.17.mask, f32[320,128]{1,0:T(8,128)S(1)} %collective-permute-done.2.far, f32[1,14,256,256]{3,2,1,0:T(8,128)S(1)} %copy-done.1, f32[2,256,256]{2,1,0:T(8,128)S(1)} %collective-permute-done.3.early, ...), custom_call_target="tpu_custom_call" | custom-call | tf_op jit(solution)/shard_map/first/pallas_call | solution.py:442
  29.2 10.9 %collective-permute-start.8 = (f32[256,256]{1,0:T(8,128)S(1)}, f32[256,256]{1,0:T(8,128)S(1)}, u32[]{:S(2)}, u32[]{:S(2)}) collective-permute-start(f32[256,256]{1,0:T(8,128)S(1)} %first.1.applied.field), channel_id=1, source_target_pairs={{0,1},{2,3},{4,5},{6,7},{8,9},{10,11},{12,13},{14,15},{1,0},{3,2},... | collective-permute-start | bytes 786440 | tf_op jit(solution)/shard_map/ppermute | solution.py:519
  40.1 0.7 collective-permute-start.7
  40.8 2.3 %next_inverse.1 = (f32[256,256]{1,0:T(8,128)S(1)}, f32[1,128]{1,0:T(1,128)S(1)}) custom-call(f32[320,128]{1,0:T(8,128)S(1)} %collective-permute-done.1.near, f32[320,128]{1,0:T(8,128)S(1)} %collective-permute-done.2.far, f32[256,256]{1,0:T(8,128)S(1)} %get-tuple-element.16.field.bond, f32[256,256]{1,0:T(8,128)S(1)} %first.1.applied.field), custom_call_target="tpu_custom_call" | custom-call | tf_op jit(solution)/shard_map/next_inverse/pallas_call | solution.py:346
  43.0 0.0 collective-permute-done.8.near
  43.1 2.5 %local_terms.3.part = f32[256,256]{1,0:T(8,128)S(1)} custom-call(f32[256,256]{1,0:T(8,128)S(1)} %first.1.applied.field, f32[256,256]{1,0:T(8,128)S(1)} %collective-permute-done.8.near, f32[1,14,256,256]{3,2,1,0:T(8,128)S(1)} %copy-done.1, f32[1,14,256,256]{3,2,1,0:T(8,128)S(1)} %copy-done, f32[4,256,256]{2,1,0:T(8,128)S(1)} %collective-permute-done.6.right_near), custom_call_target="tpu_custom_call" | custom-call | tf_op jit(solution)/shard_map/local_terms/pallas_call | solution.py:413
  45.6 0.0 collective-permute-done.7.far
  45.6 2.0 %second.1 = (f32[256,256]{1,0:T(8,128)S(1)}, f32[16,1,128]{2,1,0:T(1,128)}) custom-call(f32[256,256]{1,0:T(8,128)S(1)} %get-tuple-element.17.mask, f32[256,256]{1,0:T(8,128)S(1)} %collective-permute-done.7.far, f32[1,14,256,256]{3,2,1,0:T(8,128)S(1)} %copy-done.1, f32[2,256,256]{2,1,0:T(8,128)S(1)} %collective-permute-done.3.early, ...), custom_call_target="tpu_custom_call" | custom-call | tf_op jit(solution)/shard_map/second/pallas_call | solution.py:473
  47.6 11.2 %all-to-all-start = ((f32[16,1,128]{2,1,0:T(1,128)}), f32[16,1,128]{2,1,0:T(1,128)S(1)}, u32[]{:S(2)}, u32[]{:S(2)}) async-start(f32[16,1,128]{2,1,0:T(1,128)} %get-tuple-element.24), calls=%async_computation | async-start | bytes 16384 | tf_op jit(solution)/shard_map/all_to_all | solution.py:543
  58.8 5.3 %upper_rows.1.top = f32[256,256]{1,0:T(8,128)S(1)} custom-call(s32[16]{0:T(128)S(1)} %copy-done.3, f32[320,128]{1,0:T(8,128)S(1)} %get-tuple-element.15.packed, f32[1,2,256,256]{3,2,1,0:T(8,128)S(1)} %copy-done.2), custom_call_target="tpu_custom_call" | custom-call | tf_op jit(solution)/shard_map/upper_rows/pallas_call | solution.py:318
  64.1 3.9 %lower_rows.1 = f32[1,2,256,256]{3,2,1,0:T(8,128)} custom-call(s32[16]{0:T(128)S(1)} %copy-done.3, f32[320,128]{1,0:T(8,128)S(1)} %collective-permute-done.1.near, f32[320,128]{1,0:T(8,128)S(1)} %collective-permute-done.2.far, f32[256,256]{1,0:T(8,128)S(1)} %get-tuple-element.22.inv, f32[1,2,256,256]{3,2,1,0:T(8,128)S(1)} %copy-done.2, ...), custom_call_target="tpu_custom_call" | custom-call | tf_op jit(solution)/shard_map/lower_rows/pallas_call | solution.py:375
  68.0 0.0 all-to-all-done.gathered
  68.0 0.9 %final.1 = f32[1,256,256]{2,1,0:T(8,128)} custom-call(f32[16,1,128]{2,1,0:T(1,128)S(1)} %all-to-all-done.gathered, f32[256,256]{1,0:T(8,128)S(1)} %get-tuple-element.16.field.bond, f32[256,256]{1,0:T(8,128)S(1)} %first.1.applied.field, f32[256,256]{1,0:T(8,128)S(1)} %get-tuple-element.25.twice), custom_call_target="tpu_custom_call" | custom-call | tf_op jit(solution)/shard_map/final/pallas_call | solution.py:500
Async XLA Ops:
  0.6 24.7 %copy-start = (f32[1,14,256,256]{3,2,1,0:T(8,128)S(1)}, f32[1,14,256,256]{3,2,1,0:T(8,128)}, u32[]{:S(2)}) copy-start(f32[1,14,256,256]{3,2,1,0:T(8,128)} %right.7) | copy-start | bytes 11010052
  0.6 8.3 %copy-start.2 = (f32[1,2,256,256]{3,2,1,0:T(8,128)S(1)}, f32[1,2,256,256]{3,2,1,0:T(8,128)}, u32[]{:S(2)}) copy-start(f32[1,2,256,256]{3,2,1,0:T(8,128)} %site.7) | copy-start | bytes 1572868
  0.7 8.3 %copy-start.3 = (s32[16]{0:T(128)S(1)}, s32[16]{0:T(128)}, u32[]{:S(2)}) copy-start(s32[16]{0:T(128)} %sizes.5) | copy-start | bytes 196
  0.7 24.6 %copy-start.1 = (f32[1,14,256,256]{3,2,1,0:T(8,128)S(1)}, f32[1,14,256,256]{3,2,1,0:T(8,128)}, u32[]{:S(2)}) copy-start(f32[1,14,256,256]{3,2,1,0:T(8,128)} %left.7) | copy-start | bytes 11010052
  2.4 22.9 %collective-permute-start.6 = (f32[4,256,256]{2,1,0:T(8,128)S(1)}, f32[4,256,256]{2,1,0:T(8,128)S(1)}, u32[]{:S(2)}, u32[]{:S(2)}) collective-permute-start(f32[4,256,256]{2,1,0:T(8,128)S(1)} %get-tuple-element.21), channel_id=1, source_target_pairs={{0,1},{2,3},{4,5},{6,7},{8,9},{10,11},{12,13},{14,15},{1,0},{3,2},... | collective-permute-start | bytes 3145736 | tf_op jit(solution)/shard_map/ppermute | solution.py:519
  4.7 4.2 %collective-permute-start = (f32[256,256]{1,0:T(8,128)S(1)}, f32[256,256]{1,0:T(8,128)S(1)}, u32[]{:S(2)}, u32[]{:S(2)}) collective-permute-start(f32[256,256]{1,0:T(8,128)S(1)} %get-tuple-element.14), channel_id=1, source_target_pairs={{0,1},{1,2},{2,3},{3,4},{4,5},{5,6},{6,7},{7,8},{8,9},{9,10},{10,1... | collective-permute-start | bytes 786440 | tf_op jit(solution)/shard_map/ppermute | solution.py:513
  6.8 21.0 %collective-permute-start.4 = (f32[2,256,256]{2,1,0:T(8,128)S(1)}, f32[2,256,256]{2,1,0:T(8,128)S(1)}, u32[]{:S(2)}, u32[]{:S(2)}) collective-permute-start(f32[2,256,256]{2,1,0:T(8,128)S(1)} %get-tuple-element.19), channel_id=1, source_target_pairs={{1,2},{3,4},{5,6},{7,8},{9,10},{11,12},{13,14},{2,1},{4,3},{6,5},{... | collective-permute-start | bytes 1572872 | tf_op jit(solution)/shard_map/ppermute | solution.py:519
  7.5 20.3 %collective-permute-start.5 = (f32[2,256,256]{2,1,0:T(8,128)S(1)}, f32[2,256,256]{2,1,0:T(8,128)S(1)}, u32[]{:S(2)}, u32[]{:S(2)}) collective-permute-start(f32[2,256,256]{2,1,0:T(8,128)S(1)} %get-tuple-element.20), channel_id=1, source_target_pairs={{1,2},{5,6},{9,10},{13,14},{2,1},{6,5},{10,9},{14,13},{17,18},{21,... | collective-permute-start | bytes 1572872 | tf_op jit(solution)/shard_map/ppermute | solution.py:519
  8.2 19.6 %collective-permute-start.3 = (f32[2,256,256]{2,1,0:T(8,128)S(1)}, f32[2,256,256]{2,1,0:T(8,128)S(1)}, u32[]{:S(2)}, u32[]{:S(2)}) collective-permute-start(f32[2,256,256]{2,1,0:T(8,128)S(1)} %get-tuple-element.18), channel_id=1, source_target_pairs={{3,4},{7,8},{11,12},{4,3},{8,7},{12,11},{19,20},{23,24},{27,28},{2... | collective-permute-start | bytes 1572872 | tf_op jit(solution)/shard_map/ppermute | solution.py:519
  16.8 7.9 %collective-permute-start.1 = (f32[320,128]{1,0:T(8,128)S(1)}, f32[320,128]{1,0:T(8,128)S(1)}, u32[]{:S(2)}, u32[]{:S(2)}) collective-permute-start(f32[320,128]{1,0:T(8,128)S(1)} %get-tuple-element.15.packed), channel_id=1, source_target_pairs={{0,1},{2,3},{4,5},{6,7},{8,9},{10,11},{12,13},{14,15},{1,0},{3,2},... | collective-permute-start | bytes 491528 | tf_op jit(solution)/shard_map/ppermute | solution.py:519
  24.6 3.2 %collective-permute-start.2 = (f32[320,128]{1,0:T(8,128)S(1)}, f32[320,128]{1,0:T(8,128)S(1)}, u32[]{:S(2)}, u32[]{:S(2)}) collective-permute-start(f32[320,128]{1,0:T(8,128)S(1)} %get-tuple-element.15.packed), channel_id=1, source_target_pairs={{1,2},{3,4},{5,6},{7,8},{9,10},{11,12},{13,14},{2,1},{4,3},{6,5},{... | collective-permute-start | bytes 491528 | tf_op jit(solution)/shard_map/ppermute | solution.py:519
  29.2 13.9 %collective-permute-start.8 = (f32[256,256]{1,0:T(8,128)S(1)}, f32[256,256]{1,0:T(8,128)S(1)}, u32[]{:S(2)}, u32[]{:S(2)}) collective-permute-start(f32[256,256]{1,0:T(8,128)S(1)} %first.1.applied.field), channel_id=1, source_target_pairs={{0,1},{2,3},{4,5},{6,7},{8,9},{10,11},{12,13},{14,15},{1,0},{3,2},... | collective-permute-start | bytes 786440 | tf_op jit(solution)/shard_map/ppermute | solution.py:519
  40.1 5.5 %collective-permute-start.7 = (f32[256,256]{1,0:T(8,128)S(1)}, f32[256,256]{1,0:T(8,128)S(1)}, u32[]{:S(2)}, u32[]{:S(2)}) collective-permute-start(f32[256,256]{1,0:T(8,128)S(1)} %first.1.applied.field), channel_id=1, source_target_pairs={{1,2},{3,4},{5,6},{7,8},{9,10},{11,12},{13,14},{2,1},{4,3},{6,5},{... | collective-permute-start | bytes 786440 | tf_op jit(solution)/shard_map/ppermute | solution.py:519
  47.6 20.4 %all-to-all-start = ((f32[16,1,128]{2,1,0:T(1,128)}), f32[16,1,128]{2,1,0:T(1,128)S(1)}, u32[]{:S(2)}, u32[]{:S(2)}) async-start(f32[16,1,128]{2,1,0:T(1,128)} %get-tuple-element.24), calls=%async_computation | async-start | bytes 16384 | tf_op jit(solution)/shard_map/all_to_all | solution.py:543

commit v5 on v4

--- a/solution.py
+++ b/solution.py
@@ -8,6 +8,7 @@
 W_DN = 4
 W_UP = 4
 PANEL = 16
+CHUNKS = 2
 LANES = 128
 
 f32, bf16 = jnp.float32, jnp.bfloat16
@@ -483,7 +484,7 @@
     )(mask, far, left, *right_far, part, bond, applied, known)
 
 
-def final_kernel(gathered, bond, applied, twice, out):
+def final_kernel(gathered, bond, applied, twice, out, staged, sems):
     sums = jnp.sum(gathered[...], 0)
     bb, ba, aa, bt, at, tt = (jnp.broadcast_to(sums[:, i : i + 1], (1, bond.shape[-1])) for i in range(6))
     rate = ba / bb
@@ -492,7 +493,15 @@
     norm = c0 * (c0 * bb + 2.0 * (c1 * ba + bt)) + c1 * (c1 * aa + 2.0 * at) + tt
     scale = jnp.sqrt(bb / norm)
     steps = (c0 * scale, (c1 * time_step) * scale, (0.5 * time_step * time_step) * scale)
-    out[0] = steps[0] * bond[...] + steps[1] * applied[...] + steps[2] * twice[...]
+    copies = []
+    size = staged.shape[0] // CHUNKS
+    for i in range(CHUNKS):
+        part = pl.ds(i * size, size)
+        staged[part, :] = steps[0] * bond[part, :] + steps[1] * applied[part, :] + steps[2] * twice[part, :]
+        copies.append(pltpu.make_async_copy(staged.at[part], out.at[0, part], sems.at[i]))
+        copies[i].start()
+    for copy in copies:
+        copy.wait()
 
 
 def final(gathered, bond, applied, twice):
@@ -501,7 +510,8 @@
         final_kernel,
         out_shape=jax.ShapeDtypeStruct((1, n, n), f32),
         in_specs=[VM] * 4,
-        out_specs=VM,
+        out_specs=ANY,
+        scratch_shapes=[pltpu.VMEM((n, n), f32), pltpu.SemaphoreType.DMA((CHUNKS,))],
         compiler_params=params(4),
         name="final",
     )(gathered, bond, applied, twice)

time: 69.1 us -> 69.3 us (level)
  no operation moved by 1% of the time
where the time goes in v5:
time: 69.3 us; the launch traced here: 69 us
  starting transfers between devices  35 us (51%)
  Pallas kernels  31.9 us (46%)
  waiting for transfers between devices  1.05 us (2%)
  between operations  1.04 us (2%)
    ppermute x8, starting transfers between devices, swapped(): return lax.ppermute(value, 'row', pairs + [(j, i) for i, j in pairs])  21.7 us
    all_to_all x1, starting transfers between devices, bond_update(): gathered = lax.all_to_all(spread, 'row', 0, 0, tiled=True)  11.2 us
    pallas_call x1, Pallas kernels, factor(): pl.pallas_call(factor_kernel, out_shape=[jax.ShapeDtypeStruct((n, n), f32...  7.79 us
    pallas_call x1, Pallas kernels, upper_rows(): pl.pallas_call(upper_rows_kernel, out_shape=jax.ShapeDtypeStruct((n, n),...  5.25 us
    pallas_call x2, Pallas kernels, local_terms(): pl.pallas_call(local_kernel, out_shape=jax.ShapeDtypeStruct((n, n), f32),...  5 us
    pallas_call x1, Pallas kernels, lower_rows(): pl.pallas_call(lower_rows_kernel, out_shape=jax.ShapeDtypeStruct((1, 2, n...  3.88 us
    pallas_call x1, Pallas kernels, next_inverse(): pl.pallas_call(next_inverse_kernel, out_shape=[jax.ShapeDtypeStruct((n, n...  2.26 us
    ppermute x1, starting transfers between devices, shifted_by(): lax.ppermute(value, 'row', [(source, source + steps) for source in range(...  2.1 us
  transfers between devices with their start and end apart: 10, of which 1 were waited for; matrix products, arithmetic and copies ran while one was open for 0% of the time, Pallas kernels for 38%

profile of v5, /device:TPU:0, one launch (start us, length us, event | category | flops | bytes accessed | tf_op | source)
XLA Modules:
  0.0 69.0 jit_solution(12871535368588518643)
XLA Ops:
  0.6 0.0 copy-start
  0.6 0.0 copy-start.2
  0.7 0.0 copy-start.3
  0.7 0.0 copy-start.1
  0.7 1.7 %take_rest.1 = (f32[2,256,256]{2,1,0:T(8,128)S(1)}, f32[2,256,256]{2,1,0:T(8,128)S(1)}, f32[4,256,256]{2,1,0:T(8,128)S(1)}) custom-call(f32[1,14,256,256]{3,2,1,0:T(8,128)} %right.7), custom_call_target="tpu_custom_call" | custom-call | tf_op jit(solution)/shard_map/take_rest/pallas_call | solution.py:125
  2.4 0.6 collective-permute-start.6
  3.0 1.7 %take_early.1 = (f32[256,256]{1,0:T(8,128)S(1)}, f32[2,256,256]{2,1,0:T(8,128)S(1)}) custom-call(f32[1,2,256,256]{3,2,1,0:T(8,128)} %site.7, f32[1,14,256,256]{3,2,1,0:T(8,128)} %right.7), custom_call_target="tpu_custom_call" | custom-call | tf_op jit(solution)/shard_map/take_early/pallas_call | solution.py:112
  4.7 2.1 %collective-permute-start = (f32[256,256]{1,0:T(8,128)S(1)}, f32[256,256]{1,0:T(8,128)S(1)}, u32[]{:S(2)}, u32[]{:S(2)}) collective-permute-start(f32[256,256]{1,0:T(8,128)S(1)} %get-tuple-element.14), channel_id=1, source_target_pairs={{0,1},{1,2},{2,3},{3,4},{4,5},{5,6},{6,7},{7,8},{8,9},{9,10},{10,1... | collective-permute-start | bytes 786440 | tf_op jit(solution)/shard_map/ppermute | solution.py:523
  6.8 0.7 %collective-permute-start.4 = (f32[2,256,256]{2,1,0:T(8,128)S(1)}, f32[2,256,256]{2,1,0:T(8,128)S(1)}, u32[]{:S(2)}, u32[]{:S(2)}) collective-permute-start(f32[2,256,256]{2,1,0:T(8,128)S(1)} %get-tuple-element.19), channel_id=1, source_target_pairs={{1,2},{3,4},{5,6},{7,8},{9,10},{11,12},{13,14},{2,1},{4,3},{6,5},{... | collective-permute-start | bytes 1572872 | tf_op jit(solution)/shard_map/ppermute | solution.py:529
  7.5 0.7 %collective-permute-start.5 = (f32[2,256,256]{2,1,0:T(8,128)S(1)}, f32[2,256,256]{2,1,0:T(8,128)S(1)}, u32[]{:S(2)}, u32[]{:S(2)}) collective-permute-start(f32[2,256,256]{2,1,0:T(8,128)S(1)} %get-tuple-element.20), channel_id=1, source_target_pairs={{1,2},{5,6},{9,10},{13,14},{2,1},{6,5},{10,9},{14,13},{17,18},{21,... | collective-permute-start | bytes 1572872 | tf_op jit(solution)/shard_map/ppermute | solution.py:529
  8.2 0.7 %collective-permute-start.3 = (f32[2,256,256]{2,1,0:T(8,128)S(1)}, f32[2,256,256]{2,1,0:T(8,128)S(1)}, u32[]{:S(2)}, u32[]{:S(2)}) collective-permute-start(f32[2,256,256]{2,1,0:T(8,128)S(1)} %get-tuple-element.18), channel_id=1, source_target_pairs={{3,4},{7,8},{11,12},{4,3},{8,7},{12,11},{19,20},{23,24},{27,28},{2... | collective-permute-start | bytes 1572872 | tf_op jit(solution)/shard_map/ppermute | solution.py:529
  8.9 0.0 collective-permute-done.lower
  9.0 0.0 copy-done.2
  9.0 0.0 copy-done.3
  9.0 7.8 %factor.1 = (f32[256,256]{1,0:T(8,128)S(1)}, f32[320,128]{1,0:T(8,128)S(1)}, f32[256,256]{1,0:T(8,128)S(1)}) custom-call(s32[16]{0:T(128)S(1)} %copy-done.3, f32[1,2,256,256]{3,2,1,0:T(8,128)S(1)} %copy-done.2, f32[256,256]{1,0:T(8,128)S(1)} %collective-permute-done.lower), custom_call_target="tpu_custom_call" | custom-call | tf_op jit(solution)/shard_map/factor/pallas_call | solution.py:251
  16.8 6.8 %collective-permute-start.1 = (f32[320,128]{1,0:T(8,128)S(1)}, f32[320,128]{1,0:T(8,128)S(1)}, u32[]{:S(2)}, u32[]{:S(2)}) collective-permute-start(f32[320,128]{1,0:T(8,128)S(1)} %get-tuple-element.15.packed), channel_id=1, source_target_pairs={{0,1},{2,3},{4,5},{6,7},{8,9},{10,11},{12,13},{14,15},{1,0},{3,2},... | collective-permute-start | bytes 491528 | tf_op jit(solution)/shard_map/ppermute | solution.py:529
  23.6 1.0 %collective-permute-done.1.near = f32[320,128]{1,0:T(8,128)S(1)} collective-permute-done((f32[320,128]{1,0:T(8,128)S(1)}, f32[320,128]{1,0:T(8,128)S(1)}, u32[]{:S(2)}, u32[]{:S(2)}) %collective-permute-start.1) | collective-permute-done | bytes 163872 | tf_op jit(solution)/shard_map/ppermute | solution.py:529
  24.6 0.7 collective-permute-start.2
  25.3 0.0 collective-permute-done.6.right_near
  25.3 0.0 copy-done
  25.3 0.0 copy-done.1
  25.3 2.5 %local_terms.2.part = f32[256,256]{1,0:T(8,128)S(1)} custom-call(f32[256,256]{1,0:T(8,128)S(1)} %get-tuple-element.16.field.bond, f32[320,128]{1,0:T(8,128)S(1)} %collective-permute-done.1.near, f32[1,14,256,256]{3,2,1,0:T(8,128)S(1)} %copy-done.1, f32[1,14,256,256]{3,2,1,0:T(8,128)S(1)} %copy-done, f32[4,256,256]{2,1,0:T(8,128)S(1)} %collective-permute-done.6.right_near), custom_call_target="tpu_custom_call" | custom-call | tf_op jit(solution)/shard_map/local_terms/pallas_call | solution.py:414
  27.8 0.0 collective-permute-done.2.far
  27.8 0.0 collective-permute-done.4.middle
  27.9 0.0 collective-permute-done.5.late
  27.9 0.0 collective-permute-done.3.early
  27.9 1.3 %first.1.applied.field = f32[256,256]{1,0:T(8,128)S(1)} custom-call(f32[256,256]{1,0:T(8,128)S(1)} %get-tuple-element.17.mask, f32[320,128]{1,0:T(8,128)S(1)} %collective-permute-done.2.far, f32[1,14,256,256]{3,2,1,0:T(8,128)S(1)} %copy-done.1, f32[2,256,256]{2,1,0:T(8,128)S(1)} %collective-permute-done.3.early, ...), custom_call_target="tpu_custom_call" | custom-call | tf_op jit(solution)/shard_map/first/pallas_call | solution.py:443
  29.2 10.9 %collective-permute-start.8 = (f32[256,256]{1,0:T(8,128)S(1)}, f32[256,256]{1,0:T(8,128)S(1)}, u32[]{:S(2)}, u32[]{:S(2)}) collective-permute-start(f32[256,256]{1,0:T(8,128)S(1)} %first.1.applied.field), channel_id=1, source_target_pairs={{0,1},{2,3},{4,5},{6,7},{8,9},{10,11},{12,13},{14,15},{1,0},{3,2},... | collective-permute-start | bytes 786440 | tf_op jit(solution)/shard_map/ppermute | solution.py:529
  40.1 0.7 collective-permute-start.7
  40.8 2.3 %next_inverse.1 = (f32[256,256]{1,0:T(8,128)S(1)}, f32[1,128]{1,0:T(1,128)S(1)}) custom-call(f32[320,128]{1,0:T(8,128)S(1)} %collective-permute-done.1.near, f32[320,128]{1,0:T(8,128)S(1)} %collective-permute-done.2.far, f32[256,256]{1,0:T(8,128)S(1)} %get-tuple-element.16.field.bond, f32[256,256]{1,0:T(8,128)S(1)} %first.1.applied.field), custom_call_target="tpu_custom_call" | custom-call | tf_op jit(solution)/shard_map/next_inverse/pallas_call | solution.py:347
  43.0 0.0 collective-permute-done.8.near
  43.1 2.5 %local_terms.3.part = f32[256,256]{1,0:T(8,128)S(1)} custom-call(f32[256,256]{1,0:T(8,128)S(1)} %first.1.applied.field, f32[256,256]{1,0:T(8,128)S(1)} %collective-permute-done.8.near, f32[1,14,256,256]{3,2,1,0:T(8,128)S(1)} %copy-done.1, f32[1,14,256,256]{3,2,1,0:T(8,128)S(1)} %copy-done, f32[4,256,256]{2,1,0:T(8,128)S(1)} %collective-permute-done.6.right_near), custom_call_target="tpu_custom_call" | custom-call | tf_op jit(solution)/shard_map/local_terms/pallas_call | solution.py:414
  45.6 0.0 collective-permute-done.7.far
  45.6 2.0 %second.1 = (f32[256,256]{1,0:T(8,128)S(1)}, f32[16,1,128]{2,1,0:T(1,128)}) custom-call(f32[256,256]{1,0:T(8,128)S(1)} %get-tuple-element.17.mask, f32[256,256]{1,0:T(8,128)S(1)} %collective-permute-done.7.far, f32[1,14,256,256]{3,2,1,0:T(8,128)S(1)} %copy-done.1, f32[2,256,256]{2,1,0:T(8,128)S(1)} %collective-permute-done.3.early, ...), custom_call_target="tpu_custom_call" | custom-call | tf_op jit(solution)/shard_map/second/pallas_call | solution.py:474
  47.6 11.2 %all-to-all-start = ((f32[16,1,128]{2,1,0:T(1,128)}), f32[16,1,128]{2,1,0:T(1,128)S(1)}, u32[]{:S(2)}, u32[]{:S(2)}) async-start(f32[16,1,128]{2,1,0:T(1,128)} %get-tuple-element.24), calls=%async_computation | async-start | bytes 16384 | tf_op jit(solution)/shard_map/all_to_all | solution.py:553
  58.8 5.3 %upper_rows.1.top = f32[256,256]{1,0:T(8,128)S(1)} custom-call(s32[16]{0:T(128)S(1)} %copy-done.3, f32[320,128]{1,0:T(8,128)S(1)} %get-tuple-element.15.packed, f32[1,2,256,256]{3,2,1,0:T(8,128)S(1)} %copy-done.2), custom_call_target="tpu_custom_call" | custom-call | tf_op jit(solution)/shard_map/upper_rows/pallas_call | solution.py:319
  64.1 3.9 %lower_rows.1 = f32[1,2,256,256]{3,2,1,0:T(8,128)} custom-call(s32[16]{0:T(128)S(1)} %copy-done.3, f32[320,128]{1,0:T(8,128)S(1)} %collective-permute-done.1.near, f32[320,128]{1,0:T(8,128)S(1)} %collective-permute-done.2.far, f32[256,256]{1,0:T(8,128)S(1)} %get-tuple-element.22.inv, f32[1,2,256,256]{3,2,1,0:T(8,128)S(1)} %copy-done.2, ...), custom_call_target="tpu_custom_call" | custom-call | tf_op jit(solution)/shard_map/lower_rows/pallas_call | solution.py:376
  68.0 0.0 all-to-all-done.gathered
  68.0 0.9 %final.1 = f32[1,256,256]{2,1,0:T(8,128)} custom-call(f32[16,1,128]{2,1,0:T(1,128)S(1)} %all-to-all-done.gathered, f32[256,256]{1,0:T(8,128)S(1)} %get-tuple-element.16.field.bond, f32[256,256]{1,0:T(8,128)S(1)} %first.1.applied.field, f32[256,256]{1,0:T(8,128)S(1)} %get-tuple-element.25.twice), custom_call_target="tpu_custom_call" | custom-call | tf_op jit(solution)/shard_map/final/pallas_call | solution.py:509
Async XLA Ops:
  0.6 24.7 %copy-start = (f32[1,14,256,256]{3,2,1,0:T(8,128)S(1)}, f32[1,14,256,256]{3,2,1,0:T(8,128)}, u32[]{:S(2)}) copy-start(f32[1,14,256,256]{3,2,1,0:T(8,128)} %right.7) | copy-start | bytes 11010052
  0.6 8.3 %copy-start.2 = (f32[1,2,256,256]{3,2,1,0:T(8,128)S(1)}, f32[1,2,256,256]{3,2,1,0:T(8,128)}, u32[]{:S(2)}) copy-start(f32[1,2,256,256]{3,2,1,0:T(8,128)} %site.7) | copy-start | bytes 1572868
  0.7 8.3 %copy-start.3 = (s32[16]{0:T(128)S(1)}, s32[16]{0:T(128)}, u32[]{:S(2)}) copy-start(s32[16]{0:T(128)} %sizes.5) | copy-start | bytes 196
  0.7 24.6 %copy-start.1 = (f32[1,14,256,256]{3,2,1,0:T(8,128)S(1)}, f32[1,14,256,256]{3,2,1,0:T(8,128)}, u32[]{:S(2)}) copy-start(f32[1,14,256,256]{3,2,1,0:T(8,128)} %left.7) | copy-start | bytes 11010052
  2.4 22.9 %collective-permute-start.6 = (f32[4,256,256]{2,1,0:T(8,128)S(1)}, f32[4,256,256]{2,1,0:T(8,128)S(1)}, u32[]{:S(2)}, u32[]{:S(2)}) collective-permute-start(f32[4,256,256]{2,1,0:T(8,128)S(1)} %get-tuple-element.21), channel_id=1, source_target_pairs={{0,1},{2,3},{4,5},{6,7},{8,9},{10,11},{12,13},{14,15},{1,0},{3,2},... | collective-permute-start | bytes 3145736 | tf_op jit(solution)/shard_map/ppermute | solution.py:529
  4.7 4.2 %collective-permute-start = (f32[256,256]{1,0:T(8,128)S(1)}, f32[256,256]{1,0:T(8,128)S(1)}, u32[]{:S(2)}, u32[]{:S(2)}) collective-permute-start(f32[256,256]{1,0:T(8,128)S(1)} %get-tuple-element.14), channel_id=1, source_target_pairs={{0,1},{1,2},{2,3},{3,4},{4,5},{5,6},{6,7},{7,8},{8,9},{9,10},{10,1... | collective-permute-start | bytes 786440 | tf_op jit(solution)/shard_map/ppermute | solution.py:523
  6.8 21.0 %collective-permute-start.4 = (f32[2,256,256]{2,1,0:T(8,128)S(1)}, f32[2,256,256]{2,1,0:T(8,128)S(1)}, u32[]{:S(2)}, u32[]{:S(2)}) collective-permute-start(f32[2,256,256]{2,1,0:T(8,128)S(1)} %get-tuple-element.19), channel_id=1, source_target_pairs={{1,2},{3,4},{5,6},{7,8},{9,10},{11,12},{13,14},{2,1},{4,3},{6,5},{... | collective-permute-start | bytes 1572872 | tf_op jit(solution)/shard_map/ppermute | solution.py:529
  7.5 20.3 %collective-permute-start.5 = (f32[2,256,256]{2,1,0:T(8,128)S(1)}, f32[2,256,256]{2,1,0:T(8,128)S(1)}, u32[]{:S(2)}, u32[]{:S(2)}) collective-permute-start(f32[2,256,256]{2,1,0:T(8,128)S(1)} %get-tuple-element.20), channel_id=1, source_target_pairs={{1,2},{5,6},{9,10},{13,14},{2,1},{6,5},{10,9},{14,13},{17,18},{21,... | collective-permute-start | bytes 1572872 | tf_op jit(solution)/shard_map/ppermute | solution.py:529
  8.2 19.6 %collective-permute-start.3 = (f32[2,256,256]{2,1,0:T(8,128)S(1)}, f32[2,256,256]{2,1,0:T(8,128)S(1)}, u32[]{:S(2)}, u32[]{:S(2)}) collective-permute-start(f32[2,256,256]{2,1,0:T(8,128)S(1)} %get-tuple-element.18), channel_id=1, source_target_pairs={{3,4},{7,8},{11,12},{4,3},{8,7},{12,11},{19,20},{23,24},{27,28},{2... | collective-permute-start | bytes 1572872 | tf_op jit(solution)/shard_map/ppermute | solution.py:529
  16.8 7.9 %collective-permute-start.1 = (f32[320,128]{1,0:T(8,128)S(1)}, f32[320,128]{1,0:T(8,128)S(1)}, u32[]{:S(2)}, u32[]{:S(2)}) collective-permute-start(f32[320,128]{1,0:T(8,128)S(1)} %get-tuple-element.15.packed), channel_id=1, source_target_pairs={{0,1},{2,3},{4,5},{6,7},{8,9},{10,11},{12,13},{14,15},{1,0},{3,2},... | collective-permute-start | bytes 491528 | tf_op jit(solution)/shard_map/ppermute | solution.py:529
  24.6 3.2 %collective-permute-start.2 = (f32[320,128]{1,0:T(8,128)S(1)}, f32[320,128]{1,0:T(8,128)S(1)}, u32[]{:S(2)}, u32[]{:S(2)}) collective-permute-start(f32[320,128]{1,0:T(8,128)S(1)} %get-tuple-element.15.packed), channel_id=1, source_target_pairs={{1,2},{3,4},{5,6},{7,8},{9,10},{11,12},{13,14},{2,1},{4,3},{6,5},{... | collective-permute-start | bytes 491528 | tf_op jit(solution)/shard_map/ppermute | solution.py:529
  29.2 13.9 %collective-permute-start.8 = (f32[256,256]{1,0:T(8,128)S(1)}, f32[256,256]{1,0:T(8,128)S(1)}, u32[]{:S(2)}, u32[]{:S(2)}) collective-permute-start(f32[256,256]{1,0:T(8,128)S(1)} %first.1.applied.field), channel_id=1, source_target_pairs={{0,1},{2,3},{4,5},{6,7},{8,9},{10,11},{12,13},{14,15},{1,0},{3,2},... | collective-permute-start | bytes 786440 | tf_op jit(solution)/shard_map/ppermute | solution.py:529
  40.1 5.5 %collective-permute-start.7 = (f32[256,256]{1,0:T(8,128)S(1)}, f32[256,256]{1,0:T(8,128)S(1)}, u32[]{:S(2)}, u32[]{:S(2)}) collective-permute-start(f32[256,256]{1,0:T(8,128)S(1)} %first.1.applied.field), channel_id=1, source_target_pairs={{1,2},{3,4},{5,6},{7,8},{9,10},{11,12},{13,14},{2,1},{4,3},{6,5},{... | collective-permute-start | bytes 786440 | tf_op jit(solution)/shard_map/ppermute | solution.py:529
  47.6 20.4 %all-to-all-start = ((f32[16,1,128]{2,1,0:T(1,128)}), f32[16,1,128]{2,1,0:T(1,128)S(1)}, u32[]{:S(2)}, u32[]{:S(2)}) async-start(f32[16,1,128]{2,1,0:T(1,128)} %get-tuple-element.24), calls=%async_computation | async-start | bytes 16384 | tf_op jit(solution)/shard_map/all_to_all | solution.py:553

commit v6 on v5

--- a/solution.py
+++ b/solution.py
@@ -91,13 +91,12 @@
 
 def take_rest_kernel(right, middle, late, near, sems):
     q = lax.axis_index("row")
-    half = late.shape[0]
+    half = middle.shape[0]
     start = first_far(q)
-    turn = jnp.where(far_kind(q) == 0, start + half, start)
     run_copies(
         (
-            pltpu.make_async_copy(right.at[0, pl.ds(turn, half)], middle, sems.at[0]),
-            pltpu.make_async_copy(right.at[0, pl.ds(start + half, half)], late, sems.at[1]),
+            pltpu.make_async_copy(right.at[0, pl.ds(start + half, half)], middle, sems.at[0]),
+            pltpu.make_async_copy(right.at[0, pl.ds(start, 2 * half)], late, sems.at[1]),
             pltpu.make_async_copy(right.at[0, pl.ds(lax.rem(q, 2) * W_DN, W_DN)], near, sems.at[2]),
         )
     )
@@ -124,7 +123,11 @@
     n = right.shape[-1]
     return pl.pallas_call(
         take_rest_kernel,
-        out_shape=[jax.ShapeDtypeStruct((W_UP // 2, n, n), f32)] * 2 + [jax.ShapeDtypeStruct((W_DN, n, n), f32)],
+        out_shape=[
+            jax.ShapeDtypeStruct((W_UP // 2, n, n), f32),
+            jax.ShapeDtypeStruct((W_UP, n, n), f32),
+            jax.ShapeDtypeStruct((W_DN, n, n), f32),
+        ],
         in_specs=[HB],
         out_specs=[ANY] * 3,
         scratch_shapes=[pltpu.SemaphoreType.DMA((3,))],
@@ -429,8 +432,8 @@
     total = part[...]
     f = split2(field_of(far, n))
     for a in range(2 * half):
-        pair = (early[a], middle[a]) if a < half else (middle[a - half], late[a - half])
-        total = total + channel(left, lax.rem(q, 2) * W_DN + a, f, jnp.where(kind, *pair))
+        of_kind = early[a] if a < half else middle[a - half]
+        total = total + channel(left, lax.rem(q, 2) * W_DN + a, f, jnp.where(kind, of_kind, late[a]))
     return jnp.where(mask[...] > 0.0, total, 0.0)
 
 
@@ -535,7 +538,7 @@
     early = swapped(early, 3, 4)
     lower = shifted_by(source, 1)
     middle, late, to_near = take_rest(right)
-    middle = swapped(middle, 1)
+    middle = swapped(middle, 3, 4)
     late = swapped(late, 1, 4)
     right_far = (early, middle, late)
     right_near = swapped(to_near, 0)

time: 69.3 us -> 81.5 us (1.18)
  starting transfers between devices: 35 us -> 47.6 us
    ppermute x8, starting transfers between devices: 21.7 us -> 31 us  [swapped(): return lax.ppermute(value, 'row', pairs + [(j, i) for i, j in pairs])]
    ppermute x1, starting transfers between devices: 2.1 us -> 5.88 us  [shifted_by(): lax.ppermute(value, 'row', [(source, source + steps) for source in range(...]
  transfers between devices with their start and end apart: 10 -> 10, of which waited for: 1 -> 1; matrix products, arithmetic and copies ran while one was open for 0% -> 0% of each run, Pallas kernels for 38% -> 31%
where the time goes in v6:
time: 81.5 us; the launch traced here: 81.2 us
  starting transfers between devices  47.6 us (58%)
  Pallas kernels  31.5 us (39%)
  waiting for transfers between devices  1.05 us (1%)
  between operations  1.04 us (1%)
    ppermute x8, starting transfers between devices, swapped(): return lax.ppermute(value, 'row', pairs + [(j, i) for i, j in pairs])  31 us
    all_to_all x1, starting transfers between devices, bond_update(): gathered = lax.all_to_all(spread, 'row', 0, 0, tiled=True)  10.8 us
    pallas_call x1, Pallas kernels, factor(): pl.pallas_call(factor_kernel, out_shape=[jax.ShapeDtypeStruct((n, n), f32...  7.79 us
    ppermute x1, starting transfers between devices, shifted_by(): lax.ppermute(value, 'row', [(source, source + steps) for source in range(...  5.88 us
    pallas_call x1, Pallas kernels, upper_rows(): pl.pallas_call(upper_rows_kernel, out_shape=jax.ShapeDtypeStruct((n, n),...  5.25 us
    pallas_call x2, Pallas kernels, local_terms(): pl.pallas_call(local_kernel, out_shape=jax.ShapeDtypeStruct((n, n), f32),...  5.07 us
    pallas_call x1, Pallas kernels, lower_rows(): pl.pallas_call(lower_rows_kernel, out_shape=jax.ShapeDtypeStruct((1, 2, n...  3.87 us
    pallas_call x1, Pallas kernels, next_inverse(): pl.pallas_call(next_inverse_kernel, out_shape=[jax.ShapeDtypeStruct((n, n...  2.26 us
  transfers between devices with their start and end apart: 10, of which 1 were waited for; matrix products, arithmetic and copies ran while one was open for 0% of the time, Pallas kernels for 31%

profile of v6, /device:TPU:0, one launch (start us, length us, event | category | flops | bytes accessed | tf_op | source)
XLA Modules:
  0.0 81.2 jit_solution(7577391578568920481)
XLA Ops:
  0.6 0.0 copy-start
  0.6 0.0 copy-start.2
  0.7 0.0 copy-start.3
  0.7 0.0 copy-start.1
  0.7 1.9 %take_rest.1 = (f32[2,256,256]{2,1,0:T(8,128)S(1)}, f32[4,256,256]{2,1,0:T(8,128)S(1)}, f32[4,256,256]{2,1,0:T(8,128)S(1)}) custom-call(f32[1,14,256,256]{3,2,1,0:T(8,128)} %right.7), custom_call_target="tpu_custom_call" | custom-call | tf_op jit(solution)/shard_map/take_rest/pallas_call | solution.py:124
  2.6 0.6 collective-permute-start.6
  3.1 0.8 %collective-permute-start.5 = (f32[4,256,256]{2,1,0:T(8,128)S(1)}, f32[4,256,256]{2,1,0:T(8,128)S(1)}, u32[]{:S(2)}, u32[]{:S(2)}) collective-permute-start(f32[4,256,256]{2,1,0:T(8,128)S(1)} %get-tuple-element.20), channel_id=1, source_target_pairs={{1,2},{5,6},{9,10},{13,14},{2,1},{6,5},{10,9},{14,13},{17,18},{21,... | collective-permute-start | bytes 3145736 | tf_op jit(solution)/shard_map/ppermute | solution.py:532
  4.0 1.1 %take_early.1 = (f32[256,256]{1,0:T(8,128)S(1)}, f32[2,256,256]{2,1,0:T(8,128)S(1)}) custom-call(f32[1,2,256,256]{3,2,1,0:T(8,128)} %site.7, f32[1,14,256,256]{3,2,1,0:T(8,128)} %right.7), custom_call_target="tpu_custom_call" | custom-call | tf_op jit(solution)/shard_map/take_early/pallas_call | solution.py:111
  5.1 5.9 %collective-permute-start = (f32[256,256]{1,0:T(8,128)S(1)}, f32[256,256]{1,0:T(8,128)S(1)}, u32[]{:S(2)}, u32[]{:S(2)}) collective-permute-start(f32[256,256]{1,0:T(8,128)S(1)} %get-tuple-element.14), channel_id=1, source_target_pairs={{0,1},{1,2},{2,3},{3,4},{4,5},{5,6},{6,7},{7,8},{8,9},{9,10},{10,1... | collective-permute-start | bytes 786440 | tf_op jit(solution)/shard_map/ppermute | solution.py:526
  11.0 0.7 collective-permute-start.3
  11.7 0.7 collective-permute-start.4
  12.4 0.0 collective-permute-done.lower
  12.4 0.0 copy-done.2
  12.4 0.0 copy-done.3
  12.5 7.8 %factor.1 = (f32[256,256]{1,0:T(8,128)S(1)}, f32[320,128]{1,0:T(8,128)S(1)}, f32[256,256]{1,0:T(8,128)S(1)}) custom-call(s32[16]{0:T(128)S(1)} %copy-done.3, f32[1,2,256,256]{3,2,1,0:T(8,128)S(1)} %copy-done.2, f32[256,256]{1,0:T(8,128)S(1)} %collective-permute-done.lower), custom_call_target="tpu_custom_call" | custom-call | tf_op jit(solution)/shard_map/factor/pallas_call | solution.py:254
  20.2 21.3 %collective-permute-start.1 = (f32[320,128]{1,0:T(8,128)S(1)}, f32[320,128]{1,0:T(8,128)S(1)}, u32[]{:S(2)}, u32[]{:S(2)}) collective-permute-start(f32[320,128]{1,0:T(8,128)S(1)} %get-tuple-element.15.packed), channel_id=1, source_target_pairs={{0,1},{2,3},{4,5},{6,7},{8,9},{10,11},{12,13},{14,15},{1,0},{3,2},... | collective-permute-start | bytes 491528 | tf_op jit(solution)/shard_map/ppermute | solution.py:532
  41.5 1.0 %collective-permute-done.1.near = f32[320,128]{1,0:T(8,128)S(1)} collective-permute-done((f32[320,128]{1,0:T(8,128)S(1)}, f32[320,128]{1,0:T(8,128)S(1)}, u32[]{:S(2)}, u32[]{:S(2)}) %collective-permute-start.1) | collective-permute-done | bytes 163872 | tf_op jit(solution)/shard_map/ppermute | solution.py:532
  42.6 0.7 collective-permute-start.2
  43.2 0.0 collective-permute-done.6.right_near
  43.2 0.0 copy-done
  43.3 0.0 copy-done.1
  43.3 2.5 %local_terms.2.part = f32[256,256]{1,0:T(8,128)S(1)} custom-call(f32[256,256]{1,0:T(8,128)S(1)} %get-tuple-element.16.field.bond, f32[320,128]{1,0:T(8,128)S(1)} %collective-permute-done.1.near, f32[1,14,256,256]{3,2,1,0:T(8,128)S(1)} %copy-done.1, f32[1,14,256,256]{3,2,1,0:T(8,128)S(1)} %copy-done, f32[4,256,256]{2,1,0:T(8,128)S(1)} %collective-permute-done.6.right_near), custom_call_target="tpu_custom_call" | custom-call | tf_op jit(solution)/shard_map/local_terms/pallas_call | solution.py:417
  45.8 0.0 collective-permute-done.2.far
  45.8 0.0 collective-permute-done.3.early
  45.8 0.0 collective-permute-done.4.middle
  45.8 0.0 collective-permute-done.5.late
  45.9 1.3 %first.1.applied.field = f32[256,256]{1,0:T(8,128)S(1)} custom-call(f32[256,256]{1,0:T(8,128)S(1)} %get-tuple-element.17.mask, f32[320,128]{1,0:T(8,128)S(1)} %collective-permute-done.2.far, f32[1,14,256,256]{3,2,1,0:T(8,128)S(1)} %copy-done.1, f32[2,256,256]{2,1,0:T(8,128)S(1)} %collective-permute-done.3.early, ...), custom_call_target="tpu_custom_call" | custom-call | tf_op jit(solution)/shard_map/first/pallas_call | solution.py:446
  47.2 5.5 %collective-permute-start.8 = (f32[256,256]{1,0:T(8,128)S(1)}, f32[256,256]{1,0:T(8,128)S(1)}, u32[]{:S(2)}, u32[]{:S(2)}) collective-permute-start(f32[256,256]{1,0:T(8,128)S(1)} %first.1.applied.field), channel_id=1, source_target_pairs={{0,1},{2,3},{4,5},{6,7},{8,9},{10,11},{12,13},{14,15},{1,0},{3,2},... | collective-permute-start | bytes 786440 | tf_op jit(solution)/shard_map/ppermute | solution.py:532
  52.7 0.7 collective-permute-start.7
  53.4 2.3 %next_inverse.1 = (f32[256,256]{1,0:T(8,128)S(1)}, f32[1,128]{1,0:T(1,128)S(1)}) custom-call(f32[320,128]{1,0:T(8,128)S(1)} %collective-permute-done.1.near, f32[320,128]{1,0:T(8,128)S(1)} %collective-permute-done.2.far, f32[256,256]{1,0:T(8,128)S(1)} %get-tuple-element.16.field.bond, f32[256,256]{1,0:T(8,128)S(1)} %first.1.applied.field), custom_call_target="tpu_custom_call" | custom-call | tf_op jit(solution)/shard_map/next_inverse/pallas_call | solution.py:350
  55.7 0.0 collective-permute-done.8.near
  55.7 2.5 %local_terms.3.part = f32[256,256]{1,0:T(8,128)S(1)} custom-call(f32[256,256]{1,0:T(8,128)S(1)} %first.1.applied.field, f32[256,256]{1,0:T(8,128)S(1)} %collective-permute-done.8.near, f32[1,14,256,256]{3,2,1,0:T(8,128)S(1)} %copy-done.1, f32[1,14,256,256]{3,2,1,0:T(8,128)S(1)} %copy-done, f32[4,256,256]{2,1,0:T(8,128)S(1)} %collective-permute-done.6.right_near), custom_call_target="tpu_custom_call" | custom-call | tf_op jit(solution)/shard_map/local_terms/pallas_call | solution.py:417
  58.2 0.0 collective-permute-done.7.far
  58.2 2.1 %second.1 = (f32[256,256]{1,0:T(8,128)S(1)}, f32[16,1,128]{2,1,0:T(1,128)}) custom-call(f32[256,256]{1,0:T(8,128)S(1)} %get-tuple-element.17.mask, f32[256,256]{1,0:T(8,128)S(1)} %collective-permute-done.7.far, f32[1,14,256,256]{3,2,1,0:T(8,128)S(1)} %copy-done.1, f32[2,256,256]{2,1,0:T(8,128)S(1)} %collective-permute-done.3.early, ...), custom_call_target="tpu_custom_call" | custom-call | tf_op jit(solution)/shard_map/second/pallas_call | solution.py:477
  60.3 10.8 %all-to-all-start = ((f32[16,1,128]{2,1,0:T(1,128)}), f32[16,1,128]{2,1,0:T(1,128)S(1)}, u32[]{:S(2)}, u32[]{:S(2)}) async-start(f32[16,1,128]{2,1,0:T(1,128)} %get-tuple-element.24), calls=%async_computation | async-start | bytes 16384 | tf_op jit(solution)/shard_map/all_to_all | solution.py:556
  71.1 5.2 %upper_rows.1.top = f32[256,256]{1,0:T(8,128)S(1)} custom-call(s32[16]{0:T(128)S(1)} %copy-done.3, f32[320,128]{1,0:T(8,128)S(1)} %get-tuple-element.15.packed, f32[1,2,256,256]{3,2,1,0:T(8,128)S(1)} %copy-done.2), custom_call_target="tpu_custom_call" | custom-call | tf_op jit(solution)/shard_map/upper_rows/pallas_call | solution.py:322
  76.3 3.9 %lower_rows.1 = f32[1,2,256,256]{3,2,1,0:T(8,128)} custom-call(s32[16]{0:T(128)S(1)} %copy-done.3, f32[320,128]{1,0:T(8,128)S(1)} %collective-permute-done.1.near, f32[320,128]{1,0:T(8,128)S(1)} %collective-permute-done.2.far, f32[256,256]{1,0:T(8,128)S(1)} %get-tuple-element.22.inv, f32[1,2,256,256]{3,2,1,0:T(8,128)S(1)} %copy-done.2, ...), custom_call_target="tpu_custom_call" | custom-call | tf_op jit(solution)/shard_map/lower_rows/pallas_call | solution.py:379
  80.2 0.0 all-to-all-done.gathered
  80.2 0.9 %final.1 = f32[1,256,256]{2,1,0:T(8,128)} custom-call(f32[16,1,128]{2,1,0:T(1,128)S(1)} %all-to-all-done.gathered, f32[256,256]{1,0:T(8,128)S(1)} %get-tuple-element.16.field.bond, f32[256,256]{1,0:T(8,128)S(1)} %first.1.applied.field, f32[256,256]{1,0:T(8,128)S(1)} %get-tuple-element.25.twice), custom_call_target="tpu_custom_call" | custom-call | tf_op jit(solution)/shard_map/final/pallas_call | solution.py:512
Async XLA Ops:
  0.6 42.6 %copy-start = (f32[1,14,256,256]{3,2,1,0:T(8,128)S(1)}, f32[1,14,256,256]{3,2,1,0:T(8,128)}, u32[]{:S(2)}) copy-start(f32[1,14,256,256]{3,2,1,0:T(8,128)} %right.7) | copy-start | bytes 11010052
  0.6 11.8 %copy-start.2 = (f32[1,2,256,256]{3,2,1,0:T(8,128)S(1)}, f32[1,2,256,256]{3,2,1,0:T(8,128)}, u32[]{:S(2)}) copy-start(f32[1,2,256,256]{3,2,1,0:T(8,128)} %site.7) | copy-start | bytes 1572868
  0.7 11.8 %copy-start.3 = (s32[16]{0:T(128)S(1)}, s32[16]{0:T(128)}, u32[]{:S(2)}) copy-start(s32[16]{0:T(128)} %sizes.5) | copy-start | bytes 196
  0.7 42.6 %copy-start.1 = (f32[1,14,256,256]{3,2,1,0:T(8,128)S(1)}, f32[1,14,256,256]{3,2,1,0:T(8,128)}, u32[]{:S(2)}) copy-start(f32[1,14,256,256]{3,2,1,0:T(8,128)} %left.7) | copy-start | bytes 11010052
  2.6 40.7 %collective-permute-start.6 = (f32[4,256,256]{2,1,0:T(8,128)S(1)}, f32[4,256,256]{2,1,0:T(8,128)S(1)}, u32[]{:S(2)}, u32[]{:S(2)}) collective-permute-start(f32[4,256,256]{2,1,0:T(8,128)S(1)} %get-tuple-element.21), channel_id=1, source_target_pairs={{0,1},{2,3},{4,5},{6,7},{8,9},{10,11},{12,13},{14,15},{1,0},{3,2},... | collective-permute-start | bytes 3145736 | tf_op jit(solution)/shard_map/ppermute | solution.py:532
  3.1 42.7 %collective-permute-start.5 = (f32[4,256,256]{2,1,0:T(8,128)S(1)}, f32[4,256,256]{2,1,0:T(8,128)S(1)}, u32[]{:S(2)}, u32[]{:S(2)}) collective-permute-start(f32[4,256,256]{2,1,0:T(8,128)S(1)} %get-tuple-element.20), channel_id=1, source_target_pairs={{1,2},{5,6},{9,10},{13,14},{2,1},{6,5},{10,9},{14,13},{17,18},{21,... | collective-permute-start | bytes 3145736 | tf_op jit(solution)/shard_map/ppermute | solution.py:532
  5.1 7.3 %collective-permute-start = (f32[256,256]{1,0:T(8,128)S(1)}, f32[256,256]{1,0:T(8,128)S(1)}, u32[]{:S(2)}, u32[]{:S(2)}) collective-permute-start(f32[256,256]{1,0:T(8,128)S(1)} %get-tuple-element.14), channel_id=1, source_target_pairs={{0,1},{1,2},{2,3},{3,4},{4,5},{5,6},{6,7},{7,8},{8,9},{9,10},{10,1... | collective-permute-start | bytes 786440 | tf_op jit(solution)/shard_map/ppermute | solution.py:526
  11.0 34.8 %collective-permute-start.3 = (f32[2,256,256]{2,1,0:T(8,128)S(1)}, f32[2,256,256]{2,1,0:T(8,128)S(1)}, u32[]{:S(2)}, u32[]{:S(2)}) collective-permute-start(f32[2,256,256]{2,1,0:T(8,128)S(1)} %get-tuple-element.18), channel_id=1, source_target_pairs={{3,4},{7,8},{11,12},{4,3},{8,7},{12,11},{19,20},{23,24},{27,28},{2... | collective-permute-start | bytes 1572872 | tf_op jit(solution)/shard_map/ppermute | solution.py:532
  11.7 34.1 %collective-permute-start.4 = (f32[2,256,256]{2,1,0:T(8,128)S(1)}, f32[2,256,256]{2,1,0:T(8,128)S(1)}, u32[]{:S(2)}, u32[]{:S(2)}) collective-permute-start(f32[2,256,256]{2,1,0:T(8,128)S(1)} %get-tuple-element.19), channel_id=1, source_target_pairs={{3,4},{7,8},{11,12},{4,3},{8,7},{12,11},{19,20},{23,24},{27,28},{2... | collective-permute-start | bytes 1572872 | tf_op jit(solution)/shard_map/ppermute | solution.py:532
  20.2 22.3 %collective-permute-start.1 = (f32[320,128]{1,0:T(8,128)S(1)}, f32[320,128]{1,0:T(8,128)S(1)}, u32[]{:S(2)}, u32[]{:S(2)}) collective-permute-start(f32[320,128]{1,0:T(8,128)S(1)} %get-tuple-element.15.packed), channel_id=1, source_target_pairs={{0,1},{2,3},{4,5},{6,7},{8,9},{10,11},{12,13},{14,15},{1,0},{3,2},... | collective-permute-start | bytes 491528 | tf_op jit(solution)/shard_map/ppermute | solution.py:532
  42.6 3.2 %collective-permute-start.2 = (f32[320,128]{1,0:T(8,128)S(1)}, f32[320,128]{1,0:T(8,128)S(1)}, u32[]{:S(2)}, u32[]{:S(2)}) collective-permute-start(f32[320,128]{1,0:T(8,128)S(1)} %get-tuple-element.15.packed), channel_id=1, source_target_pairs={{1,2},{3,4},{5,6},{7,8},{9,10},{11,12},{13,14},{2,1},{4,3},{6,5},{... | collective-permute-start | bytes 491528 | tf_op jit(solution)/shard_map/ppermute | solution.py:532
  47.2 8.5 %collective-permute-start.8 = (f32[256,256]{1,0:T(8,128)S(1)}, f32[256,256]{1,0:T(8,128)S(1)}, u32[]{:S(2)}, u32[]{:S(2)}) collective-permute-start(f32[256,256]{1,0:T(8,128)S(1)} %first.1.applied.field), channel_id=1, source_target_pairs={{0,1},{2,3},{4,5},{6,7},{8,9},{10,11},{12,13},{14,15},{1,0},{3,2},... | collective-permute-start | bytes 786440 | tf_op jit(solution)/shard_map/ppermute | solution.py:532
  52.7 5.5 %collective-permute-start.7 = (f32[256,256]{1,0:T(8,128)S(1)}, f32[256,256]{1,0:T(8,128)S(1)}, u32[]{:S(2)}, u32[]{:S(2)}) collective-permute-start(f32[256,256]{1,0:T(8,128)S(1)} %first.1.applied.field), channel_id=1, source_target_pairs={{1,2},{3,4},{5,6},{7,8},{9,10},{11,12},{13,14},{2,1},{4,3},{6,5},{... | collective-permute-start | bytes 786440 | tf_op jit(solution)/shard_map/ppermute | solution.py:532
  60.3 19.9 %all-to-all-start = ((f32[16,1,128]{2,1,0:T(1,128)}), f32[16,1,128]{2,1,0:T(1,128)S(1)}, u32[]{:S(2)}, u32[]{:S(2)}) async-start(f32[16,1,128]{2,1,0:T(1,128)} %get-tuple-element.24), calls=%async_computation | async-start | bytes 16384 | tf_op jit(solution)/shard_map/all_to_all | solution.py:556
